TPU v7x, 32 devices: a whole 2x2x4 slice. The times are simulated.
32 devices in a mesh: dp: 8 (over z, core), tensor: 4 (over y, x).
Axes of the slice: x: 2, y: 2, z: 4, core: 2. Of those that a mesh axis runs over, the one named last changes fastest.
Arguments:
- block_input: bfloat16 [4096, 2048], P('dp'), may hold values from -6 to 6
- cotangent: bfloat16 [4096, 2048], P('dp'), may hold values from -6 to 6
- lengths: int32 [8], P('dp'), may hold values from 1 to 512, as said below
- attn_gain: bfloat16 [2048], P('dp'), may hold values from 0.5 to 1.5
- attn_shift: bfloat16 [2048], P('dp'), may hold values from -3 to 3
- ffn_gain: bfloat16 [2048], P('dp'), may hold values from 0.5 to 1.5
- ffn_shift: bfloat16 [2048], P('dp'), may hold values from -3 to 3
- qkv_weight: bfloat16 [3, 2048, 2048], P(None, 'dp', 'tensor')
- qkv_bias: bfloat16 [3, 2048], P(None, ('tensor', 'dp')), may hold values from -3 to 3
- out_weight: bfloat16 [2048, 2048], P('tensor', 'dp'), may hold values from -1 to 1
- out_bias: bfloat16 [2048], P('dp'), may hold values from -3 to 3
- up_weight: bfloat16 [2048, 8192], P('dp', 'tensor'), may hold values from -0.125 to 0.125
- up_bias: bfloat16 [8192], P(('tensor', 'dp')), may hold values from -3 to 3
- down_weight: bfloat16 [8192, 2048], P('tensor', 'dp'), may hold values from -0.0625 to 0.0625
Outputs:
- block_output: bfloat16 [4096, 2048], P('dp')
- dblock_input: bfloat16 [4096, 2048], P('dp')
- dattn_gain: float32 [2048], P('dp')
- dattn_shift: float32 [2048], P('dp')
- dffn_gain: float32 [2048], P('dp')
- dffn_shift: float32 [2048], P('dp')
- dqkv_weight: float32 [3, 2048, 2048], P(None, 'dp', 'tensor')
- dqkv_bias: float32 [3, 2048], P(None, ('tensor', 'dp'))
- dout_weight: float32 [2048, 2048], P('tensor', 'dp')
- dout_bias: float32 [2048], P('dp')
- dup_weight: float32 [2048, 8192], P('dp', 'tensor')
- dup_bias: float32 [8192], P(('tensor', 'dp'))
- ddown_weight: float32 [8192, 2048], P('tensor', 'dp')
Inputs may be any that keep to these rules, and one draw needn't show every extreme that they name: `lengths`: one sequence for each index of dp; some sequence uses all 512 slots.
All inputs are finite; a program needn't handle non-finite values.
Results may differ from a plain program's by a relative error of at most 0.014.
Values may be sent and summed in bfloat16 or wider, within the bound.
A program may use at most 192 MiB of HBM per device.

v0:
```python
import math

import jax
import jax.numpy as jnp
from jax import lax
from jax.sharding import PartitionSpec as P

HD = 256
ROT = 64


norm_eps = 1e-05
rope_base = 10000.0


def rope_tables(row_count, rot_width):
    half_rot = rot_width // 2
    freq_idx = jnp.arange(half_rot, dtype=jnp.float32)
    inv_freq = jnp.exp(-(2.0 * freq_idx / rot_width) * math.log(rope_base))
    angles = jnp.arange(row_count, dtype=jnp.float32)[:, None] * inv_freq[None, :]
    return (jnp.cos(angles), jnp.sin(angles))


def rotate(heads_arr, cosine, sine_tab, direction):
    half_rot = ROT // 2
    first_half = heads_arr[..., :half_rot]
    second_half = heads_arr[..., half_rot:ROT]
    rest_dims = heads_arr[..., ROT:]
    cos_b = cosine[:, None, :]
    sin_b = sine_tab[:, None, :] * direction
    new_first = first_half * cos_b - second_half * sin_b
    new_second = second_half * cos_b + first_half * sin_b
    return jnp.concatenate([new_first, new_second, rest_dims], axis=-1)


def gelu_exact(pre_act):
    return 0.5 * pre_act * (1.0 + lax.erf(pre_act * (1.0 / math.sqrt(2.0))))


def gelu_slope(pre_act):
    cdf_part = 0.5 * (1.0 + lax.erf(pre_act * (1.0 / math.sqrt(2.0))))
    return cdf_part + pre_act * jnp.exp(-0.5 * pre_act * pre_act) * (1.0 / math.sqrt(2.0 * math.pi))


def per_device(
    block_input,
    cotangent,
    lengths,
    attn_gain,
    attn_shift,
    ffn_gain,
    ffn_shift,
    qkv_weight,
    qkv_bias,
    out_weight,
    out_bias,
    up_weight,
    up_bias,
    down_weight,
):
    gathered = (
        lax.all_gather(qkv_weight, "dp", axis=1, tiled=True),
        lax.all_gather(out_weight, "dp", axis=1, tiled=True),
        lax.all_gather(up_weight, "dp", axis=0, tiled=True),
        lax.all_gather(down_weight, "dp", axis=1, tiled=True),
        lax.all_gather(qkv_bias, "dp", axis=1, tiled=True),
        lax.all_gather(up_bias, "dp", axis=0, tiled=True),
        lax.all_gather(out_bias, "dp", axis=0, tiled=True),
        lax.all_gather(attn_gain, "dp", axis=0, tiled=True),
        lax.all_gather(attn_shift, "dp", axis=0, tiled=True),
        lax.all_gather(ffn_gain, "dp", axis=0, tiled=True),
        lax.all_gather(ffn_shift, "dp", axis=0, tiled=True),
    )
    (
        qkv_full,
        out_full,
        up_full,
        down_full,
        qkv_b,
        up_b,
        outb_full,
        gain_a,
        shift_a,
        gain_f,
        shift_f,
    ) = gathered
    gain_a = gain_a.astype(jnp.float32)
    gain_f = gain_f.astype(jnp.float32)
    seq_rows = block_input.shape[0]
    local_width = qkv_full.shape[2]
    local_heads = local_width // HD
    seq_len = lengths[0]
    positions = jnp.arange(seq_rows, dtype=jnp.int32)
    scale_qk = 1.0 / math.sqrt(HD)
    block_rows = min(512, seq_rows)
    x_rows = block_input.astype(jnp.float32)
    row_mean = jnp.mean(x_rows, axis=-1, keepdims=True)
    centered = x_rows - row_mean
    inv_std = lax.rsqrt(jnp.mean(centered * centered, axis=-1, keepdims=True) + norm_eps)
    normed = centered * inv_std
    attn_in = (normed * gain_a + shift_a.astype(jnp.float32)).astype(jnp.bfloat16)
    ffn_in = (normed * gain_f + shift_f.astype(jnp.float32)).astype(jnp.bfloat16)
    qkv_rows = (
        jnp.einsum("ld,pde->ple", attn_in, qkv_full, preferred_element_type=jnp.float32)
        + qkv_b.astype(jnp.float32)[:, None, :]
    )
    cosine, sine_tab = rope_tables(seq_rows, ROT)
    query_rows = rotate(
        qkv_rows[0].reshape(seq_rows, local_heads, HD), cosine, sine_tab, 1.0
    ).astype(jnp.bfloat16)
    key_rows = rotate(qkv_rows[1].reshape(seq_rows, local_heads, HD), cosine, sine_tab, 1.0).astype(
        jnp.bfloat16
    )
    value_rows = qkv_rows[2].reshape(seq_rows, local_heads, HD).astype(jnp.bfloat16)

    def block_scores(row_lo, key_end):
        raw_scores = (
            jnp.einsum("lhe,mhe->hlm", query_rows, key_rows, preferred_element_type=jnp.float32)
            * scale_qk
        )
        key_mask = (positions[None, :key_end] <= positions[row_lo:key_end, None]) & (
            positions[None, :key_end] < seq_len
        )
        return jnp.where(key_mask[None], raw_scores, -jnp.inf)

    qblock = 0
    row_lo = qblock * block_rows
    key_end = row_lo + block_rows
    scores = block_scores(row_lo, key_end)
    row_max = jnp.max(scores, axis=-1, keepdims=True)
    exp_terms = jnp.exp(scores - row_max)
    row_total = jnp.sum(exp_terms, axis=-1, keepdims=True)
    prob_bf = (exp_terms / row_total).astype(jnp.bfloat16)
    lse_blocks = [row_max + jnp.log(row_total)]
    attn_blocks = jnp.einsum(
        "hlm,mhe->lhe", prob_bf, value_rows, preferred_element_type=jnp.float32
    ).astype(jnp.bfloat16)
    mixed_flat = attn_blocks.reshape(seq_rows, local_width)
    attn_part = jnp.dot(mixed_flat, out_full, preferred_element_type=jnp.float32)
    up_pre = jnp.dot(ffn_in, up_full, preferred_element_type=jnp.float32) + up_b.astype(jnp.float32)
    hidden = gelu_exact(up_pre).astype(jnp.bfloat16)
    ffn_part = jnp.dot(hidden, down_full, preferred_element_type=jnp.float32)
    branch_sum = lax.psum(attn_part + ffn_part, "tensor")
    block_output = (x_rows + branch_sum + outb_full.astype(jnp.float32)).astype(jnp.bfloat16)
    qkv_back, out_back, up_back, down_back = (qkv_full, out_full, up_full, down_full)
    row_valid = (positions < seq_len).astype(jnp.float32)[:, None]
    grad_rows = cotangent.astype(jnp.float32) * row_valid
    grad_bf = grad_rows.astype(jnp.bfloat16)
    dout_b = jnp.sum(grad_rows, axis=0)
    ddown_w = jnp.einsum("lf,ld->fd", hidden, grad_bf, preferred_element_type=jnp.float32)
    up_grad32 = jnp.einsum(
        "ld,fd->lf", grad_bf, down_back, preferred_element_type=jnp.float32
    ) * gelu_slope(up_pre)
    up_grad = up_grad32.astype(jnp.bfloat16)
    dup_w = jnp.einsum("ld,lf->df", ffn_in, up_grad, preferred_element_type=jnp.float32)
    dup_b = jnp.sum(up_grad32, axis=0)
    ffn_back = jnp.einsum("lf,df->ld", up_grad, up_back, preferred_element_type=jnp.float32)
    mixed_grad = (
        jnp.einsum("ld,ed->le", grad_bf, out_back, preferred_element_type=jnp.float32)
        .astype(jnp.bfloat16)
        .reshape(seq_rows, local_heads, HD)
    )
    dout_w = jnp.einsum("le,ld->ed", mixed_flat, grad_bf, preferred_element_type=jnp.float32)
    delta_rows = jnp.einsum(
        "lhe,lhe->hl", mixed_grad, attn_blocks, preferred_element_type=jnp.float32
    )
    query_grad = jnp.zeros((seq_rows, local_heads, HD), jnp.float32)
    key_grad = jnp.zeros((seq_rows, local_heads, HD), jnp.float32)
    value_grad = jnp.zeros((seq_rows, local_heads, HD), jnp.float32)
    qblock = 0
    row_lo = qblock * block_rows
    key_end = row_lo + block_rows
    scores = block_scores(row_lo, key_end)
    probs32 = jnp.exp(scores - lse_blocks[qblock])
    prob_back = probs32.astype(jnp.bfloat16)
    value_grad = value_grad.at[:key_end].add(
        jnp.einsum("hlm,lhe->mhe", prob_back, mixed_grad, preferred_element_type=jnp.float32)
    )
    prob_grad = jnp.einsum(
        "lhe,mhe->hlm", mixed_grad, value_rows, preferred_element_type=jnp.float32
    )
    score_grad = (probs32 * (prob_grad - delta_rows[:, row_lo:key_end, None]) * scale_qk).astype(
        jnp.bfloat16
    )
    query_grad = query_grad.at[row_lo:key_end].set(
        jnp.einsum("hlm,mhe->lhe", score_grad, key_rows, preferred_element_type=jnp.float32)
    )
    key_grad = key_grad.at[:key_end].add(
        jnp.einsum("hlm,lhe->mhe", score_grad, query_rows, preferred_element_type=jnp.float32)
    )
    query_grad = rotate(query_grad, cosine, sine_tab, -1.0)
    key_grad = rotate(key_grad, cosine, sine_tab, -1.0)
    qkv_grad32 = jnp.stack([query_grad, key_grad, value_grad]).reshape(3, seq_rows, local_width)
    dqkv_b = jnp.sum(qkv_grad32, axis=1)
    qkv_grad = qkv_grad32.astype(jnp.bfloat16)
    dqkv_w = jnp.einsum("ld,ple->pde", attn_in, qkv_grad, preferred_element_type=jnp.float32)
    attn_back = jnp.einsum("ple,pde->ld", qkv_grad, qkv_back, preferred_element_type=jnp.float32)
    norm_part = attn_back * gain_a + ffn_back * gain_f
    norm_stats = jnp.stack(
        [
            jnp.sum(attn_back * normed, axis=0),
            jnp.sum(attn_back, axis=0),
            jnp.sum(ffn_back * normed, axis=0),
            jnp.sum(ffn_back, axis=0),
        ]
    )
    norm_grad, stat_sum = lax.psum((norm_part, norm_stats), "tensor")
    grad_mean = jnp.mean(norm_grad, axis=-1, keepdims=True)
    grad_proj = jnp.mean(norm_grad * normed, axis=-1, keepdims=True)
    dblock_input = (grad_rows + inv_std * (norm_grad - grad_mean - normed * grad_proj)).astype(
        jnp.bfloat16
    )
    dqkv_sent, dout_sent, dup_sent, ddown_sent, dqkvb_sent, dupb_sent, doutb_sent, stats_sent = (
        lax.psum_scatter(dqkv_w, "dp", scatter_dimension=1, tiled=True),
        lax.psum_scatter(dout_w, "dp", scatter_dimension=1, tiled=True),
        lax.psum_scatter(dup_w, "dp", scatter_dimension=0, tiled=True),
        lax.psum_scatter(ddown_w, "dp", scatter_dimension=1, tiled=True),
        lax.psum_scatter(dqkv_b, "dp", scatter_dimension=1, tiled=True),
        lax.psum_scatter(dup_b, "dp", scatter_dimension=0, tiled=True),
        lax.psum_scatter(dout_b, "dp", scatter_dimension=0, tiled=True),
        lax.psum_scatter(stat_sum, "dp", scatter_dimension=1, tiled=True),
    )
    return (
        block_output,
        dblock_input,
        stats_sent[0],
        stats_sent[1],
        stats_sent[2],
        stats_sent[3],
        dqkv_sent,
        dqkvb_sent,
        dout_sent,
        doutb_sent,
        dup_sent,
        dupb_sent,
        ddown_sent,
    )


def solution(mesh):
    in_specs = (
        P("dp", None),
        P("dp", None),
        P("dp"),
        P("dp"),
        P("dp"),
        P("dp"),
        P("dp"),
        P(None, "dp", "tensor"),
        P(None, ("tensor", "dp")),
        P("tensor", "dp"),
        P("dp"),
        P("dp", "tensor"),
        P(("tensor", "dp")),
        P("tensor", "dp"),
    )
    out_specs = (
        P("dp", None),
        P("dp", None),
        P("dp"),
        P("dp"),
        P("dp"),
        P("dp"),
        P(None, "dp", "tensor"),
        P(None, ("tensor", "dp")),
        P("tensor", "dp"),
        P("dp"),
        P("dp", "tensor"),
        P(("tensor", "dp")),
        P("tensor", "dp"),
    )
    return jax.shard_map(
        per_device, mesh=mesh, in_specs=in_specs, out_specs=out_specs, check_vma=False
    )
```

profile of v0, /device:TPU:0, one launch (start us, length us, event | category | flops | bytes accessed | tf_op | source)
XLA Modules:
  0.0 1074.9 jit_solution(16801075878062956087)
XLA Ops:
  12.5 13.6 %all-gather.5 = bf16[8,1,256]{2,1,0:T(2,128)(2,1)S(1)} all-gather(bf16[1,1,256]{2,1,0:T(2,128)(2,1)S(1)} %reshape.282), channel_id=1, replica_groups=mesh['dp'=8,'tensor'=4] {'dp'}, dimensions={0}, use_global_device_ids=true | all-gather | bytes 4608 | tf_op jit(solution)/shard_map/all_gather | solution.py:67
  26.7 9.0 all-gather.4
  36.3 10.3 all-gather.3
  46.6 8.8 all-gather.1
  55.4 10.4 all-gather
  65.9 17.9 %all-gather.2 = bf16[8,64,3]{1,2,0:T(4,128)(2,1)S(1)} all-gather(bf16[1,64,3]{1,2,0:T(4,128)(2,1)S(1)} %bitcast.120), channel_id=1, replica_groups=mesh['dp'=8,'tensor'=4] {'dp'}, dimensions={0}, use_global_device_ids=true | all-gather | bytes 3456 | tf_op jit(solution)/shard_map/all_gather | solution.py:66
  87.5 4.4 convolution_convert_fusion
  92.0 17.6 %all-gather.12.cloned.1.call-done = bf16[3,2048,512]{1,2,0:T(8,128)(2,1)} async-done(((bf16[3,256,512]{1,2,0:T(8,128)(2,1)}), bf16[3,2048,512]{1,2,0:T(8,128)(2,1)}) %all-gather.12.cloned.1.call-update) | async-done | bytes 6291472 | tf_op jit(solution)/shard_map/all_gather | solution.py:62
  109.5 6.1 add_bitcast_fusion
  140.8 3.5 fusion.37
  160.9 30.5 %all-gather.16.cloned.1.call-done = bf16[2048,2048]{1,0:T(8,128)(2,1)} async-done(((bf16[256,2048]{1,0:T(8,128)(2,1)}), bf16[2048,2048]{1,0:T(8,128)(2,1)}) %all-gather.16.cloned.1.call-update) | async-done | bytes 8388624 | tf_op jit(solution)/shard_map/all_gather | solution.py:64
  191.4 9.7 fusion.53
  201.1 72.7 %all-gather.18.cloned.1.call-done = bf16[2048,2048]{1,0:T(8,128)(2,1)} async-done(((bf16[2048,256]{1,0:T(8,128)(2,1)}), bf16[2048,2048]{1,0:T(8,128)(2,1)}) %all-gather.18.cloned.1.call-update) | async-done | bytes 8388624 | tf_op jit(solution)/shard_map/all_gather | solution.py:65
  273.9 10.8 %fusion.68 = (f32[2048]{0:T(1024)S(1)}, bf16[512,2048]{1,0:T(8,128)(2,1)}) fusion(f32[512,2048]{1,0:T(8,128)} %fusion.53, f32[2048]{0:T(1024)S(1)} %bitcast.114, bf16[2048,2048]{1,0:T(8,128)(2,1)} %all-gather.18.cloned.1.call-done, bf16[512,2048]{1,0:T(8,128)(2,1)} %param.27, f32[512]{0:T(512)S(1)} %copy-done.26), kind=kOutput, calls=%fused_computation.105 | convolution fusion | flops 4310693888 | bytes 16795648 | tf_op jit(solution)/shard_map/ld,fd->lf/dot_general | solution.py:151
  284.7 8.1 fusion.61
  292.8 7.8 fusion.40
  300.6 3.4 convolution_add_fusion
  304.0 5.8 fusion.27
  312.6 167.7 %all-reduce.6.cloned.1.call-done = (f32[512,2048]{1,0:T(8,128)}, f32[512,2048]{1,0:T(8,128)}) async-done(((f32[512,2048]{1,0:T(8,128)}, f32[512,2048]{1,0:T(8,128)}), (f32[512,2048]{1,0:T(8,128)}, f32[512,2048]{1,0:T(8,128)})) %all-reduce.6.cloned.1.call-update) | async-done | bytes 8388624 | tf_op jit(solution)/shard_map/psum | solution.py:143
  480.3 6.3 fusion.62
  488.1 8.4 convolution_bitcast_fusion
  497.5 5.0 fusion.57
  502.5 13.3 %fusion.55 = f32[2048,2048]{1,0:T(8,128)} fusion(bf16[512,2048]{1,0:T(8,128)(2,1)} %param.27, f32[512]{0:T(512)S(1)} %copy-done.26, f32[512,2048]{1,0:T(8,128)} %fusion.53, f32[2048]{0:T(1024)S(1)} %bitcast.116), kind=kOutput, calls=%fused_computation.96 | convolution fusion | flops 4304404480 | bytes 23078912 | tf_op jit(solution)/shard_map/lf,ld->fd/dot_general | solution.py:150
  515.9 10.0 fusion.38
  526.5 11.8 %all-gather.6 = bf16[8,1,256]{2,1,0:T(2,128)(2,1)S(1)} all-gather(bf16[1,1,256]{2,1,0:T(2,128)(2,1)S(1)} %reshape.284), channel_id=1, replica_groups=mesh['dp'=8,'tensor'=4] {'dp'}, dimensions={0}, use_global_device_ids=true | all-gather | bytes 4608 | tf_op jit(solution)/shard_map/all_gather | solution.py:68
  541.0 6.9 fusion.28
  547.9 27.4 %all-reduce.2 = (f32[2048]{0:T(1024)S(1)}, f32[2048]{0:T(1024)S(1)}) all-reduce(f32[2048]{0:T(1024)S(1)} %get-tuple-element.141, f32[2048]{0:T(1024)S(1)} %get-tuple-element.173), channel_id=6, replica_groups=mesh['dp'=8,'tensor'=4] {'dp'}, use_global_device_ids=true, to_apply=%region_19.20.clone | all-reduce | flops 4096 | bytes 32768
  577.6 9.6 psum.24
  587.8 90.4 %reduce-scatter.11.cloned.1.call-done = f32[3,256,512]{1,2,0:T(8,128)} async-done(((f32[3,2048,512]{1,2,0:T(8,128)}), f32[3,256,512]{1,2,0:T(8,128)}) %reduce-scatter.11.cloned.1.call-update) | async-done | bytes 1572880 | tf_op jit(solution)/shard_map/reduce_scatter | solution.py:214
  681.1 48.0 %reduce-scatter.13.cloned.1.call-done = f32[512,256]{1,0:T(8,128)} async-done(((f32[512,2048]{1,0:T(8,128)}), f32[512,256]{1,0:T(8,128)}) %reduce-scatter.13.cloned.1.call-update) | async-done | bytes 524304 | tf_op jit(solution)/shard_map/reduce_scatter | solution.py:215
  729.1 169.5 %reduce-scatter.17.cloned.1.call-done = f32[2048,256]{1,0:T(8,128)} async-done(((f32[2048,2048]{1,0:T(8,128)}), f32[2048,256]{1,0:T(8,128)}) %reduce-scatter.17.cloned.1.call-update) | async-done | bytes 2097168 | tf_op jit(solution)/shard_map/reduce_scatter | solution.py:217
  898.6 169.6 %reduce-scatter.15.cloned.1.call-done = f32[256,2048]{1,0:T(8,128)} async-done(((f32[2048,2048]{1,0:T(8,128)}), f32[256,2048]{1,0:T(8,128)}) %reduce-scatter.15.cloned.1.call-update) | async-done | bytes 2097168 | tf_op jit(solution)/shard_map/reduce_scatter | solution.py:216
  (180 shorter events, 64.9 us)
Async XLA Ops:
  7.2 58.6 %copy-start.33 = (bf16[3,64]{1,0:T(4,128)(2,1)S(1)}, bf16[3,64]{1,0:T(4,128)(2,1)}, u32[]{:S(2)}) copy-start(bf16[3,64]{1,0:T(4,128)(2,1)} %param.34) | copy-start | bytes 1156
  7.2 76.6 %copy-start = (bf16[512,2048]{1,0:T(8,128)(2,1)S(1)}, bf16[512,2048]{1,0:T(8,128)(2,1)}, u32[]{:S(2)}) copy-start(bf16[512,2048]{1,0:T(8,128)(2,1)} %param.26) | copy-start | bytes 6291460
  7.3 80.3 %all-gather.14.cloned.1.call-start = ((), (), s32[]{:S(2)}) async-start(), calls=%async_computation.7 | async-start | bytes 2359296 | tf_op jit(solution)/shard_map/all_gather | solution.py:63
  8.0 101.5 %all-gather.12.cloned.1.call-start = ((), (), s32[]{:S(2)}) async-start(), calls=%async_computation.6 | async-start | bytes 7077888 | tf_op jit(solution)/shard_map/all_gather | solution.py:62
  10.3 181.1 %all-gather.16.cloned.1.call-start = ((), (), s32[]{:S(2)}) async-start(), calls=%async_computation.8 | async-start | bytes 9437184 | tf_op jit(solution)/shard_map/all_gather | solution.py:64
  11.1 262.8 %all-gather.18.cloned.1.call-start = ((), (), s32[]{:S(2)}) async-start(), calls=%async_computation.9 | async-start | bytes 9437184 | tf_op jit(solution)/shard_map/all_gather | solution.py:65
  11.7 468.6 %all-reduce.6.cloned.1.call-start = ((), (), s32[]{:S(2)}) async-start(), calls=%async_computation.16 | async-start | bytes 16777216 | tf_op jit(solution)/shard_map/psum | solution.py:143
  55.4 54.1 %copy-start.31 = (f32[8,1,256]{2,1,0:T(1,128)}, f32[8,1,256]{2,1,0:T(1,128)S(1)}, u32[]{:S(2)}) copy-start(f32[8,1,256]{2,1,0:T(1,128)S(1)} %convert_element_type.108) | copy-start | bytes 24580
  83.9 8.1 copy-start.25
  84.2 25.3 %copy-start.23 = (f32[512]{0:T(512)}, f32[512]{0:T(512)S(1)}, u32[]{:S(2)}) copy-start(f32[512]{0:T(512)S(1)} %broadcast_multiply_fusion.3) | copy-start | bytes 6148
  84.9 24.6 %copy-start.27 = (f32[512]{0:T(512)}, f32[512]{0:T(512)S(1)}, u32[]{:S(2)}) copy-start(f32[512]{0:T(512)S(1)} %add_rsqrt_fusion) | copy-start | bytes 6148
  133.5 5.7 copy-start.14
  133.5 5.7 copy-start.16
  133.5 5.6 copy-start.18
  150.8 40.6 %copy-start.24 = (f32[512]{0:T(512)S(1)}, f32[512]{0:T(512)}, u32[]{:S(2)}) copy-start(f32[512]{0:T(512)} %copy-done.23) | copy-start | bytes 6148
  150.8 40.6 %copy-start.28 = (f32[512]{0:T(512)S(1)}, f32[512]{0:T(512)}, u32[]{:S(2)}) copy-start(f32[512]{0:T(512)} %copy-done.27) | copy-start | bytes 6148
  150.8 40.6 %copy-start.29 = (f32[8,1,256]{2,1,0:T(1,128)S(1)}, f32[8,1,256]{2,1,0:T(1,128)}, u32[]{:S(2)}) copy-start(f32[8,1,256]{2,1,0:T(1,128)} %convert_element_type.111) | copy-start | bytes 24580
  191.4 82.4 %copy-start.26 = (f32[512]{0:T(512)S(1)}, f32[512]{0:T(512)}, u32[]{:S(2)}) copy-start(f32[512]{0:T(512)} %copy-done.25) | copy-start | bytes 6148
  191.4 82.4 %copy-start.30 = (f32[8,1,256]{2,1,0:T(1,128)S(1)}, f32[8,1,256]{2,1,0:T(1,128)}, u32[]{:S(2)}) copy-start(f32[8,1,256]{2,1,0:T(1,128)} %convert_element_type.112) | copy-start | bytes 24580
  273.8 10.8 %copy-start.41 = (f32[512,2048]{1,0:T(8,128)S(1)}, f32[512,2048]{1,0:T(8,128)}, u32[]{:S(2)}) copy-start(f32[512,2048]{1,0:T(8,128)} %fusion.53) | copy-start | bytes 12582916
  273.9 30.2 %slice-start = ((s8[6291456]{0:T(1024)(128)(4,1)}), s8[4194304]{0:T(1024)(128)(4,1)S(1)}, s32[]{:S(2)}) async-start(s8[6291456]{0:T(1024)(128)(4,1)} %bitcast.82), calls=%async_computation.17 | async-start | bytes 8388608
  284.7 19.3 %slice-start.1 = ((s8[6291456]{0:T(1024)(128)(4,1)}), s8[2097152]{0:T(1024)(128)(4,1)S(1)}, s32[]{:S(2)}) async-start(s8[6291456]{0:T(1024)(128)(4,1)} %bitcast.82), calls=%async_computation.18 | async-start | bytes 4194304
  292.7 7.8 copy-start.6
  292.8 7.8 copy-start.13
  309.8 229.8 %reduce-scatter.19.cloned.1.call-start = ((), (), s32[]{:S(2)}) async-start(), calls=%async_computation.14 | async-start | bytes 294912
  312.5 264.1 %reduce-scatter.21.cloned.1.call-start = ((), (), s32[]{:S(2)}) async-start(), calls=%async_computation.15 | async-start | bytes 1179648
  480.3 7.8 copy-start.32
  488.0 190.1 %reduce-scatter.11.cloned.1.call-start = ((), (), s32[]{:S(2)}) async-start(), calls=%async_computation.10 | async-start | bytes 14155776 | tf_op jit(solution)/shard_map/reduce_scatter | solution.py:214
  496.4 232.7 %reduce-scatter.13.cloned.1.call-start = ((), (), s32[]{:S(2)}) async-start(), calls=%async_computation.11 | async-start | bytes 4718592 | tf_op jit(solution)/shard_map/reduce_scatter | solution.py:215
  502.4 396.2 %reduce-scatter.17.cloned.1.call-start = ((), (), s32[]{:S(2)}) async-start(), calls=%async_computation.13 | async-start | bytes 18874368 | tf_op jit(solution)/shard_map/reduce_scatter | solution.py:217
  515.9 552.4 %reduce-scatter.15.cloned.1.call-start = ((), (), s32[]{:S(2)}) async-start(), calls=%async_computation.12 | async-start | bytes 18874368 | tf_op jit(solution)/shard_map/reduce_scatter | solution.py:216
  525.9 12.5 %copy-start.40 = (u32[32]{0:T(128)S(1)}, u32[32]{0:T(128)}, u32[]{:S(2)}) copy-start(u32[32]{0:T(128)} %constant.135) | copy-start | bytes 388
  (23 other events, 71.6 us)
Sparse Core Ops, SparseCore 0:
  9.6 33.4 all-gather.13
  45.3 64.2 all-gather.11
  111.1 80.2 all-gather.15
  192.8 80.9 all-gather.17
  309.9 170.2 all-reduce.5
  482.9 31.4 reduce-scatter.18
  517.3 30.7 reduce-scatter.20
  550.4 127.6 reduce-scatter.10
  681.0 48.1 reduce-scatter.12
  731.9 166.6 reduce-scatter.16
  901.5 166.6 reduce-scatter.14
where the time goes:
time: 1080 us; the launch traced here: 1070 us
  waiting for transfers between devices  768 us (71%)
  blocking collectives  119 us (11%)
  matrix products  103 us (10%)
  local copies, waits for them, and re-layouts  44.4 us (4%)
  other arithmetic  24.8 us (2%)
  between operations  16 us (1%)
    reduce_scatter x1, waiting for transfers between devices, per_device(): lax.psum_scatter(dup_w, 'dp', scatter_dimension=0, tiled=True)  170 us
    reduce_scatter x1, waiting for transfers between devices, per_device(): lax.psum_scatter(ddown_w, 'dp', scatter_dimension=1, tiled=True)  169 us
    psum x1, waiting for transfers between devices, per_device(): branch_sum = lax.psum(attn_part + ffn_part, 'tensor')  168 us
    reduce_scatter x1, waiting for transfers between devices, per_device(): lax.psum_scatter(dqkv_w, 'dp', scatter_dimension=1, tiled=True)  90.4 us
    all_gather x1, waiting for transfers between devices, per_device(): lax.all_gather(down_weight, 'dp', axis=1, tiled=True)  72.7 us
    reduce_scatter x1, waiting for transfers between devices, per_device(): lax.psum_scatter(dout_w, 'dp', scatter_dimension=1, tiled=True)  48 us
    all_gather x1, waiting for transfers between devices, per_device(): lax.all_gather(up_weight, 'dp', axis=0, tiled=True)  30.5 us
    unnamed x1, blocking collectives  27.4 us
  transfers between devices with their start and end apart: 11, of which 8 were waited for; matrix products, arithmetic and copies ran while one was open for 12% of the time, Pallas kernels for 0%

commit v1 on v0

--- a/solution.py
+++ b/solution.py
@@ -140,7 +140,7 @@
     up_pre = jnp.dot(ffn_in, up_full, preferred_element_type=jnp.float32) + up_b.astype(jnp.float32)
     hidden = gelu_exact(up_pre).astype(jnp.bfloat16)
     ffn_part = jnp.dot(hidden, down_full, preferred_element_type=jnp.float32)
-    branch_sum = lax.psum(attn_part + ffn_part, "tensor")
+    branch_sum = lax.psum((attn_part + ffn_part).astype(jnp.bfloat16), "tensor").astype(jnp.float32)
     block_output = (x_rows + branch_sum + outb_full.astype(jnp.float32)).astype(jnp.bfloat16)
     qkv_back, out_back, up_back, down_back = (qkv_full, out_full, up_full, down_full)
     row_valid = (positions < seq_len).astype(jnp.float32)[:, None]
@@ -204,17 +204,18 @@
             jnp.sum(ffn_back, axis=0),
         ]
     )
-    norm_grad, stat_sum = lax.psum((norm_part, norm_stats), "tensor")
+    norm_grad = lax.psum(norm_part.astype(jnp.bfloat16), "tensor").astype(jnp.float32)
+    stat_sum = lax.psum(norm_stats, "tensor")
     grad_mean = jnp.mean(norm_grad, axis=-1, keepdims=True)
     grad_proj = jnp.mean(norm_grad * normed, axis=-1, keepdims=True)
     dblock_input = (grad_rows + inv_std * (norm_grad - grad_mean - normed * grad_proj)).astype(
         jnp.bfloat16
     )
     dqkv_sent, dout_sent, dup_sent, ddown_sent, dqkvb_sent, dupb_sent, doutb_sent, stats_sent = (
-        lax.psum_scatter(dqkv_w, "dp", scatter_dimension=1, tiled=True),
-        lax.psum_scatter(dout_w, "dp", scatter_dimension=1, tiled=True),
-        lax.psum_scatter(dup_w, "dp", scatter_dimension=0, tiled=True),
-        lax.psum_scatter(ddown_w, "dp", scatter_dimension=1, tiled=True),
+        lax.psum_scatter(dqkv_w.astype(jnp.bfloat16), "dp", scatter_dimension=1, tiled=True).astype(jnp.float32),
+        lax.psum_scatter(dout_w.astype(jnp.bfloat16), "dp", scatter_dimension=1, tiled=True).astype(jnp.float32),
+        lax.psum_scatter(dup_w.astype(jnp.bfloat16), "dp", scatter_dimension=0, tiled=True).astype(jnp.float32),
+        lax.psum_scatter(ddown_w.astype(jnp.bfloat16), "dp", scatter_dimension=1, tiled=True).astype(jnp.float32),
         lax.psum_scatter(dqkv_b, "dp", scatter_dimension=1, tiled=True),
         lax.psum_scatter(dup_b, "dp", scatter_dimension=0, tiled=True),
         lax.psum_scatter(dout_b, "dp", scatter_dimension=0, tiled=True),

time: 1080 us -> 778 us (0.72)
  waiting for transfers between devices: 768 us -> 471 us
    reduce_scatter x4, waiting for transfers between devices: 477 us -> 254 us  [the longest x1 87.6 us: per_device(): lax.psum_scatter(dup_w.astype(jnp.bfloat16), 'dp', scatter_dimension=0, t...]
    psum x1, waiting for transfers between devices: 168 us -> 93.9 us  [per_device(): lax.psum((attn_part + ffn_part).astype(jnp.bfloat16), 'tensor')]
    unnamed x109 -> x105, local copies, waits for them, and re-layouts: 24.2 us -> 21.8 us
  transfers between devices with their start and end apart: 11 -> 11, of which waited for: 8 -> 8; matrix products, arithmetic and copies ran while one was open for 12% -> 17% of each run, Pallas kernels for 0% -> 0%
where the time goes in v1:
time: 778 us; the launch traced here: 772 us
  waiting for transfers between devices  471 us (61%)
  blocking collectives  118 us (15%)
  matrix products  92.9 us (12%)
  local copies, waits for them, and re-layouts  42.1 us (5%)
  other arithmetic  31.1 us (4%)
  between operations  16 us (2%)
    psum x1, waiting for transfers between devices, per_device(): lax.psum((attn_part + ffn_part).astype(jnp.bfloat16), 'tensor')  93.9 us
    reduce_scatter x1, waiting for transfers between devices, per_device(): lax.psum_scatter(dup_w.astype(jnp.bfloat16), 'dp', scatter_dimension=0, t...  87.6 us
    reduce_scatter x1, waiting for transfers between devices, per_device(): lax.psum_scatter(ddown_w.astype(jnp.bfloat16), 'dp', scatter_dimension=1,...  87.5 us
    all_gather x1, waiting for transfers between devices, per_device(): lax.all_gather(down_weight, 'dp', axis=1, tiled=True)  71.9 us
    reduce_scatter x1, waiting for transfers between devices, per_device(): lax.psum_scatter(dqkv_w.astype(jnp.bfloat16), 'dp', scatter_dimension=1,...  57.3 us
    all_gather x1, waiting for transfers between devices, per_device(): lax.all_gather(up_weight, 'dp', axis=0, tiled=True)  31.4 us
    unnamed x1, blocking collectives  26.9 us
    reduce_scatter x1, waiting for transfers between devices, per_device(): lax.psum_scatter(dout_w.astype(jnp.bfloat16), 'dp', scatter_dimension=1,...  22 us
  transfers between devices with their start and end apart: 11, of which 8 were waited for; matrix products, arithmetic and copies ran while one was open for 17% of the time, Pallas kernels for 0%

profile of v1, /device:TPU:0, one launch (start us, length us, event | category | flops | bytes accessed | tf_op | source)
XLA Modules:
  0.0 772.1 jit_solution(17943356464360327234)
XLA Ops:
  12.4 13.6 %all-gather.5 = bf16[8,1,256]{2,1,0:T(2,128)(2,1)S(1)} all-gather(bf16[1,1,256]{2,1,0:T(2,128)(2,1)S(1)} %reshape.282), channel_id=1, replica_groups=mesh['dp'=8,'tensor'=4] {'dp'}, dimensions={0}, use_global_device_ids=true | all-gather | bytes 4608 | tf_op jit(solution)/shard_map/all_gather | solution.py:67
  26.6 9.0 %all-gather.4 = bf16[8,1,256]{2,1,0:T(2,128)(2,1)S(1)} all-gather(bf16[1,1,256]{2,1,0:T(2,128)(2,1)S(1)} %reshape.280), channel_id=1, replica_groups=mesh['dp'=8,'tensor'=4] {'dp'}, dimensions={0}, use_global_device_ids=true | all-gather | bytes 4608 | tf_op jit(solution)/shard_map/all_gather | solution.py:72
  36.2 10.4 %all-gather.3 = bf16[8,1,256]{2,1,0:T(2,128)(2,1)S(1)} all-gather(bf16[1,1,256]{2,1,0:T(2,128)(2,1)S(1)} %reshape.278), channel_id=1, replica_groups=mesh['dp'=8,'tensor'=4] {'dp'}, dimensions={0}, use_global_device_ids=true | all-gather | bytes 4608 | tf_op jit(solution)/shard_map/all_gather | solution.py:71
  47.2 8.7 %all-gather = bf16[8,1,256]{2,1,0:T(2,128)(2,1)S(1)} all-gather(bf16[1,1,256]{2,1,0:T(2,128)(2,1)S(1)} %reshape.272), channel_id=1, replica_groups=mesh['dp'=8,'tensor'=4] {'dp'}, dimensions={0}, use_global_device_ids=true | all-gather | bytes 4608 | tf_op jit(solution)/shard_map/all_gather | solution.py:69
  56.0 10.5 %all-gather.2 = bf16[8,64,3]{1,2,0:T(4,128)(2,1)S(1)} all-gather(bf16[1,64,3]{1,2,0:T(4,128)(2,1)S(1)} %bitcast.121), channel_id=1, replica_groups=mesh['dp'=8,'tensor'=4] {'dp'}, dimensions={0}, use_global_device_ids=true | all-gather | bytes 3456 | tf_op jit(solution)/shard_map/all_gather | solution.py:66
  66.6 17.3 %all-gather.1 = bf16[8,1,256]{2,1,0:T(2,128)(2,1)S(1)} all-gather(bf16[1,1,256]{2,1,0:T(2,128)(2,1)S(1)} %reshape.274), channel_id=1, replica_groups=mesh['dp'=8,'tensor'=4] {'dp'}, dimensions={0}, use_global_device_ids=true | all-gather | bytes 4608 | tf_op jit(solution)/shard_map/all_gather | solution.py:70
  87.6 4.4 convolution_convert_fusion.3
  92.0 17.5 %all-gather.12.cloned.1.call-done = bf16[3,2048,512]{1,2,0:T(8,128)(2,1)} async-done(((bf16[3,256,512]{1,2,0:T(8,128)(2,1)}), bf16[3,2048,512]{1,2,0:T(8,128)(2,1)}) %all-gather.12.cloned.1.call-update) | async-done | bytes 6291472 | tf_op jit(solution)/shard_map/all_gather | solution.py:62
  109.5 6.1 add_bitcast_fusion
  132.6 2.8 fusion.62
  139.8 3.4 fusion.37
  160.0 31.4 %all-gather.16.cloned.1.call-done = bf16[2048,2048]{1,0:T(8,128)(2,1)} async-done(((bf16[256,2048]{1,0:T(8,128)(2,1)}), bf16[2048,2048]{1,0:T(8,128)(2,1)}) %all-gather.16.cloned.1.call-update) | async-done | bytes 8388624 | tf_op jit(solution)/shard_map/all_gather | solution.py:64
  191.4 10.6 %multiply_convert_fusion = (bf16[512,2048]{1,0:T(8,128)(2,1)}, f32[512,2048]{1,0:T(8,128)}) fusion(f32[2048]{0:T(1024)S(1)} %bitcast.118, bf16[2048,2048]{1,0:T(8,128)(2,1)} %all-gather.16.cloned.1.call-done, bf16[512,2048]{1,0:T(8,128)(2,1)S(1)} %copy-done, f32[2048]{0:T(1024)S(1)} %bitcast.108, f32[2048]{0:T(1024)S(1)} %bitcast.110, ...), kind=kOutput, calls=%fused_computation.44 | convolution fusion | flops 4307550208 | bytes 16805888 | tf_op jit(solution)/shard_map/dot_general | solution.py:140
  202.0 71.9 %all-gather.18.cloned.1.call-done = bf16[2048,2048]{1,0:T(8,128)(2,1)} async-done(((bf16[2048,256]{1,0:T(8,128)(2,1)}), bf16[2048,2048]{1,0:T(8,128)(2,1)}) %all-gather.18.cloned.1.call-update) | async-done | bytes 8388624 | tf_op jit(solution)/shard_map/all_gather | solution.py:65
  273.9 9.7 %fusion.63 = (f32[2048]{0:T(1024)S(1)}, bf16[512,2048]{1,0:T(8,128)(2,1)S(1)}) fusion(f32[512,2048]{1,0:T(8,128)} %get-tuple-element.170, f32[2048]{0:T(1024)S(1)} %bitcast.119, bf16[2048,2048]{1,0:T(8,128)(2,1)} %all-gather.18.cloned.1.call-done, bf16[512,2048]{1,0:T(8,128)(2,1)} %param.27, f32[512]{0:T(512)S(1)} %fusion.47), kind=kOutput, calls=%fused_computation.106 | convolution fusion | flops 4310693888 | bytes 16795648 | tf_op jit(solution)/shard_map/ld,fd->lf/dot_general | solution.py:151
  283.6 4.5 fusion.39
  288.2 8.5 %fusion.64 = f32[512,2048]{1,0:T(8,128)S(1)} fusion(bf16[512,2048]{1,0:T(8,128)(2,1)S(1)} %copy-done.38, bf16[2048,2048]{1,0:T(8,128)(2,1)} %all-gather.18.cloned.1.call-done), kind=kOutput, calls=%fused_computation.107 | convolution fusion | flops 4294967296 | bytes 14680064 | tf_op jit(solution)/shard_map/dot_general | solution.py:142
  299.4 5.4 fusion.27
  308.0 4.9 convolution_convert_fusion.2
  313.0 93.9 %all-reduce.6.cloned.1.call-done = (bf16[512,2048]{1,0:T(8,128)(2,1)}, bf16[512,2048]{1,0:T(8,128)(2,1)}) async-done(((bf16[512,2048]{1,0:T(8,128)(2,1)}, bf16[512,2048]{1,0:T(8,128)(2,1)}), (bf16[512,2048]{1,0:T(8,128)(2,1)}, bf16[512,2048]{1,0:T(8,128)(2,1)})) %all-reduce.6.cloned.1.call-update) | async-done | bytes 4194320 | tf_op jit(solution)/shard_map/psum | solution.py:143
  406.8 5.6 fusion.15
  413.9 7.5 convert_bitcast_fusion
  421.4 8.8 %convolution_convert_fusion.1 = bf16[2048,2048]{1,0:T(8,128)(2,1)} fusion(bf16[512,2048]{1,0:T(8,128)(2,1)} %copy-done.39, bf16[512,2048]{1,0:T(8,128)(2,1)S(1)} %copy-done, f32[2048]{0:T(1024)S(1)} %bitcast.109, f32[2048]{0:T(1024)S(1)} %bitcast.112, f32[512]{0:T(512)S(1)} %add_rsqrt_fusion, f32[512]{0:T(512)S(1)} %broadcast_multiply_fusion.3), kind=kOutput, calls=%fused_computation.1 | convolution fusion | flops 4305453056 | bytes 12603392 | tf_op jit(solution)/shard_map/ld,lf->df/dot_general | solution.py:155
  430.4 10.1 %convolution_convert_fusion = bf16[2048,2048]{1,0:T(8,128)(2,1)} fusion(bf16[512,2048]{1,0:T(8,128)(2,1)} %get-tuple-element.169, bf16[512,2048]{1,0:T(8,128)(2,1)} %param.27, f32[512]{0:T(512)S(1)} %fusion.47), kind=kOutput, calls=%fused_computation | convolution fusion | flops 4302307328 | bytes 12584960 | tf_op jit(solution)/shard_map/lf,ld->fd/dot_general | solution.py:150
  441.2 11.7 %all-gather.6 = bf16[8,1,256]{2,1,0:T(2,128)(2,1)S(1)} all-gather(bf16[1,1,256]{2,1,0:T(2,128)(2,1)S(1)} %reshape.284), channel_id=1, replica_groups=mesh['dp'=8,'tensor'=4] {'dp'}, dimensions={0}, use_global_device_ids=true | all-gather | bytes 4608 | tf_op jit(solution)/shard_map/all_gather | solution.py:68
  455.6 22.0 %reduce-scatter.13.cloned.1.call-done = bf16[512,256]{1,0:T(8,128)(2,1)} async-done(((bf16[512,2048]{1,0:T(8,128)(2,1)}), bf16[512,256]{1,0:T(8,128)(2,1)}) %reduce-scatter.13.cloned.1.call-update) | async-done | bytes 262160 | tf_op jit(solution)/shard_map/reduce_scatter | solution.py:216
  479.4 6.1 fusion.28
  485.5 26.9 %all-reduce.2 = (f32[2048]{0:T(1024)S(1)}, f32[2048]{0:T(1024)S(1)}) all-reduce(f32[2048]{0:T(1024)S(1)} %get-tuple-element.139, f32[2048]{0:T(1024)S(1)} %get-tuple-element.173), channel_id=6, replica_groups=mesh['dp'=8,'tensor'=4] {'dp'}, use_global_device_ids=true, to_apply=%region_19.20.clone | all-reduce | flops 4096 | bytes 32768
  514.7 9.6 %psum.24 = f32[4,256]{1,0:T(4,128)S(1)} all-reduce(f32[4,256]{1,0:T(4,128)S(1)} %copy.153), channel_id=1, replica_groups=mesh['dp'=8,'tensor'=4] {'tensor'}, use_global_device_ids=true, to_apply=%region_12.13 | all-reduce | flops 1024 | bytes 8192 | tf_op jit(solution)/shard_map/psum | solution.py:208
  524.8 57.3 %reduce-scatter.11.cloned.1.call-done = bf16[3,256,512]{1,2,0:T(8,128)(2,1)} async-done(((bf16[3,2048,512]{1,2,0:T(8,128)(2,1)}), bf16[3,256,512]{1,2,0:T(8,128)(2,1)}) %reduce-scatter.11.cloned.1.call-update) | async-done | bytes 786448 | tf_op jit(solution)/shard_map/reduce_scatter | solution.py:215
  584.7 87.6 %reduce-scatter.15.cloned.1.call-done = bf16[256,2048]{1,0:T(8,128)(2,1)} async-done(((bf16[2048,2048]{1,0:T(8,128)(2,1)}), bf16[256,2048]{1,0:T(8,128)(2,1)}) %reduce-scatter.15.cloned.1.call-update) | async-done | bytes 1048592 | tf_op jit(solution)/shard_map/reduce_scatter | solution.py:217
  675.1 87.5 %reduce-scatter.17.cloned.1.call-done = bf16[2048,256]{1,0:T(8,128)(2,1)} async-done(((bf16[2048,2048]{1,0:T(8,128)(2,1)}), bf16[2048,256]{1,0:T(8,128)(2,1)}) %reduce-scatter.17.cloned.1.call-update) | async-done | bytes 1048592 | tf_op jit(solution)/shard_map/reduce_scatter | solution.py:218
  (179 shorter events, 70.9 us)
Async XLA Ops:
  7.2 19.4 %copy-start.32 = (bf16[256]{0:T(256)(128)(2,1)S(1)}, bf16[256]{0:T(256)(128)(2,1)}, u32[]{:S(2)}) copy-start(bf16[256]{0:T(256)(128)(2,1)} %param.32) | copy-start | bytes 1540
  7.2 29.0 %copy-start.33 = (bf16[256]{0:T(256)(128)(2,1)S(1)}, bf16[256]{0:T(256)(128)(2,1)}, u32[]{:S(2)}) copy-start(bf16[256]{0:T(256)(128)(2,1)} %param.31) | copy-start | bytes 1540
  7.2 40.0 %copy-start.34 = (bf16[256]{0:T(256)(128)(2,1)S(1)}, bf16[256]{0:T(256)(128)(2,1)}, u32[]{:S(2)}) copy-start(bf16[256]{0:T(256)(128)(2,1)} %param.29) | copy-start | bytes 1540
  7.2 48.7 %copy-start.29 = (bf16[3,64]{1,0:T(4,128)(2,1)S(1)}, bf16[3,64]{1,0:T(4,128)(2,1)}, u32[]{:S(2)}) copy-start(bf16[3,64]{1,0:T(4,128)(2,1)} %param.34) | copy-start | bytes 1156
  7.2 59.3 %copy-start.35 = (bf16[256]{0:T(256)(128)(2,1)S(1)}, bf16[256]{0:T(256)(128)(2,1)}, u32[]{:S(2)}) copy-start(bf16[256]{0:T(256)(128)(2,1)} %param.30) | copy-start | bytes 1540
  7.2 76.7 %copy-start = (bf16[512,2048]{1,0:T(8,128)(2,1)S(1)}, bf16[512,2048]{1,0:T(8,128)(2,1)}, u32[]{:S(2)}) copy-start(bf16[512,2048]{1,0:T(8,128)(2,1)} %param.26) | copy-start | bytes 6291460
  7.3 80.4 %all-gather.14.cloned.1.call-start = ((), (), s32[]{:S(2)}) async-start(), calls=%async_computation.7 | async-start | bytes 2359296 | tf_op jit(solution)/shard_map/all_gather | solution.py:63
  8.0 101.5 %all-gather.12.cloned.1.call-start = ((), (), s32[]{:S(2)}) async-start(), calls=%async_computation.6 | async-start | bytes 7077888 | tf_op jit(solution)/shard_map/all_gather | solution.py:62
  10.3 181.1 %all-gather.16.cloned.1.call-start = ((), (), s32[]{:S(2)}) async-start(), calls=%async_computation.8 | async-start | bytes 9437184 | tf_op jit(solution)/shard_map/all_gather | solution.py:64
  11.1 262.8 %all-gather.18.cloned.1.call-start = ((), (), s32[]{:S(2)}) async-start(), calls=%async_computation.9 | async-start | bytes 9437184 | tf_op jit(solution)/shard_map/all_gather | solution.py:65
  11.7 395.2 %all-reduce.6.cloned.1.call-start = ((), (), s32[]{:S(2)}) async-start(), calls=%async_computation.16 | async-start | bytes 8388608 | tf_op jit(solution)/shard_map/psum | solution.py:143
  56.0 53.6 %copy-start.24 = (f32[8,1,256]{2,1,0:T(1,128)}, f32[8,1,256]{2,1,0:T(1,128)S(1)}, u32[]{:S(2)}) copy-start(f32[8,1,256]{2,1,0:T(1,128)S(1)} %convert_element_type.159) | copy-start | bytes 24580
  83.9 25.6 %copy-start.26 = (f32[8,1,256]{2,1,0:T(1,128)}, f32[8,1,256]{2,1,0:T(1,128)S(1)}, u32[]{:S(2)}) copy-start(f32[8,1,256]{2,1,0:T(1,128)S(1)} %convert_element_type.160) | copy-start | bytes 24580
  132.5 5.6 copy-start.13
  132.5 5.6 copy-start.15
  149.7 41.7 %copy-start.22 = (f32[8,1,256]{2,1,0:T(1,128)S(1)}, f32[8,1,256]{2,1,0:T(1,128)}, u32[]{:S(2)}) copy-start(f32[8,1,256]{2,1,0:T(1,128)} %convert_element_type.163) | copy-start | bytes 24580
  149.7 41.7 %copy-start.23 = (f32[8,1,256]{2,1,0:T(1,128)S(1)}, f32[8,1,256]{2,1,0:T(1,128)}, u32[]{:S(2)}) copy-start(f32[8,1,256]{2,1,0:T(1,128)} %convert_element_type.162) | copy-start | bytes 24580
  149.7 41.7 %copy-start.28 = (f32[8,1,256]{2,1,0:T(1,128)S(1)}, f32[8,1,256]{2,1,0:T(1,128)}, u32[]{:S(2)}) copy-start(f32[8,1,256]{2,1,0:T(1,128)} %convert_element_type.164) | copy-start | bytes 24580
  273.9 9.7 %copy-start.30 = (bf16[2048,2048]{1,0:T(8,128)(2,1)S(1)}, bf16[2048,2048]{1,0:T(8,128)(2,1)}, u32[]{:S(2)}) copy-start(bf16[2048,2048]{1,0:T(8,128)(2,1)} %all-gather.16.cloned.1.call-done) | copy-start | bytes 25165828
  283.6 15.8 %slice-start = ((s8[6291456]{0:T(1024)(128)(4,1)}), s8[2097152]{0:T(1024)(128)(4,1)S(1)}, s32[]{:S(2)}) async-start(s8[6291456]{0:T(1024)(128)(4,1)} %bitcast.126), calls=%async_computation.17 | async-start | bytes 4194304
  288.1 11.2 %copy-start.5 = (f32[512,2048]{1,0:T(8,128)}, f32[512,2048]{1,0:T(8,128)S(1)}, u32[]{:S(2)}) copy-start(f32[512,2048]{1,0:T(8,128)S(1)} %fusion.39) | copy-start | bytes 12582916
  288.1 8.5 %copy-start.8 = (bf16[512,2048]{1,0:T(8,128)(2,1)S(1)}, bf16[512,2048]{1,0:T(8,128)(2,1)}, u32[]{:S(2)}) copy-start(bf16[512,2048]{1,0:T(8,128)(2,1)} %all-gather.14.cloned.1.call-done) | copy-start | bytes 6291460
  288.1 8.5 %copy-start.12 = (bf16[2,256,512]{2,1,0:T(8,128)(2,1)S(1)}, bf16[2,256,512]{2,1,0:T(8,128)(2,1)}, u32[]{:S(2)}) copy-start(bf16[2,256,512]{2,1,0:T(8,128)(2,1)} %get-tuple-element.168) | copy-start | bytes 1572868
  288.2 11.2 %slice-start.1 = ((s8[6291456]{0:T(1024)(128)(4,1)}), s8[4194304]{0:T(1024)(128)(4,1)S(1)}, s32[]{:S(2)}) async-start(s8[6291456]{0:T(1024)(128)(4,1)} %bitcast.126), calls=%async_computation.18 | async-start | bytes 8388608
  304.8 149.4 %reduce-scatter.19.cloned.1.call-start = ((), (), s32[]{:S(2)}) async-start(), calls=%async_computation.14 | async-start | bytes 294912
  307.6 170.1 %reduce-scatter.13.cloned.1.call-start = ((), (), s32[]{:S(2)}) async-start(), calls=%async_computation.11 | async-start | bytes 2359296 | tf_op jit(solution)/shard_map/reduce_scatter | solution.py:216
  312.9 200.8 %reduce-scatter.21.cloned.1.call-start = ((), (), s32[]{:S(2)}) async-start(), calls=%async_computation.15 | async-start | bytes 1179648
  406.8 7.0 copy-start.27
  413.8 168.4 %reduce-scatter.11.cloned.1.call-start = ((), (), s32[]{:S(2)}) async-start(), calls=%async_computation.10 | async-start | bytes 7077888 | tf_op jit(solution)/shard_map/reduce_scatter | solution.py:215
  421.4 251.0 %reduce-scatter.15.cloned.1.call-start = ((), (), s32[]{:S(2)}) async-start(), calls=%async_computation.12 | async-start | bytes 9437184 | tf_op jit(solution)/shard_map/reduce_scatter | solution.py:217
  430.2 332.5 %reduce-scatter.17.cloned.1.call-start = ((), (), s32[]{:S(2)}) async-start(), calls=%async_computation.13 | async-start | bytes 9437184 | tf_op jit(solution)/shard_map/reduce_scatter | solution.py:218
  440.5 12.4 %copy-start.37 = (u32[32]{0:T(128)S(1)}, u32[32]{0:T(128)}, u32[]{:S(2)}) copy-start(u32[32]{0:T(128)} %constant.135) | copy-start | bytes 388
  (21 other events, 61.9 us)
Sparse Core Ops, SparseCore 0:
  9.6 33.4 all-gather.13
  45.3 64.2 all-gather.11
  111.1 80.2 all-gather.15
  192.9 80.9 all-gather.17
  305.0 101.8 all-reduce.5
  409.5 30.8 reduce-scatter.18
  443.2 34.3 reduce-scatter.12
  480.5 31.1 reduce-scatter.20
  514.0 68.1 reduce-scatter.10
  584.3 88.0 reduce-scatter.14
  674.7 87.9 reduce-scatter.16

commit v2 on v0

v2 whole, which is shorter than its diff:
```python
import functools
import math
import types

import jax
import jax.numpy as jnp
from jax import lax
from jax.experimental import pallas as pl
from jax.experimental.pallas import tpu as pltpu
from jax.sharding import PartitionSpec as P

HD = 256
ROT = 64
UNIT = 256
ROWS = 128
MESH = pl.DeviceIdType.MESH

norm_eps = 1e-05
rope_base = 10000.0

F32 = jnp.float32
BF16 = jnp.bfloat16


def dot(a, b):
    return lax.dot_general(a, b, (((1,), (0,)), ((), ())), preferred_element_type=F32)


def dot_nt(a, b):
    return lax.dot_general(a, b, (((1,), (1,)), ((), ())), preferred_element_type=F32)


def dot_tn(a, b):
    return lax.dot_general(a, b, (((0,), (0,)), ((), ())), preferred_element_type=F32)


def ds(i, size):
    return pl.ds(pl.multiple_of(i * size, size), size)


def layer_kernel(
    d,
    len_ref,
    x_hbm,
    cot_hbm,
    wl,
    norm_ref,
    bias_ref,
    rope_ref,
    part_hbm,
    dw_hbm,
    small_ref,
    bg_ref,
    W,
    A,
    At,
    X,
    Acc,
    Y,
    G,
    QK,
    PB,
    DS,
    S,
    SB,
    SR,
    LR,
    stage,
    in_sem,
    own_sem,
    ag_recv,
    agR,
    agL,
    agS,
    credit,
    sb_sem,
    sr_sem,
    ls_sem,
    lr_sem,
    out_sem,
):
    n, T, D, Dsl, U = d.n, d.T, d.D, d.Dsl, d.U
    NW, NS, NSR, NLR, L, LAG = d.NW, d.NS, d.NSR, d.NLR, d.L, d.LAG
    A4 = 4 * d.heads
    me = lax.axis_index("dp")
    z = me // 2
    c = me % 2
    right, left, sib = me + 2, me - 2, z * 2 + (1 - c)
    has_r = z < n - 1
    has_l = z > 0
    seq_len = len_ref[0]

    def rcopy(src, dst, ss, rs, dev):
        return pltpu.make_async_remote_copy(
            src_ref=src,
            dst_ref=dst,
            send_sem=ss,
            recv_sem=rs,
            device_id={"dp": dev},
            device_id_type=MESH,
        )

    def signal(sem, dev):
        pl.semaphore_signal(sem, inc=1, device_id={"dp": dev}, device_id_type=MESH)

    def aidx(u):
        attn = jnp.where(u % 4 == 3, 2, 0)
        ffn = jnp.where((u - A4) % 2 == 0, 1, 2)
        return jnp.where(u < A4, attn, ffn)

    def ag_first(u):
        slot = u % NW

        @pl.when(u >= NW)
        def _():
            @pl.when(has_r)
            def _():
                pl.semaphore_wait(credit.at[0], 1)

            @pl.when(has_l)
            def _():
                pl.semaphore_wait(credit.at[1], 1)

            pl.semaphore_wait(credit.at[2], 1)

        pltpu.make_async_copy(wl.at[u], W.at[slot, me], own_sem.at[slot]).start()

        @pl.when(has_r)
        def _():
            rcopy(wl.at[u], W.at[slot, me], agR.at[slot, z], ag_recv.at[slot, me], right).start()

        @pl.when(has_l)
        def _():
            rcopy(wl.at[u], W.at[slot, me], agL.at[slot, z], ag_recv.at[slot, me], left).start()

        rcopy(wl.at[u], W.at[slot, me], agS.at[slot, z], ag_recv.at[slot, me], sib).start()

    def ag_tile(slot, sj, sem, dev):
        return rcopy(W.at[slot, sj], W.at[slot, sj], sem, ag_recv.at[slot, sj], dev)

    def ag_relay(u, k):
        slot = u % NW

        @pl.when(z - k >= 0)
        def _():
            j = z - k
            sj = j * 2 + c
            ag_tile(slot, sj, agS.at[slot, j], sib).wait_recv()

            @pl.when(has_r)
            def _():
                ag_tile(slot, sj, agR.at[slot, j], right).start()

            ag_tile(slot, sj, agS.at[slot, j], sib).start()

        @pl.when(z + k <= n - 1)
        def _():
            j = z + k
            sj = j * 2 + c
            ag_tile(slot, sj, agS.at[slot, j], sib).wait_recv()

            @pl.when(has_l)
            def _():
                ag_tile(slot, sj, agL.at[slot, j], left).start()

            ag_tile(slot, sj, agS.at[slot, j], sib).start()

    def ag_step(s):
        @pl.when(s + L < U)
        def _():
            ag_first(s + L)

        for k in range(1, n):
            u = s + L - k

            @pl.when((u >= 0) & (u < U))
            def _(u=u, k=k):
                ag_relay(u, k)

    def ag_wait(u):
        slot = u % NW
        pltpu.make_async_copy(wl.at[u], W.at[slot, me], own_sem.at[slot]).wait()
        for j in range(n):
            ag_tile(slot, j * 2 + 1 - c, agS.at[slot, j], sib).wait_recv()

    def ag_finish(u):
        slot = u % NW
        for j in range(n):

            @pl.when(has_r & (j <= z))
            def _(j=j):
                ag_tile(slot, j * 2 + c, agR.at[slot, j], right).wait_send()

            @pl.when(has_l & (j >= z))
            def _(j=j):
                ag_tile(slot, j * 2 + c, agL.at[slot, j], left).wait_send()

            ag_tile(slot, j * 2 + c, agS.at[slot, j], sib).wait_send()

        @pl.when(u + NW < U)
        def _():
            @pl.when(has_r)
            def _():
                signal(credit.at[1], right)

            @pl.when(has_l)
            def _():
                signal(credit.at[0], left)

            signal(credit.at[2], sib)

    def sb_copy(u):
        return rcopy(
            SB.at[u % 2], SR.at[u % NSR], sb_sem.at[u % 2], sr_sem.at[u % NSR], sib
        )

    def ls_copy(v, zt, to_right):
        slot = zt + 1 if to_right else zt
        return rcopy(
            S.at[v % NS, zt],
            LR.at[v % NLR, slot],
            ls_sem.at[v % NS, zt],
            lr_sem.at[v % NLR, slot],
            right if to_right else left,
        )

    def dw_half(u, core, put):
        a = aidx(u)
        g = G[u % 4]
        for j in range(n):
            put(j, dot(At[a, core, j * Dsl : (j + 1) * Dsl, :], g).astype(BF16))

    def dw_sib(u):
        @pl.when(u >= 2)
        def _():
            sb_copy(u - 2).wait_send()

        def put(j, v):
            SB[u % 2, j] = v

        dw_half(u, 1 - c, put)
        sb_copy(u).start()

    def rs_finish(v):
        for zt in range(n):

            @pl.when(zt != z)
            def _(zt=zt):
                ls_copy(v, zt, True).wait_send()

    def dw_own(u):
        @pl.when(u >= NS)
        def _():
            rs_finish(u - NS)

        def put(j, v):
            S[u % NS, j] = v

        dw_half(u, c, put)

    def add_into(v, zt, other):
        S[v % NS, zt] = (S[v % NS, zt].astype(F32) + other.astype(F32)).astype(BF16)

    def combine(v):
        sb_copy(v).wait_recv()
        for zt in range(n):
            add_into(v, zt, SR[v % NSR, zt])

    def send_right(v):
        for zt in range(1, n):

            @pl.when(zt > z)
            def _(zt=zt):
                @pl.when(has_l)
                def _():
                    ls_copy(v, zt, True).wait_recv()
                    add_into(v, zt, LR[v % NLR, zt + 1])

                ls_copy(v, zt, True).start()

    def send_left(v):
        for zt in range(0, n - 1):

            @pl.when(zt < z)
            def _(zt=zt):
                @pl.when(has_r)
                def _():
                    ls_copy(v, zt, False).wait_recv()
                    add_into(v, zt, LR[v % NLR, zt])

                ls_copy(v, zt, False).start()

    def out_copy(v):
        return pltpu.make_async_copy(stage.at[v % 2], dw_hbm.at[v], out_sem.at[v % 2])

    def final(v):
        @pl.when(v >= 2)
        def _():
            out_copy(v - 2).wait()

        slot = v % 2
        stage[slot] = S[v % NS, z].astype(F32)

        @pl.when(has_l)
        def _():
            ls_copy(v, z, True).wait_recv()
            stage[slot] += LR[v % NLR, z + 1].astype(F32)

        @pl.when(has_r)
        def _():
            ls_copy(v, z, False).wait_recv()
            stage[slot] += LR[v % NLR, z].astype(F32)

        out_copy(v).start()

    def rs_step(s):
        base = s - LAG - 1

        def guarded(v, f):
            @pl.when((v >= 0) & (v < U))
            def _():
                f(v)

        guarded(base, combine)
        guarded(base - z, send_right)
        guarded(base - (n - 1 - z), send_left)
        guarded(base - jnp.maximum(z, n - 1 - z), final)

    def layer_norm(x):
        mean = jnp.mean(x, axis=-1, keepdims=True)
        cen = x - mean
        inv = lax.rsqrt(jnp.mean(cen * cen, axis=-1, keepdims=True) + norm_eps)
        return cen * inv

    def ln_block(i):
        rows = ds(i, ROWS)
        normed = layer_norm(X[rows, :].astype(F32))
        A[0, rows, :] = (normed * norm_ref[0:1, :] + norm_ref[1:2, :]).astype(BF16)
        A[1, rows, :] = (normed * norm_ref[2:3, :] + norm_ref[3:4, :]).astype(BF16)
        pos = lax.broadcasted_iota(jnp.int32, (ROWS, D), 0) + i * ROWS
        grad = jnp.where(pos < seq_len, A[2, rows, :].astype(F32), 0.0)
        A[2, rows, :] = grad.astype(BF16)
        small_ref[4:5, :] += jnp.sum(grad, axis=0, keepdims=True)
        for a in range(3):
            for j in range(2 * n):
                At[a, j % 2, (j // 2) * Dsl : (j // 2 + 1) * Dsl, rows] = jnp.transpose(
                    A[a, rows, j * Dsl : (j + 1) * Dsl]
                )
            Acc[a, rows, :] = jnp.zeros((ROWS, D), F32)

    def y_step(u):
        ag_wait(u)
        w = W[u % NW].reshape(D, UNIT)
        Y[u % 4] = dot(A[aidx(u)], w)

    def acc_step(u):
        a = aidx(u)
        g = G[u % 4]
        for j in range(2 * n):
            cols = slice(j * Dsl, (j + 1) * Dsl)
            Acc[a, :, cols] += dot_nt(g, W[u % NW, j])

    lane = lax.broadcasted_iota(jnp.int32, (T, 128), 1)

    def rotate(y, sign):
        lo = y[:, :128]
        swapped = jnp.where(lane < 32, pltpu.roll(lo, 96, 1), pltpu.roll(lo, 32, 1))
        lo = lo * rope_ref[0] + swapped * (rope_ref[1] * sign)
        return jnp.concatenate([lo, y[:, 128:]], axis=1)

    def attn_core(s):
        u0 = s - 3
        QK[0] = rotate(Y[0] + bias_ref[u0, 0:1, :], 1.0).astype(BF16)
        QK[1] = rotate(Y[1] + bias_ref[u0 + 1, 0:1, :], 1.0).astype(BF16)
        QK[2] = (Y[2] + bias_ref[u0 + 2, 0:1, :]).astype(BF16)
        QK[3] = Y[3].astype(BF16)
        scale = 1.0 / math.sqrt(HD)

        def block(i, carry):
            rows = ds(i, ROWS)
            raw = dot_nt(QK[0, rows, :], QK[1]) * scale
            qpos = lax.broadcasted_iota(jnp.int32, (ROWS, T), 0) + i * ROWS
            kpos = lax.broadcasted_iota(jnp.int32, (ROWS, T), 1)
            scores = jnp.where((kpos <= qpos) & (kpos < seq_len), raw, -jnp.inf)
            top = jnp.max(scores, axis=-1, keepdims=True)
            e = jnp.exp(scores - top)
            p = e / jnp.sum(e, axis=-1, keepdims=True)
            pb = p.astype(BF16)
            PB[rows, :] = pb
            mixed = dot(pb, QK[2]).astype(BF16)
            G[3, rows, :] = mixed
            mg = QK[3, rows, :]
            delta = jnp.sum(mg.astype(F32) * mixed.astype(F32), axis=-1, keepdims=True)
            dp = dot_nt(mg, QK[2])
            dsb = (p * (dp - delta) * scale).astype(BF16)
            DS[rows, :] = dsb
            Y[0, rows, :] = dot(dsb, QK[1])
            return carry

        lax.fori_loop(0, T // ROWS, block, 0)
        Y[1] = dot_tn(DS[...], QK[0])
        for r in range(3):
            if r == 2:
                g = dot_tn(PB[...], QK[3])
            else:
                g = rotate(Y[r], -1.0)
            bg_ref[u0 + r] = jnp.broadcast_to(jnp.sum(g, axis=0, keepdims=True), (8, UNIT))
            G[r] = g.astype(BF16)

    def ffn_core(s):
        b = bias_ref[s - 1, 0:1, :]
        yu, yd = (s - 1) % 4, s % 4
        step = 64

        def block(i, total):
            rows = ds(i, step)
            v = Y[yu, rows, :] + b
            cdf2 = 1.0 + lax.erf(v * (1.0 / math.sqrt(2.0)))
            G[yd, rows, :] = (0.5 * v * cdf2).astype(BF16)
            slope = 0.5 * cdf2 + v * jnp.exp(-0.5 * v * v) * (1.0 / math.sqrt(2.0 * math.pi))
            g = Y[yd, rows, :] * slope
            G[yu, rows, :] = g.astype(BF16)
            return total + jnp.sum(g, axis=0, keepdims=True)

        total = lax.fori_loop(0, T // step, block, jnp.zeros((1, UNIT), F32))
        bg_ref[s - 1] = jnp.broadcast_to(total, (8, UNIT))

    barrier = pltpu.get_barrier_semaphore()

    @pl.when(has_r)
    def _():
        signal(barrier, right)

    @pl.when(has_l)
    def _():
        signal(barrier, left)

    signal(barrier, sib)
    peers = 1 + jnp.minimum(z, 1) + jnp.minimum(n - 1 - z, 1)
    pl.semaphore_wait(barrier, peers)

    x_in = pltpu.make_async_copy(x_hbm, X, in_sem.at[0])
    c_in = pltpu.make_async_copy(cot_hbm, A.at[2], in_sem.at[1])
    x_in.start()
    c_in.start()
    ag_step(-L)
    small_ref[...] = jnp.zeros_like(small_ref)
    bg_ref[...] = jnp.zeros_like(bg_ref)
    x_in.wait()
    c_in.wait()
    blocks = T // ROWS

    def fill(i, carry):
        @pl.when(i < blocks)
        def _():
            ln_block(i)

        @pl.when(i < L - 1)
        def _():
            ag_step(i + 1 - L)

        return carry

    lax.fori_loop(0, max(L - 1, blocks), fill, 0)

    def body(s, carry):
        ag_step(s)

        @pl.when(s < U)
        def _():
            y_step(s)

        @pl.when((s < A4) & (s % 4 == 3))
        def _():
            attn_core(s)

        @pl.when((s >= A4) & (s < U) & ((s - A4) % 2 == 1))
        def _():
            ffn_core(s)

        u = s - LAG

        @pl.when((u >= 0) & (u < U))
        def _():
            dw_sib(u)

        rs_step(s)

        @pl.when((u >= 0) & (u < U))
        def _():
            dw_own(u)
            acc_step(u)

        @pl.when((u >= 1) & (u < U + 1))
        def _():
            ag_finish(u - 1)

        return carry

    lax.fori_loop(0, U + LAG + n, body, 0)

    def tail(i, carry):
        rows = ds(i, ROWS)
        normed = layer_norm(X[rows, :].astype(F32))
        ab = Acc[0, rows, :]
        fb = Acc[1, rows, :]
        small_ref[0:1, :] += jnp.sum(ab * normed, axis=0, keepdims=True)
        small_ref[1:2, :] += jnp.sum(ab, axis=0, keepdims=True)
        small_ref[2:3, :] += jnp.sum(fb * normed, axis=0, keepdims=True)
        small_ref[3:4, :] += jnp.sum(fb, axis=0, keepdims=True)
        A[1, rows, :] = (ab * norm_ref[0:1, :] + fb * norm_ref[2:3, :]).astype(BF16)
        A[0, rows, :] = Acc[2, rows, :].astype(BF16)
        return carry

    lax.fori_loop(0, blocks, tail, 0)
    copies = [
        pltpu.make_async_copy(A.at[i], part_hbm.at[i], in_sem.at[i]) for i in range(2)
    ]
    for cp in copies:
        cp.start()
    for v in range(max(0, U - NS), U):
        rs_finish(v)
    for v in range(max(0, U - 2), U):
        sb_copy(v).wait_send()
        out_copy(v).wait()
    for cp in copies:
        cp.wait()


def run_layer(d, seq_len, x, cot, wl, norms, bias, rope):
    n, T, D, Dsl, U = d.n, d.T, d.D, d.Dsl, d.U
    dma = pltpu.SemaphoreType.DMA
    vm = pl.BlockSpec(memory_space=pltpu.VMEM)
    hbm = pl.BlockSpec(memory_space=pl.ANY)
    flops = 6 * U * T * D * UNIT
    return pl.pallas_call(
        functools.partial(layer_kernel, d),
        out_shape=(
            jax.ShapeDtypeStruct((2, T, D), BF16),
            jax.ShapeDtypeStruct((U, Dsl, UNIT), F32),
            jax.ShapeDtypeStruct((8, D), F32),
            jax.ShapeDtypeStruct((U, 8, UNIT), F32),
        ),
        in_specs=[pl.BlockSpec(memory_space=pltpu.SMEM), hbm, hbm, hbm, vm, vm, vm],
        out_specs=(hbm, hbm, vm, vm),
        scratch_shapes=[
            pltpu.VMEM((d.NW, 2 * n, Dsl, UNIT), BF16),
            pltpu.VMEM((3, T, D), BF16),
            pltpu.VMEM((3, 2, n * Dsl, T), BF16),
            pltpu.VMEM((T, D), BF16),
            pltpu.VMEM((3, T, D), F32),
            pltpu.VMEM((4, T, UNIT), F32),
            pltpu.VMEM((4, T, UNIT), BF16),
            pltpu.VMEM((4, T, UNIT), BF16),
            pltpu.VMEM((T, T), BF16),
            pltpu.VMEM((T, T), BF16),
            pltpu.VMEM((d.NS, n, Dsl, UNIT), BF16),
            pltpu.VMEM((2, n, Dsl, UNIT), BF16),
            pltpu.VMEM((d.NSR, n, Dsl, UNIT), BF16),
            pltpu.VMEM((d.NLR, n + 1, Dsl, UNIT), BF16),
            pltpu.VMEM((2, Dsl, UNIT), F32),
            dma((2,)),
            dma((d.NW,)),
            dma((d.NW, 2 * n)),
            dma((d.NW, n)),
            dma((d.NW, n)),
            dma((d.NW, n)),
            pltpu.SemaphoreType.REGULAR((3,)),
            dma((2,)),
            dma((d.NSR,)),
            dma((d.NS, n)),
            dma((d.NLR, n + 1)),
            dma((2,)),
        ],
        compiler_params=pltpu.CompilerParams(
            collective_id=0, has_side_effects=True, vmem_limit_bytes=67_000_000
        ),
        cost_estimate=pl.CostEstimate(
            flops=flops, bytes_accessed=4 * U * Dsl * UNIT * 8, transcendentals=T * UNIT * U
        ),
    )(seq_len, x, cot, wl, norms, bias, rope)


def rope_pair(rows):
    half = ROT // 2
    freq_idx = jnp.arange(half, dtype=F32)
    inv_freq = jnp.exp(-(2.0 * freq_idx / ROT) * math.log(rope_base))
    angles = jnp.arange(rows, dtype=F32)[:, None] * inv_freq[None, :]
    cosine, sine = jnp.cos(angles), jnp.sin(angles)
    rest = 128 - ROT
    return jnp.stack(
        [
            jnp.concatenate([cosine, cosine, jnp.ones((rows, rest), F32)], axis=1),
            jnp.concatenate([-sine, sine, jnp.zeros((rows, rest), F32)], axis=1),
        ]
    )


def per_device(
    n_dp,
    block_input,
    cotangent,
    lengths,
    attn_gain,
    attn_shift,
    ffn_gain,
    ffn_shift,
    qkv_weight,
    qkv_bias,
    out_weight,
    out_bias,
    up_weight,
    up_bias,
    down_weight,
):
    T, D = block_input.shape
    n = n_dp // 2
    Dsl = D // n_dp
    width = qkv_weight.shape[2]
    heads = width // HD
    hidden = up_weight.shape[1]
    chunks = hidden // UNIT
    U = 4 * heads + 2 * chunks
    L, LAG = n + 1, 3
    d = types.SimpleNamespace(
        n=n, T=T, D=D, Dsl=Dsl, U=U, heads=heads, chunks=chunks, L=L, LAG=LAG,
        NW=min(U, L + LAG + 6), NS=min(U, n + 3), NSR=4, NLR=n + 2,
    )

    nb, ub = qkv_bias.shape[1], up_bias.shape[0]
    packed = jnp.concatenate(
        [attn_gain, attn_shift, ffn_gain, ffn_shift, out_bias, qkv_bias.reshape(-1), up_bias]
    )
    packed = lax.all_gather(packed, "dp", axis=0).astype(F32)
    norm_rows = [packed[:, i * Dsl : (i + 1) * Dsl].reshape(D) for i in range(5)]
    outb_full = norm_rows[4]
    qkv_b = packed[:, 5 * Dsl : 5 * Dsl + 3 * nb].reshape(n_dp, 3, nb)
    qkv_b = qkv_b.transpose(1, 0, 2).reshape(3, heads, HD)
    up_b = packed[:, 5 * Dsl + 3 * nb :].reshape(chunks, UNIT)
    norms = jnp.stack(norm_rows[:4] + [jnp.zeros((D,), F32)] * 4)
    bias = jnp.concatenate(
        [
            jnp.concatenate(
                [qkv_b.transpose(1, 0, 2), jnp.zeros((heads, 1, UNIT), F32)], axis=1
            ).reshape(4 * heads, UNIT),
            jnp.stack([up_b, jnp.zeros_like(up_b)], axis=1).reshape(2 * chunks, UNIT),
        ]
    )
    bias = jnp.broadcast_to(bias[:, None, :], (U, 8, UNIT))

    qkv_u = qkv_weight.reshape(3, Dsl, heads, UNIT).transpose(2, 0, 1, 3)
    out_u = out_weight.reshape(heads, 1, UNIT, Dsl).transpose(0, 1, 3, 2)
    up_u = up_weight.reshape(Dsl, chunks, 1, UNIT).transpose(1, 2, 0, 3)
    down_u = down_weight.reshape(chunks, 1, UNIT, Dsl).transpose(0, 1, 3, 2)
    wl = jnp.concatenate(
        [
            jnp.concatenate([qkv_u, out_u], axis=1).reshape(4 * heads, Dsl, UNIT),
            jnp.concatenate([up_u, down_u], axis=1).reshape(2 * chunks, Dsl, UNIT),
        ]
    )

    part, dw, small, bg = run_layer(
        d, lengths, block_input, cotangent, wl, norms, bias, rope_pair(T)
    )

    part = lax.psum(part, "tensor").astype(F32)
    stats = lax.psum(small[:4], "tensor")
    x_rows = block_input.astype(F32)
    block_output = (x_rows + part[0] + outb_full).astype(BF16)
    mean = jnp.mean(x_rows, axis=-1, keepdims=True)
    centered = x_rows - mean
    inv_std = lax.rsqrt(jnp.mean(centered * centered, axis=-1, keepdims=True) + norm_eps)
    normed = centered * inv_std
    row_valid = (jnp.arange(T, dtype=jnp.int32) < lengths[0]).astype(F32)[:, None]
    grad_rows = cotangent.astype(F32) * row_valid
    norm_grad = part[1]
    grad_mean = jnp.mean(norm_grad, axis=-1, keepdims=True)
    grad_proj = jnp.mean(norm_grad * normed, axis=-1, keepdims=True)
    dblock_input = (grad_rows + inv_std * (norm_grad - grad_mean - normed * grad_proj)).astype(BF16)

    dqkv_b = bg[: 4 * heads, 0].reshape(heads, 4, UNIT)[:, :3].transpose(1, 0, 2)
    dup_b = bg[4 * heads :, 0].reshape(chunks, 2, UNIT)[:, 0].reshape(hidden)
    sent = jnp.concatenate(
        [
            stats.reshape(4, n_dp, Dsl).transpose(1, 0, 2).reshape(n_dp, 4 * Dsl),
            small[4].reshape(n_dp, Dsl),
            dqkv_b.reshape(3, n_dp, nb).transpose(1, 0, 2).reshape(n_dp, 3 * nb),
            dup_b.reshape(n_dp, ub),
        ],
        axis=1,
    )
    sent = lax.psum_scatter(sent, "dp", scatter_dimension=0, tiled=False)
    stats_s = sent[: 4 * Dsl].reshape(4, Dsl)
    doutb = sent[4 * Dsl : 5 * Dsl]
    dqkvb = sent[5 * Dsl : 5 * Dsl + 3 * nb].reshape(3, nb)
    dupb = sent[5 * Dsl + 3 * nb :]

    dwa = dw[: 4 * heads].reshape(heads, 4, Dsl, UNIT)
    dwf = dw[4 * heads :].reshape(chunks, 2, Dsl, UNIT)
    dqkv = dwa[:, :3].transpose(1, 2, 0, 3).reshape(3, Dsl, width)
    dout = dwa[:, 3].transpose(0, 2, 1).reshape(width, Dsl)
    dup = dwf[:, 0].transpose(1, 0, 2).reshape(Dsl, hidden)
    ddown = dwf[:, 1].transpose(0, 2, 1).reshape(hidden, Dsl)
    return (
        block_output,
        dblock_input,
        stats_s[0],
        stats_s[1],
        stats_s[2],
        stats_s[3],
        dqkv,
        dqkvb,
        dout,
        doutb,
        dup,
        dupb,
        ddown,
    )


def solution(mesh):
    in_specs = (
        P("dp", None),
        P("dp", None),
        P("dp"),
        P("dp"),
        P("dp"),
        P("dp"),
        P("dp"),
        P(None, "dp", "tensor"),
        P(None, ("tensor", "dp")),
        P("tensor", "dp"),
        P("dp"),
        P("dp", "tensor"),
        P(("tensor", "dp")),
        P("tensor", "dp"),
    )
    out_specs = (
        P("dp", None),
        P("dp", None),
        P("dp"),
        P("dp"),
        P("dp"),
        P("dp"),
        P(None, "dp", "tensor"),
        P(None, ("tensor", "dp")),
        P("tensor", "dp"),
        P("dp"),
        P("dp", "tensor"),
        P(("tensor", "dp")),
        P("tensor", "dp"),
    )
    return jax.shard_map(
        functools.partial(per_device, mesh.shape["dp"]),
        mesh=mesh,
        in_specs=in_specs,
        out_specs=out_specs,
        check_vma=False,
    )
```

time: 1080 us -> 515 us (0.48)
  waiting for transfers between devices: 768 us -> 34.1 us
  Pallas kernels: 0 us -> 333 us
  matrix products: 103 us -> 0 us
  blocking collectives: 119 us -> 75.4 us
    reduce_scatter x4 -> x0, waiting for transfers between devices: 477 us -> none  [the longest x1 170 us: per_device(): lax.psum_scatter(dup_w, 'dp', scatter_dimension=0, tiled=True)]
    pallas_call x0 -> x1, Pallas kernels: none -> 333 us  [run_layer(): pl.pallas_call(functools.partial(layer_kernel, d), out_shape=(jax.ShapeDt...]
    psum x1, waiting for transfers between devices: 168 us -> 34.1 us  [per_device(): part = lax.psum(part, 'tensor').astype(F32)]
    all_gather x4 -> x0, waiting for transfers between devices: 121 us -> none  [the longest x1 72.7 us: per_device(): lax.all_gather(down_weight, 'dp', axis=1, tiled=True)]
    dot_general x18 -> x0, matrix products: 103 us -> none  [the longest x1 13.3 us: per_device(): jnp.einsum('lf,ld->fd', hidden, grad_bf, preferred_element_type=jnp.float32)]
    all_gather x7 -> x0, blocking collectives: 81.8 us -> none  [the longest x1 17.9 us: per_device(): lax.all_gather(qkv_bias, 'dp', axis=1, tiled=True)]
    unnamed x1 -> x2, blocking collectives: 27.4 us -> 57.6 us
    unnamed x109 -> x25, local copies, waits for them, and re-layouts: 24.2 us -> 2.92 us
  transfers between devices with their start and end apart: 11 -> 1, of which waited for: 8 -> 1; matrix products, arithmetic and copies ran while one was open for 12% -> 5% of each run, Pallas kernels for 0% -> 0%
where the time goes in v2:
time: 515 us; the launch traced here: 514 us
  Pallas kernels  333 us (65%)
  blocking collectives  75.4 us (15%)
  local copies, waits for them, and re-layouts  40.7 us (8%)
  waiting for transfers between devices  34.1 us (7%)
  other arithmetic  15.9 us (3%)
  between operations  15.7 us (3%)
    pallas_call x1, Pallas kernels, run_layer(): pl.pallas_call(functools.partial(layer_kernel, d), out_shape=(jax.ShapeDt...  333 us
    unnamed x2, blocking collectives  57.6 us
    psum x1, waiting for transfers between devices, per_device(): part = lax.psum(part, 'tensor').astype(F32)  34.1 us
    psum x1, blocking collectives, per_device(): stats = lax.psum(small[:4], 'tensor')  17.8 us
  transfers between devices with their start and end apart: 1, of which 1 were waited for; matrix products, arithmetic and copies ran while one was open for 5% of the time, Pallas kernels for 0%

profile of v2, /device:TPU:0, one launch (start us, length us, event | category | flops | bytes accessed | tf_op | source)
XLA Modules:
  0.0 514.4 jit_solution(7731363727302322599)
XLA Ops:
  7.3 0.8 reshape.147
  8.1 1.3 fusion.17
  10.1 4.1 concatenate.30
  14.4 30.3 %all-reduce.2 = bf16[13824]{0:T(1024)(128)(2,1)S(1)} all-reduce(bf16[13824]{0:T(1024)(128)(2,1)S(1)} %dynamic-update-slice), channel_id=2, replica_groups=mesh['dp'=8,'tensor'=4] {'dp'}, use_global_device_ids=true, to_apply=%add.2 | all-reduce | flops 13824 | bytes 55296
  46.0 1.8 copy.60
  47.8 1.7 fusion.13
  49.5 1.2 copy.93
  51.2 1.5 copy.62
  52.7 1.2 maximum_bitcast_fusion
  53.8 0.8 pad_maximum_fusion.3.rope_ref
  54.7 1.0 pad_maximum_fusion.2
  55.9 2.0 pad_maximum_fusion.wl
  58.0 0.7 stack.22.norm_ref
  59.3 332.7 %shard_map.237 = (bf16[2,512,2048]{2,1,0:T(8,128)(2,1)}, f32[24,256,256]{2,1,0:T(8,128)}, f32[8,2048]{1,0:T(8,128)}, f32[24,8,256]{2,1,0:T(8,128)}) custom-call(s32[1]{0:T(128)} %copy.99.len_ref, bf16[512,2048]{1,0:T(8,128)(2,1)} %x_hbm.1, bf16[512,2048]{1,0:T(8,128)(2,1)} %cot_hbm.1, bf16[24,256,256]{2,1,0:T(8,128)(2,1)} %pad_maximum_fusion.wl, ...), custom_call_target="tpu_custom_call" | custom-call | flops 38654705664 | bytes 50331648 | tf_op jit(solution)/shard_map/pallas_call | solution.py:536
  392.0 1.8 slice.120
  393.9 5.3 %slice.126 = f32[16,256,256]{2,1,0:T(8,128)} slice(f32[24,256,256]{2,1,0:T(8,128)} %get-tuple-element.20), slice={[8:24], [0:256], [0:256]} | slice | bytes 8388608 | tf_op jit(solution)/shard_map/slice | solution.py:699
  399.3 1.0 slice_reduce_fusion.1
  400.4 0.9 slice_reduce_fusion.2
  401.4 17.8 %psum.15 = f32[8,1024]{1,0:T(8,128)S(1)} all-reduce(f32[8,1024]{1,0:T(8,128)S(1)} %bitcast.119), channel_id=1, replica_groups=mesh['dp'=8,'tensor'=4] {'tensor'}, use_global_device_ids=true, to_apply=%region_5.0 | all-reduce | flops 8192 | bytes 65536 | tf_op jit(solution)/shard_map/psum | solution.py:667
  419.3 27.3 %all-reduce.3 = f32[8,1728]{1,0:T(8,128)S(1)} all-reduce(f32[8,1728]{1,0:T(8,128)S(1)} %concatenate.35), channel_id=3, replica_groups=mesh['dp'=8,'tensor'=4] {'dp'}, use_global_device_ids=true, to_apply=%region_6.0.clone | all-reduce | flops 13824 | bytes 110592
  446.6 0.7 dynamic-slice_reduce_fusion
  448.0 4.6 slice_bitcast_fusion.1
  452.6 3.1 copy.71
  455.9 1.4 copy.78
  457.3 1.1 slice_bitcast_fusion.4
  458.4 1.0 copy.69
  459.4 3.2 copy.79
  462.6 1.3 fusion.16
  464.9 34.1 %all-reduce.6.cloned.1.call-done = bf16[2,512,2048]{2,1,0:T(8,128)(2,1)} async-done(((bf16[2,512,2048]{2,1,0:T(8,128)(2,1)}), bf16[2,512,2048]{2,1,0:T(8,128)(2,1)}) %all-reduce.6.cloned.1.call-update) | async-done | bytes 4194320 | tf_op jit(solution)/shard_map/psum | solution.py:666
  499.0 3.3 convert_element_type.27
  502.5 0.9 fusion.4
  504.1 3.5 fusion.8
  (65 shorter events, 5.5 us)
Async XLA Ops:
  7.2 43.5 %copy-start.3 = (bf16[256,2048]{1,0:T(8,128)(2,1)S(1)}, bf16[256,2048]{1,0:T(8,128)(2,1)}, u32[]{:S(2)}) copy-start(bf16[256,2048]{1,0:T(8,128)(2,1)} %param.25) | copy-start | bytes 3145732
  7.2 491.8 %all-reduce.6.cloned.1.call-start = ((), (), s32[]{:S(2)}) async-start(), calls=%async_computation | async-start | bytes 8388608 | tf_op jit(solution)/shard_map/psum | solution.py:666
  393.8 61.9 %copy-start.1 = (f32[8,256,256]{2,1,0:T(8,128)}, f32[8,256,256]{2,1,0:T(8,128)S(1)}, u32[]{:S(2)}) copy-start(f32[8,256,256]{2,1,0:T(8,128)S(1)} %slice.120) | copy-start | bytes 6291460
  393.9 5.4 %copy-start.4 = (f32[8,2048]{1,0:T(8,128)S(1)}, f32[8,2048]{1,0:T(8,128)}, u32[]{:S(2)}) copy-start(f32[8,2048]{1,0:T(8,128)} %get-tuple-element.18) | copy-start | bytes 196612
  455.9 8.0 %copy-start = (bf16[512,2048]{1,0:T(8,128)(2,1)S(1)}, bf16[512,2048]{1,0:T(8,128)(2,1)}, u32[]{:S(2)}) copy-start(bf16[512,2048]{1,0:T(8,128)(2,1)} %x_hbm.1) | copy-start | bytes 6291460
  502.5 1.6 copy-start.2
Sparse Core Ops, SparseCore 0:
  392.1 106.7 all-reduce.5

commit v3 on v2

v3 whole, which is shorter than its diff:
```python
import functools
import math
import types

import jax
import jax.numpy as jnp
from jax import lax
from jax.experimental import pallas as pl
from jax.experimental.pallas import tpu as pltpu
from jax.sharding import PartitionSpec as P

HD = 256
ROT = 64
UNIT = 256
ROWS = 128
MESH = pl.DeviceIdType.MESH

norm_eps = 1e-05
rope_base = 10000.0

F32 = jnp.float32
BF16 = jnp.bfloat16


def dot(a, b):
    return lax.dot_general(a, b, (((1,), (0,)), ((), ())), preferred_element_type=F32)


def dot_nt(a, b):
    return lax.dot_general(a, b, (((1,), (1,)), ((), ())), preferred_element_type=F32)


def dot_tn(a, b):
    return lax.dot_general(a, b, (((0,), (0,)), ((), ())), preferred_element_type=F32)


def ds(i, size):
    return pl.ds(pl.multiple_of(i * size, size), size)


def layer_kernel(
    d,
    len_ref,
    sp_ref,
    rope_ref,
    x_hbm,
    cot_hbm,
    wqkv,
    wout,
    wup,
    wdown,
    o_hbm,
    dx_hbm,
    dqkv_hbm,
    dout_hbm,
    dup_hbm,
    ddown_hbm,
    pr_hbm,
    so_ref,
    sb_ref,
    W,
    A,
    At,
    Acc,
    Y,
    G,
    QK,
    PB,
    DS,
    S,
    DL,
    DR,
    SB,
    SR,
    LR,
    stage,
    stage_t,
    OT,
    RP,
    NB,
    BI,
    SM,
    BG,
    BGC,
    RS1,
    RB2,
    ST,
    RT,
    in_sem,
    own_sem,
    ag_recv,
    agR,
    agL,
    agS,
    credit,
    lcredit,
    ready,
    sb_sem,
    sr_sem,
    ls_sem,
    lr_sem,
    out_sem,
    sp_s,
    sp_r,
    sm_s,
    sm_r,
    st_s,
    st_r,
    pr_s,
    pr_r,
    fo_s,
    fo_r,
    loc_sem,
    raw_sem,
):
    n, tn, T, D, Dsl, U, heads = d.n, d.tn, d.T, d.D, d.Dsl, d.U, d.heads
    n_dp, NW, NS, NSR, NLR, LAG = 2 * d.n, d.NW, d.NS, d.NSR, d.NLR, d.LAG
    E, ES, E0 = d.E, d.ES, d.E0
    Tr = T // tn
    A4 = 4 * heads
    chunks = d.chunks
    me = lax.axis_index("dp")
    mt = lax.axis_index("tensor")
    z = me // 2
    c = me % 2
    right, left, sib = me + 2, me - 2, z * 2 + (1 - c)
    has_r = z < n - 1
    has_l = z > 0
    seq_len = len_ref[0]

    def rcopy_to(src, dst, ss, rs, where):
        return pltpu.make_async_remote_copy(
            src_ref=src,
            dst_ref=dst,
            send_sem=ss,
            recv_sem=rs,
            device_id=where,
            device_id_type=MESH,
        )

    def rcopy(src, dst, ss, rs, dev):
        return rcopy_to(src, dst, ss, rs, {"dp": dev})

    def signal(sem, dev, axis="dp"):
        pl.semaphore_signal(sem, inc=1, device_id={axis: dev}, device_id_type=MESH)

    def aidx(u):
        attn = jnp.where(u % 4 == 3, 2, 0)
        ffn = jnp.where((u - A4) % 2 == 0, 1, 2)
        return jnp.where(u < A4, attn, ffn)

    def each_dp(f):
        for p in range(n_dp):

            @pl.when(p != me)
            def _(p=p):
                f(p)

    def each_tensor(f):
        for p in range(tn):

            @pl.when(p != mt)
            def _(p=p):
                f(p)

    def own_tile(u, f):
        @pl.when((u < A4) & (u % 4 != 3))
        def _():
            f(wqkv.at[u % 4, :, ds(u // 4, UNIT)])

        @pl.when((u < A4) & (u % 4 == 3))
        def _():
            f(OT.at[u // 4])

        @pl.when((u >= A4) & (u % 2 == 0))
        def _():
            f(wup.at[:, ds((u - A4) // 2, UNIT)])

        @pl.when((u >= A4) & (u % 2 == 1))
        def _():
            f(OT.at[heads + (u - A4) // 2])

    def ag_tile(slot, sj, sem, dev):
        return rcopy(W.at[slot, sj], W.at[slot, sj], sem, ag_recv.at[slot, sj], dev)

    def ag_self(u):
        slot = u % NW

        @pl.when(u >= NW)
        def _():
            pl.semaphore_wait(credit.at[2], 1)

        def go(src):
            pltpu.make_async_copy(src, W.at[slot, me], own_sem.at[slot]).start()
            rcopy(src, W.at[slot, me], agS.at[slot, z], ag_recv.at[slot, me], sib).start()

        own_tile(u, go)

    def relay(u, j, has_next, sems, dev):
        slot = u % NW
        sj = j * 2 + c
        ag_tile(slot, sj, agS.at[slot, j], sib).wait_recv()

        @pl.when(has_next)
        def _():
            ag_tile(slot, sj, sems.at[slot, j], dev).start()

        ag_tile(slot, sj, agS.at[slot, j], sib).start()

    def ag_line(u, has_next, credit_sem, sems, dev, sign):
        slot = u % NW

        @pl.when(has_next)
        def _():
            @pl.when(u >= NW)
            def _():
                pl.semaphore_wait(credit_sem, 1)

            def go(src):
                rcopy(src, W.at[slot, me], sems.at[slot, z], ag_recv.at[slot, me], dev).start()

            own_tile(u, go)

        for k in range(1, n):
            j = z + sign * k

            @pl.when((j >= 0) & (j < n))
            def _(j=j):
                relay(u, j, has_next, sems, dev)

    def guarded(v, f):
        @pl.when((v >= 0) & (v < U))
        def _():
            f(v)

    def ag_step(s):
        guarded(s + ES, ag_self)
        guarded(
            s + E + d.gap * (n - 1 - z),
            lambda u: ag_line(u, has_r, credit.at[0], agR, right, -1),
        )
        guarded(s + E + d.gap * z, lambda u: ag_line(u, has_l, credit.at[1], agL, left, 1))

    def ag_wait(u):
        slot = u % NW
        pltpu.make_async_copy(OT.at[0], W.at[slot, me], own_sem.at[slot]).wait()
        for j in range(n):
            ag_tile(slot, j * 2 + 1 - c, agS.at[slot, j], sib).wait_recv()

    def ag_finish(u):
        slot = u % NW
        for j in range(n):

            @pl.when(has_r & (j <= z))
            def _(j=j):
                ag_tile(slot, j * 2 + c, agR.at[slot, j], right).wait_send()

            @pl.when(has_l & (j >= z))
            def _(j=j):
                ag_tile(slot, j * 2 + c, agL.at[slot, j], left).wait_send()

            ag_tile(slot, j * 2 + c, agS.at[slot, j], sib).wait_send()

        @pl.when(u + NW < U)
        def _():
            @pl.when(has_r)
            def _():
                signal(credit.at[1], right)

            @pl.when(has_l)
            def _():
                signal(credit.at[0], left)

            signal(credit.at[2], sib)

    def part_ref(v, zt):
        if zt == 0:
            return DL.at[v]
        if zt == n - 1:
            return DR.at[v]
        return S.at[v % NS, zt - 1]

    def sb_copy(u):
        return rcopy(SB.at[u % 2], SR.at[u % NSR], sb_sem.at[u % 2], sr_sem.at[u % NSR], sib)

    def ls_copy(v, zt, to_right):
        slot = zt if to_right else zt - 1
        return rcopy(
            S.at[v % NS, zt - 1],
            LR.at[v % NLR, slot],
            ls_sem.at[v % NS, zt - 1],
            lr_sem.at[v % NLR, slot],
            right if to_right else left,
        )

    def dw_half(u, core, put):
        a = aidx(u)
        g = G[u % 4]
        for j in range(n):
            put(j, dot(At[a, core, j * Dsl : (j + 1) * Dsl, :], g).astype(BF16))

    def dw_sib(u):
        @pl.when(u >= 2)
        def _():
            sb_copy(u - 2).wait_send()

        def put(j, v):
            SB[u % 2, j] = v

        dw_half(u, 1 - c, put)
        sb_copy(u).start()

    def rs_finish(v):
        for zt in range(1, n - 1):

            @pl.when(zt != z)
            def _(zt=zt):
                ls_copy(v, zt, True).wait_send()

    def dw_own(u):
        @pl.when(u >= NS)
        def _():
            rs_finish(u - NS)

        def put(j, v):
            part_ref(u, j)[...] = v

        dw_half(u, c, put)

    def add_into(ref, other):
        ref[...] = (ref[...].astype(F32) + other[...].astype(F32)).astype(BF16)

    def combine(v):
        sb_copy(v).wait_recv()
        for zt in range(n):
            add_into(part_ref(v, zt), SR.at[v % NSR, zt])

    def send_right(v):
        @pl.when((z + 1 <= n - 2) & (v >= NLR))
        def _():
            pl.semaphore_wait(lcredit.at[0], 1)

        for zt in range(1, n - 1):

            @pl.when(zt > z)
            def _(zt=zt):
                @pl.when(has_l)
                def _():
                    ls_copy(v, zt, True).wait_recv()
                    add_into(S.at[v % NS, zt - 1], LR.at[v % NLR, zt])

                ls_copy(v, zt, True).start()

    def send_left(v):
        @pl.when((z - 1 >= 1) & (v >= NLR))
        def _():
            pl.semaphore_wait(lcredit.at[1], 1)

        for zt in range(1, n - 1):

            @pl.when(zt < z)
            def _(zt=zt):
                @pl.when(has_r)
                def _():
                    ls_copy(v, zt, False).wait_recv()
                    add_into(S.at[v % NS, zt - 1], LR.at[v % NLR, zt - 1])

                ls_copy(v, zt, False).start()

    def out_wait(v):
        pltpu.make_async_copy(
            stage.at[v % 2], dup_hbm.at[:, 0:UNIT], out_sem.at[v % 2]
        ).wait()

    def out_start(v):
        slot = v % 2
        sem = out_sem.at[slot]

        @pl.when((v < A4) & (v % 4 != 3))
        def _():
            pltpu.make_async_copy(
                stage.at[slot], dqkv_hbm.at[v % 4, :, ds(v // 4, UNIT)], sem
            ).start()

        @pl.when((v >= A4) & (v % 2 == 0))
        def _():
            pltpu.make_async_copy(
                stage.at[slot], dup_hbm.at[:, ds((v - A4) // 2, UNIT)], sem
            ).start()

        @pl.when(((v < A4) & (v % 4 == 3)) | ((v >= A4) & (v % 2 == 1)))
        def _():
            stage_t[slot] = jnp.transpose(stage[slot])

            @pl.when(v < A4)
            def _():
                pltpu.make_async_copy(
                    stage_t.at[slot], dout_hbm.at[ds(v // 4, UNIT), :], sem
                ).start()

            @pl.when(v >= A4)
            def _():
                pltpu.make_async_copy(
                    stage_t.at[slot], ddown_hbm.at[ds((v - A4) // 2, UNIT), :], sem
                ).start()

    def final(v):
        @pl.when((z >= 1) & (z <= n - 2))
        def _():
            @pl.when(v >= 2)
            def _():
                out_wait(v - 2)

            slot = v % 2
            ls_copy(v, z, True).wait_recv()
            ls_copy(v, z, False).wait_recv()
            stage[slot] = (
                S[v % NS, z - 1].astype(F32)
                + LR[v % NLR, z].astype(F32)
                + LR[v % NLR, z - 1].astype(F32)
            )
            out_start(v)

            @pl.when(v + NLR < U)
            def _():
                signal(lcredit.at[0], left)
                signal(lcredit.at[1], right)

    def rs_step(s):
        base = s - LAG - 1
        guarded(base, combine)
        guarded(base - z, send_right)
        guarded(base - (n - 1 - z), send_left)
        guarded(base - jnp.maximum(z, n - 1 - z), final)

    def p2_slot(i):
        return W.at[i // n_dp, i % n_dp], ag_recv.at[i // n_dp, i % n_dp]

    def p2_copy(u, to_right):
        dst, rs = p2_slot(u if to_right else U + u)
        src = DR.at[u] if to_right else DL.at[u]
        sems = agR if to_right else agL
        return rcopy(src, dst, sems.at[u // n, u % n], rs, right if to_right else left)

    def p2_side(u, to_right):
        has_prev, has_next = (has_l, has_r) if to_right else (has_r, has_l)
        mine = DR.at[u] if to_right else DL.at[u]
        got, _ = p2_slot(u if to_right else U + u)
        cp = p2_copy(u, to_right)

        @pl.when(has_prev)
        def _():
            cp.wait_recv()

        @pl.when(has_next)
        def _():
            @pl.when(has_prev)
            def _():
                add_into(mine, got)

            cp.start()

        @pl.when(jnp.logical_not(has_next))
        def _():
            @pl.when(u >= 2)
            def _():
                out_wait(u - 2)

            stage[u % 2] = mine[...].astype(F32) + got[...].astype(F32)
            out_start(u)

    def p2_step(i):
        guarded(i - z, lambda u: p2_side(u, True))
        guarded(i - (n - 1 - z), lambda u: p2_side(u, False))

    def layer_norm(x):
        mean = jnp.mean(x, axis=-1, keepdims=True)
        cen = x - mean
        inv = lax.rsqrt(jnp.mean(cen * cen, axis=-1, keepdims=True) + norm_eps)
        return cen * inv, inv

    def ln_block(i):
        rows = ds(i, ROWS)
        normed, _ = layer_norm(A[0, rows, :].astype(F32))
        A[0, rows, :] = (normed * NB[0:1, :] + NB[1:2, :]).astype(BF16)
        A[1, rows, :] = (normed * NB[2:3, :] + NB[3:4, :]).astype(BF16)
        pos = lax.broadcasted_iota(jnp.int32, (ROWS, D), 0) + i * ROWS
        grad = jnp.where(pos < seq_len, A[2, rows, :].astype(F32), 0.0)
        A[2, rows, :] = grad.astype(BF16)
        SM[4:5, :] += jnp.sum(grad, axis=0, keepdims=True)
        for a in range(3):
            for j in range(2 * n):
                At[a, j % 2, (j // 2) * Dsl : (j // 2 + 1) * Dsl, rows] = jnp.transpose(
                    A[a, rows, j * Dsl : (j + 1) * Dsl]
                )
            Acc[a, rows, :] = jnp.zeros((ROWS, D), F32)

    def y_step(u):
        ag_wait(u)
        w = W[u % NW].reshape(D, UNIT)
        Y[u % 4] = dot(A[aidx(u)], w)

    def acc_step(u):
        a = aidx(u)
        g = G[u % 4]
        for j in range(2 * n):
            cols = slice(j * Dsl, (j + 1) * Dsl)
            Acc[a, :, cols] += dot_nt(g, W[u % NW, j])

    lane = lax.broadcasted_iota(jnp.int32, (T, 128), 1)

    def rotate(y, sign):
        lo = y[:, :128]
        swapped = jnp.where(lane < 32, pltpu.roll(lo, 96, 1), pltpu.roll(lo, 32, 1))
        lo = lo * rope_ref[0] + swapped * (rope_ref[1] * sign)
        return jnp.concatenate([lo, y[:, 128:]], axis=1)

    def attn_core(s):
        u0 = s - 3
        QK[0] = rotate(Y[0] + BI[u0, 0:1, :], 1.0).astype(BF16)
        QK[1] = rotate(Y[1] + BI[u0 + 1, 0:1, :], 1.0).astype(BF16)
        QK[2] = (Y[2] + BI[u0 + 2, 0:1, :]).astype(BF16)
        QK[3] = Y[3].astype(BF16)
        scale = 1.0 / math.sqrt(HD)

        def block(i, carry):
            rows = ds(i, ROWS)
            raw = dot_nt(QK[0, rows, :], QK[1]) * scale
            qpos = lax.broadcasted_iota(jnp.int32, (ROWS, T), 0) + i * ROWS
            kpos = lax.broadcasted_iota(jnp.int32, (ROWS, T), 1)
            scores = jnp.where((kpos <= qpos) & (kpos < seq_len), raw, -jnp.inf)
            top = jnp.max(scores, axis=-1, keepdims=True)
            e = jnp.exp(scores - top)
            p = e / jnp.sum(e, axis=-1, keepdims=True)
            pb = p.astype(BF16)
            PB[rows, :] = pb
            mixed = dot(pb, QK[2]).astype(BF16)
            G[3, rows, :] = mixed
            mg = QK[3, rows, :]
            delta = jnp.sum(mg.astype(F32) * mixed.astype(F32), axis=-1, keepdims=True)
            dp = dot_nt(mg, QK[2])
            dsb = (p * (dp - delta) * scale).astype(BF16)
            DS[rows, :] = dsb
            Y[0, rows, :] = dot(dsb, QK[1])
            return carry

        lax.fori_loop(0, T // ROWS, block, 0)
        Y[1] = dot_tn(DS[...], QK[0])
        for r in range(3):
            if r == 2:
                g = dot_tn(PB[...], QK[3])
            else:
                g = rotate(Y[r], -1.0)
            BG[u0 + r] = jnp.broadcast_to(jnp.sum(g, axis=0, keepdims=True), (8, UNIT))
            G[r] = g.astype(BF16)

    def ffn_core(s):
        b = BI[s - 1, 0:1, :]
        yu, yd = (s - 1) % 4, s % 4
        step = 64

        def block(i, total):
            rows = ds(i, step)
            v = Y[yu, rows, :] + b
            cdf2 = 1.0 + lax.erf(v * (1.0 / math.sqrt(2.0)))
            G[yd, rows, :] = (0.5 * v * cdf2).astype(BF16)
            slope = 0.5 * cdf2 + v * jnp.exp(-0.5 * v * v) * (1.0 / math.sqrt(2.0 * math.pi))
            g = Y[yd, rows, :] * slope
            G[yu, rows, :] = g.astype(BF16)
            return total + jnp.sum(g, axis=0, keepdims=True)

        total = lax.fori_loop(0, T // step, block, jnp.zeros((1, UNIT), F32))
        BG[s - 1] = jnp.broadcast_to(total, (8, UNIT))

    barrier = pltpu.get_barrier_semaphore()
    each_dp(lambda p: signal(barrier, p))
    each_tensor(lambda p: signal(barrier, p, "tensor"))
    x_in = pltpu.make_async_copy(x_hbm, A.at[0], in_sem.at[0])
    c_in = pltpu.make_async_copy(cot_hbm, A.at[2], in_sem.at[1])
    x_in.start()
    c_in.start()
    spots = [
        buf.at[i, r * UNIT : (r + 1) * UNIT, 0:Dsl]
        for buf in (QK, G)
        for i in range(4)
        for r in range(T // UNIT)
    ]
    raws = [
        pltpu.make_async_copy(
            wout.at[i * UNIT : (i + 1) * UNIT, :]
            if i < heads
            else wdown.at[(i - heads) * UNIT : (i - heads + 1) * UNIT, :],
            spots[i],
            raw_sem.at[i],
        )
        for i in range(heads + chunks)
    ]
    for cp in raws:
        cp.start()
    pl.semaphore_wait(barrier, n_dp - 1 + tn - 1)

    def sp_copy(p, where):
        return rcopy(sp_ref, RP.at[where], sp_s.at[p], sp_r.at[where], p)

    each_dp(lambda p: sp_copy(p, me).start())
    RP[me] = sp_ref[...]

    def early(s, carry):
        ag_step(s)
        return carry

    lax.fori_loop(-E0, 3 - E0, early, 0)
    for i, cp in enumerate(raws):
        cp.wait()
        OT[i] = jnp.transpose(spots[i][...])
    SM[...] = jnp.zeros_like(SM)
    BG[...] = jnp.zeros_like(BG)
    BI[...] = jnp.zeros_like(BI)
    each_dp(lambda p: sp_copy(p, p).wait_recv())
    for p in range(n_dp):
        NB[:, p * Dsl : (p + 1) * Dsl] = RP[p, 0:8, 0:Dsl]
    for i in range(3 * heads + chunks):
        row = RP[0, 8 + i : 9 + i, :]
        for p in range(1, n_dp):
            row = row + RP[p, 8 + i : 9 + i, :]
        u = 4 * (i // 3) + i % 3 if i < 3 * heads else A4 + 2 * (i - 3 * heads)
        BI[u] = jnp.broadcast_to(row, (8, UNIT))
    x_in.wait()
    c_in.wait()
    blocks = T // ROWS

    def fill(i, carry):
        @pl.when(i < blocks)
        def _():
            ln_block(i)

        @pl.when(i < E0 - 3)
        def _():
            ag_step(i + 3 - E0)

        return carry

    lax.fori_loop(0, max(E0 - 3, blocks), fill, 0)

    def body(s, carry):
        ag_step(s)
        guarded(s, y_step)

        @pl.when(s == A4)
        def _():
            x_in.start()

        @pl.when((s < A4) & (s % 4 == 3))
        def _():
            attn_core(s)

        @pl.when((s >= A4) & (s < U) & (s % 2 == 1))
        def _():
            ffn_core(s)

        u = s - LAG
        guarded(u, dw_sib)
        rs_step(s)

        def rest(u):
            dw_own(u)
            acc_step(u)

        guarded(u, rest)
        guarded(u - 1, ag_finish)
        return carry

    lax.fori_loop(0, U + LAG, body, 0)
    ag_finish(U - 1)
    x_in.wait()

    @pl.when(has_r)
    def _():
        signal(ready.at[1], right)

    @pl.when(has_l)
    def _():
        signal(ready.at[0], left)

    def pr_copy(k, i, where):
        return rcopy_to(
            A.at[k, ds(i, Tr), :],
            pr_hbm.at[k, ds(where, Tr), :],
            pr_s.at[k, i],
            pr_r.at[k, where],
            {"tensor": i},
        )

    def part_send(i):
        @pl.when((i >= 0) & (i != mt))
        def _():
            pr_copy(0, i, mt).start()
            pr_copy(1, i, mt).start()

    def partial(i, carry):
        rows = ds(i, Tr)
        normed, _ = layer_norm(A[0, rows, :].astype(F32))
        ab = Acc[0, rows, :]
        fb = Acc[1, rows, :]
        SM[0:1, :] += jnp.sum(ab * normed, axis=0, keepdims=True)
        SM[1:2, :] += jnp.sum(ab, axis=0, keepdims=True)
        SM[2:3, :] += jnp.sum(fb * normed, axis=0, keepdims=True)
        SM[3:4, :] += jnp.sum(fb, axis=0, keepdims=True)
        ng = ab * NB[0:1, :] + fb * NB[2:3, :]
        Acc[0, rows, :] = ng
        @pl.when(i != mt)
        def _():
            A[1, rows, :] = ng.astype(BF16)
            A[0, rows, :] = Acc[2, rows, :].astype(BF16)

        part_send(i - 1)
        return carry

    lax.fori_loop(0, tn, partial, 0)
    for u in range(U):
        BGC[u : u + 1, :] = BG[u, 0:1, :]
    part_send(tn - 1)

    def sm_copy(p, where):
        return rcopy(
            SM.at[:, ds(p, Dsl)], RS1.at[where], sm_s.at[0, p], sm_r.at[0, where], p
        )

    def bg_copy(p, where):
        return rcopy(BGC, RB2.at[where], sm_s.at[1, p], sm_r.at[1, where], p)

    def small_send(p):
        sm_copy(p, me).start()
        bg_copy(p, me).start()

    each_dp(small_send)
    RS1[me] = SM[:, ds(me, Dsl)]
    RB2[me] = BGC[...]

    @pl.when(has_r)
    def _():
        pl.semaphore_wait(ready.at[0], 1)

    @pl.when(has_l)
    def _():
        pl.semaphore_wait(ready.at[1], 1)

    def drain(i, carry):
        @pl.when(i < n)
        def _():
            rs_step(i + U + LAG)

        p2_step(i)
        return carry

    steps = U + n - 1
    middle = min(d.I1, steps)
    lax.fori_loop(0, middle, drain, 0)

    def small_wait(p):
        sm_copy(p, p).wait_recv()
        bg_copy(p, p).wait_recv()

    each_dp(small_wait)
    total = RS1[0]
    bias_total = RB2[0]
    for p in range(1, n_dp):
        total = total + RS1[p]
        bias_total = bias_total + RB2[p]
    sb_ref[...] = bias_total
    ST[...] = total

    def pr_load(k, p):
        rows = ds(p, Tr)
        return pltpu.make_async_copy(
            pr_hbm.at[k, rows, :], A.at[k, rows, :], loc_sem.at[k, p]
        )

    def part_take(p):
        for k in range(2):
            pr_copy(k, p, mt).wait_send()
            pr_copy(k, p, p).wait_recv()
            pr_load(k, p).start()

    each_tensor(part_take)
    own = ds(mt, Tr)

    def part_add(p):
        for k in range(2):
            pr_load(k, p).wait()
            Acc[2 - 2 * k, own, :] += A[k, ds(p, Tr), :].astype(F32)

    each_tensor(part_add)

    def st_copy(p, where):
        return rcopy_to(ST, RT.at[where], st_s.at[p], st_r.at[where], {"tensor": p})

    each_tensor(lambda p: st_copy(p, mt).start())
    xr = A[0, own, :].astype(F32)
    normed, inv = layer_norm(xr)
    ng = Acc[0, own, :]
    gm = jnp.mean(ng, axis=-1, keepdims=True)
    gp = jnp.mean(ng * normed, axis=-1, keepdims=True)
    A[0, own, :] = (xr + Acc[2, own, :] + NB[4:5, :]).astype(BF16)
    A[1, own, :] = (A[2, own, :].astype(F32) + inv * (ng - gm - normed * gp)).astype(BF16)
    outs = (o_hbm, dx_hbm)

    def fo_copy(k, p, where):
        return rcopy_to(
            A.at[k, own, :],
            outs[k].at[ds(where, Tr), :],
            fo_s.at[k, p],
            fo_r.at[k, where],
            {"tensor": p},
        )

    def fo_send(p):
        fo_copy(0, p, mt).start()
        fo_copy(1, p, mt).start()

    each_tensor(fo_send)
    home = [
        pltpu.make_async_copy(A.at[k, own, :], outs[k].at[own, :], in_sem.at[k])
        for k in range(2)
    ]
    for cp in home:
        cp.start()
    lax.fori_loop(middle, steps, drain, 0)

    each_tensor(lambda p: st_copy(p, p).wait_recv())
    RT[mt] = ST[...]
    whole = RT[0]
    for p in range(1, tn):
        whole = whole + RT[p]
    row = lax.broadcasted_iota(jnp.int32, (8, Dsl), 0)
    so_ref[...] = jnp.where(row < 4, whole, ST[...])

    def ends(p):
        for k in range(2):
            fo_copy(k, p, mt).wait_send()
            fo_copy(k, p, p).wait_recv()
        st_copy(p, mt).wait_send()

    each_tensor(ends)

    def dp_ends(p):
        sp_copy(p, me).wait_send()
        sm_copy(p, me).wait_send()
        bg_copy(p, me).wait_send()

    each_dp(dp_ends)
    for cp in home:
        cp.wait()

    def p2_ends(u, carry):
        @pl.when(has_r)
        def _():
            p2_copy(u, True).wait_send()

        @pl.when(has_l)
        def _():
            p2_copy(u, False).wait_send()

        return carry

    lax.fori_loop(0, U, p2_ends, 0)
    for v in range(max(0, U - NS), U):
        rs_finish(v)
    for v in range(max(0, U - 2), U):
        sb_copy(v).wait_send()
        out_wait(v)


def run_layer(d, seq_len, sp, rope, x, cot, wqkv, wout, wup, wdown):
    n, tn, T, D, Dsl, U = d.n, d.tn, d.T, d.D, d.Dsl, d.U
    n_dp = 2 * n
    width, hidden = d.heads * UNIT, d.chunks * UNIT
    rp, up = sp.shape[0], (U + 7) // 8 * 8
    dma = pltpu.SemaphoreType.DMA
    reg = pltpu.SemaphoreType.REGULAR
    vm = pl.BlockSpec(memory_space=pltpu.VMEM)
    hbm = pl.BlockSpec(memory_space=pl.ANY)
    tile = (Dsl, UNIT)
    return pl.pallas_call(
        functools.partial(layer_kernel, d),
        out_shape=(
            jax.ShapeDtypeStruct((T, D), BF16),
            jax.ShapeDtypeStruct((T, D), BF16),
            jax.ShapeDtypeStruct((3, Dsl, width), F32),
            jax.ShapeDtypeStruct((width, Dsl), F32),
            jax.ShapeDtypeStruct((Dsl, hidden), F32),
            jax.ShapeDtypeStruct((hidden, Dsl), F32),
            jax.ShapeDtypeStruct((2, T, D), BF16),
            jax.ShapeDtypeStruct((8, Dsl), F32),
            jax.ShapeDtypeStruct((up, UNIT), F32),
        ),
        in_specs=[pl.BlockSpec(memory_space=pltpu.SMEM), vm, vm] + [hbm] * 6,
        out_specs=(hbm,) * 7 + (vm, vm),
        scratch_shapes=[
            pltpu.VMEM((d.NW, n_dp) + tile, BF16),
            pltpu.VMEM((3, T, D), BF16),
            pltpu.VMEM((3, 2, n * Dsl, T), BF16),
            pltpu.VMEM((3, T, D), F32),
            pltpu.VMEM((4, T, UNIT), F32),
            pltpu.VMEM((4, T, UNIT), BF16),
            pltpu.VMEM((4, T, UNIT), BF16),
            pltpu.VMEM((T, T), BF16),
            pltpu.VMEM((T, T), BF16),
            pltpu.VMEM((d.NS, n - 2) + tile, BF16),
            pltpu.VMEM((U,) + tile, BF16),
            pltpu.VMEM((U,) + tile, BF16),
            pltpu.VMEM((2, n) + tile, BF16),
            pltpu.VMEM((d.NSR, n) + tile, BF16),
            pltpu.VMEM((d.NLR, n - 1) + tile, BF16),
            pltpu.VMEM((2,) + tile, F32),
            pltpu.VMEM((2, UNIT, Dsl), F32),
            pltpu.VMEM((d.heads + d.chunks,) + tile, BF16),
            pltpu.VMEM((n_dp, rp, UNIT), F32),
            pltpu.VMEM((8, D), F32),
            pltpu.VMEM((U, 8, UNIT), F32),
            pltpu.VMEM((8, D), F32),
            pltpu.VMEM((U, 8, UNIT), F32),
            pltpu.VMEM((up, UNIT), F32),
            pltpu.VMEM((n_dp, 8, Dsl), F32),
            pltpu.VMEM((n_dp, up, UNIT), F32),
            pltpu.VMEM((8, Dsl), F32),
            pltpu.VMEM((tn, 8, Dsl), F32),
            dma((2,)),
            dma((d.NW,)),
            dma((d.NW, n_dp)),
            dma((d.NW, n)),
            dma((d.NW, n)),
            dma((d.NW, n)),
            reg((3,)),
            reg((2,)),
            reg((2,)),
            dma((2,)),
            dma((d.NSR,)),
            dma((d.NS, n - 2)),
            dma((d.NLR, n - 1)),
            dma((2,)),
            dma((n_dp,)),
            dma((n_dp,)),
            dma((2, n_dp)),
            dma((2, n_dp)),
            dma((tn,)),
            dma((tn,)),
            dma((2, tn)),
            dma((2, tn)),
            dma((2, tn)),
            dma((2, tn)),
            dma((2, tn)),
            dma((d.heads + d.chunks,)),
        ],
        compiler_params=pltpu.CompilerParams(
            collective_id=0, has_side_effects=True, vmem_limit_bytes=67_000_000
        ),
        cost_estimate=pl.CostEstimate(
            flops=6 * U * T * D * UNIT,
            bytes_accessed=6 * U * Dsl * UNIT + 8 * T * D,
            transcendentals=T * UNIT * U,
        ),
    )(seq_len, sp, rope, x, cot, wqkv, wout, wup, wdown)


def rope_pair(rows):
    half = ROT // 2
    freq_idx = jnp.arange(half, dtype=F32)
    inv_freq = jnp.exp(-(2.0 * freq_idx / ROT) * math.log(rope_base))
    angles = jnp.arange(rows, dtype=F32)[:, None] * inv_freq[None, :]
    cosine, sine = jnp.cos(angles), jnp.sin(angles)
    rest = 128 - ROT
    return jnp.stack(
        [
            jnp.concatenate([cosine, cosine, jnp.ones((rows, rest), F32)], axis=1),
            jnp.concatenate([-sine, sine, jnp.zeros((rows, rest), F32)], axis=1),
        ]
    )


def per_device(
    n_dp,
    tn,
    block_input,
    cotangent,
    lengths,
    attn_gain,
    attn_shift,
    ffn_gain,
    ffn_shift,
    qkv_weight,
    qkv_bias,
    out_weight,
    out_bias,
    up_weight,
    up_bias,
    down_weight,
):
    T, D = block_input.shape
    n = n_dp // 2
    Dsl = D // n_dp
    width = qkv_weight.shape[2]
    heads = width // HD
    hidden = up_weight.shape[1]
    chunks = hidden // UNIT
    U = 4 * heads + 2 * chunks
    gap = 2 if n <= 4 else 1
    e0 = 1
    d = types.SimpleNamespace(
        n=n,
        tn=tn,
        T=T,
        D=D,
        Dsl=Dsl,
        U=U,
        heads=heads,
        chunks=chunks,
        LAG=3,
        E=e0,
        gap=gap,
        ES=e0 + gap * (n - 2),
        E0=e0 + gap * (n - 1),
        NW=min(U, e0 + gap * (n - 1) + 6),
        NS=min(U, n + 3),
        NSR=4,
        NLR=n + 2,
        I1=14,
    )
    me = lax.axis_index("dp")

    nb, ub = qkv_bias.shape[1], up_bias.shape[0]
    norm_rows = jnp.stack([attn_gain, attn_shift, ffn_gain, ffn_shift, out_bias])
    norm_rows = jnp.pad(norm_rows.astype(F32), ((0, 3), (0, UNIT - Dsl)))
    qkv_rows = jnp.where(
        jnp.arange(width) // nb == me, jnp.tile(qkv_bias.astype(F32), (1, n_dp)), 0.0
    )
    qkv_rows = qkv_rows.reshape(3, heads, UNIT).transpose(1, 0, 2).reshape(3 * heads, UNIT)
    up_rows = jnp.where(jnp.arange(hidden) // ub == me, jnp.tile(up_bias.astype(F32), n_dp), 0.0)
    bias_rows = jnp.concatenate([qkv_rows, up_rows.reshape(chunks, UNIT)])
    spare = -bias_rows.shape[0] % 8
    sp = jnp.concatenate([norm_rows, jnp.pad(bias_rows, ((0, spare), (0, 0)))])

    out, dx, dqkv, dout, dup, ddown, _, so, sb = run_layer(
        d,
        lengths,
        sp,
        rope_pair(T),
        block_input,
        cotangent,
        qkv_weight,
        out_weight,
        up_weight,
        down_weight,
    )
    dqkv_b = sb[: 4 * heads].reshape(heads, 4, UNIT)[:, :3].transpose(1, 0, 2).reshape(3, width)
    dup_b = sb[4 * heads : U].reshape(chunks, 2, UNIT)[:, 0].reshape(hidden)
    return (
        out,
        dx,
        so[0],
        so[1],
        so[2],
        so[3],
        dqkv,
        lax.dynamic_slice_in_dim(dqkv_b, me * nb, nb, axis=1),
        dout,
        so[4],
        dup,
        lax.dynamic_slice_in_dim(dup_b, me * ub, ub, axis=0),
        ddown,
    )


def solution(mesh):
    in_specs = (
        P("dp", None),
        P("dp", None),
        P("dp"),
        P("dp"),
        P("dp"),
        P("dp"),
        P("dp"),
        P(None, "dp", "tensor"),
        P(None, ("tensor", "dp")),
        P("tensor", "dp"),
        P("dp"),
        P("dp", "tensor"),
        P(("tensor", "dp")),
        P("tensor", "dp"),
    )
    out_specs = (
        P("dp", None),
        P("dp", None),
        P("dp"),
        P("dp"),
        P("dp"),
        P("dp"),
        P(None, "dp", "tensor"),
        P(None, ("tensor", "dp")),
        P("tensor", "dp"),
        P("dp"),
        P("dp", "tensor"),
        P(("tensor", "dp")),
        P("tensor", "dp"),
    )
    return jax.shard_map(
        functools.partial(per_device, mesh.shape["dp"], mesh.shape["tensor"]),
        mesh=mesh,
        in_specs=in_specs,
        out_specs=out_specs,
        check_vma=False,
    )
```

time: 515 us -> 394 us (0.77)
  blocking collectives: 75.4 us -> 0 us
  Pallas kernels: 333 us -> 373 us
  waiting for transfers between devices: 34.1 us -> 0 us
  local copies, waits for them, and re-layouts: 40.7 us -> 16 us
  between operations: 15.7 us -> 1.54 us
  other arithmetic: 15.9 us -> 2.7 us
    unnamed x2 -> x0, blocking collectives: 57.6 us -> none
    pallas_call x1, Pallas kernels: 333 us -> 373 us  [run_layer(): pl.pallas_call(functools.partial(layer_kernel, d), out_shape=(jax.ShapeDt...]
    psum x1 -> x0, waiting for transfers between devices: 34.1 us -> none  [per_device(): part = lax.psum(part, 'tensor').astype(F32)]
    psum x1 -> x0, blocking collectives: 17.8 us -> none  [per_device(): stats = lax.psum(small[:4], 'tensor')]
    reshape x14 -> x3, local copies, waits for them, and re-layouts: 11.1 us -> 0.04 us  [the longest x1 0.02 us: per_device(): dup_b = sb[4 * heads:U].reshape(chunks, 2, UNIT)[:, 0].reshape(hidden)]
    transpose x6 -> x1, local copies, waits for them, and re-layouts: 9.82 us -> 0.01 us  [per_device(): qkv_rows.reshape(3, heads, UNIT).transpose(1, 0, 2).reshape(3 * heads, UNIT)]
    unnamed x25 -> x30, local copies, waits for them, and re-layouts: 2.92 us -> 11.5 us
    slice x10 -> x4, local copies, waits for them, and re-layouts: 11.1 us -> 2.89 us  [the longest x1 1.46 us: per_device(): so[4]]
  transfers between devices with their start and end apart: 1 -> 0, of which waited for: 1 -> 0; matrix products, arithmetic and copies ran while one was open for 5% -> 0% of each run, Pallas kernels for 0% -> 0%
where the time goes in v3:
time: 394 us; the launch traced here: 393 us
  Pallas kernels  373 us (95%)
  local copies, waits for them, and re-layouts  16 us (4%)
    pallas_call x1, Pallas kernels, run_layer(): pl.pallas_call(functools.partial(layer_kernel, d), out_shape=(jax.ShapeDt...  373 us
    unnamed x30, local copies, waits for them, and re-layouts  11.5 us

profile of v3, /device:TPU:0, one launch (start us, length us, event | category | flops | bytes accessed | tf_op | source)
XLA Modules:
  0.0 393.3 jit_solution(13470230667431513703)
XLA Ops:
  0.6 0.0 copy-start.5
  0.7 0.0 copy-start.6
  0.7 0.0 copy-start.7
  0.7 0.0 copy-start.8
  0.7 0.0 copy-start.9
  0.7 0.0 copy-start.10
  0.7 1.0 fusion.1
  1.7 0.1 pad.18.clone
  1.8 0.1 pad.21.clone
  1.9 0.2 maximum_bitcast_fusion
  2.1 0.8 pad_maximum_fusion.rope_ref
  3.0 0.1 tile.7
  3.1 0.0 copy-done.7
  3.1 0.0 copy-done.8
  3.2 0.0 copy-done.9
  3.3 0.6 pad_maximum_fusion.1.sp_ref
  4.5 373.1 %shard_map.237 = (bf16[512,2048]{1,0:T(8,128)(2,1)}, bf16[512,2048]{1,0:T(8,128)(2,1)}, f32[3,256,512]{2,1,0:T(8,128)}, f32[512,256]{1,0:T(8,128)}, f32[256,2048...) custom-call(s32[1]{0:T(128)S(6)} %copy.36.len_ref, ...), custom_call_target="tpu_custom_call" | custom-call | flops 38654705664 | bytes 17825792 | tf_op jit(solution)/shard_map/pallas_call | solution.py:884
  377.6 0.7 slice.34
  378.4 0.6 dynamic_slice.7
  379.0 0.7 slice.31
  379.7 0.6 constant_dynamic-slice_fusion
  380.3 1.5 fusion.9
  381.8 3.3 copy.37
  385.1 1.3 copy.38
  386.4 0.8 copy-done.3
  387.3 1.1 copy.39
  388.4 0.2 copy-done.4
  388.7 0.8 copy.40
  389.5 0.2 copy-done.1
  389.6 1.3 copy.41
  390.9 1.0 copy-done
  392.0 1.3 copy.42
  (32 shorter events, 0.2 us)
Async XLA Ops:
  0.6 2.3 copy-start.5
  0.7 2.4 copy-start.6
  0.7 2.5 copy-start.7
  0.7 2.5 copy-start.8
  0.7 2.5 copy-start.9
  0.7 2.5 copy-start.10
  0.7 2.5 copy-start.11
  381.8 3.3 copy-start.2
  385.1 2.2 copy-start.3
  387.3 1.4 copy-start.4
  387.3 2.3 copy-start.1
  389.6 2.3 copy-start

commit v4 on v3

--- a/solution.py
+++ b/solution.py
@@ -13,6 +13,7 @@
 ROT = 64
 UNIT = 256
 ROWS = 128
+SLAB = 64
 MESH = pl.DeviceIdType.MESH
 
 norm_eps = 1e-05
@@ -60,7 +61,6 @@
     sb_ref,
     W,
     A,
-    At,
     Acc,
     Y,
     G,
@@ -68,14 +68,11 @@
     PB,
     DS,
     S,
-    DL,
-    DR,
     SB,
     SR,
     LR,
     stage,
     stage_t,
-    OT,
     RP,
     NB,
     BI,
@@ -92,7 +89,6 @@
     agR,
     agL,
     agS,
-    credit,
     lcredit,
     ready,
     sb_sem,
@@ -106,18 +102,24 @@
     sm_r,
     st_s,
     st_r,
-    pr_s,
-    pr_r,
-    fo_s,
-    fo_r,
+    s1_s,
+    s1_r,
+    s2_s,
+    s2_r,
+    f1_s,
+    f1_r,
+    f2_s,
+    f2_r,
     loc_sem,
     raw_sem,
+    p2_s,
+    p2_r,
 ):
     n, tn, T, D, Dsl, U, heads = d.n, d.tn, d.T, d.D, d.Dsl, d.U, d.heads
-    n_dp, NW, NS, NSR, NLR, LAG = 2 * d.n, d.NW, d.NS, d.NSR, d.NLR, d.LAG
-    E, ES, E0 = d.E, d.ES, d.E0
+    n_dp, NS, NSR, NLR = 2 * d.n, d.NS, d.NSR, d.NLR
     Tr = T // tn
-    A4 = 4 * heads
+    F0 = d.F0
+    F1 = F0 + 4 * heads
     chunks = d.chunks
     me = lax.axis_index("dp")
     mt = lax.axis_index("tensor")
@@ -144,10 +146,38 @@
     def signal(sem, dev, axis="dp"):
         pl.semaphore_signal(sem, inc=1, device_id={axis: dev}, device_id_type=MESH)
 
+    def is_attn(u):
+        return (u >= F0) & (u < F1)
+
+    def chunk_of(u):
+        return jnp.where(u < F0, u // 2, (u - 4 * heads) // 2)
+
+    def head_of(u):
+        return (u - F0) // 4
+
     def aidx(u):
         attn = jnp.where(u % 4 == 3, 2, 0)
-        ffn = jnp.where((u - A4) % 2 == 0, 1, 2)
-        return jnp.where(u < A4, attn, ffn)
+        ffn = jnp.where(u % 2 == 0, 1, 2)
+        return jnp.where(is_attn(u), attn, ffn)
+
+    def by_kind(u, qkv, o, up, down):
+        ffn = jnp.logical_not(is_attn(u))
+
+        @pl.when(is_attn(u) & (u % 4 != 3))
+        def _():
+            qkv()
+
+        @pl.when(is_attn(u) & (u % 4 == 3))
+        def _():
+            o()
+
+        @pl.when(ffn & (u % 2 == 0))
+        def _():
+            up()
+
+        @pl.when(ffn & (u % 2 == 1))
+        def _():
+            down()
 
     def each_dp(f):
         for p in range(n_dp):
@@ -164,63 +194,45 @@
                 f(p)
 
     def own_tile(u, f):
-        @pl.when((u < A4) & (u % 4 != 3))
-        def _():
-            f(wqkv.at[u % 4, :, ds(u // 4, UNIT)])
-
-        @pl.when((u < A4) & (u % 4 == 3))
-        def _():
-            f(OT.at[u // 4])
-
-        @pl.when((u >= A4) & (u % 2 == 0))
-        def _():
-            f(wup.at[:, ds((u - A4) // 2, UNIT)])
-
-        @pl.when((u >= A4) & (u % 2 == 1))
-        def _():
-            f(OT.at[heads + (u - A4) // 2])
-
-    def ag_tile(slot, sj, sem, dev):
-        return rcopy(W.at[slot, sj], W.at[slot, sj], sem, ag_recv.at[slot, sj], dev)
+        by_kind(
+            u,
+            lambda: f(wqkv.at[u % 4, :, ds(head_of(u), UNIT)]),
+            lambda: f(W.at[u, me]),
+            lambda: f(wup.at[:, ds(chunk_of(u), UNIT)]),
+            lambda: f(W.at[u, me]),
+        )
+
+    def ag_tile(u, sj, sem, dev):
+        return rcopy(W.at[u, sj], W.at[u, sj], sem, ag_recv.at[u, sj], dev)
+
+    def own_load(src, u):
+        return pltpu.make_async_copy(src, W.at[u, me], own_sem.at[u])
 
     def ag_self(u):
-        slot = u % NW
-
-        @pl.when(u >= NW)
-        def _():
-            pl.semaphore_wait(credit.at[2], 1)
-
         def go(src):
-            pltpu.make_async_copy(src, W.at[slot, me], own_sem.at[slot]).start()
-            rcopy(src, W.at[slot, me], agS.at[slot, z], ag_recv.at[slot, me], sib).start()
+            rcopy(src, W.at[u, me], agS.at[u, z], ag_recv.at[u, me], sib).start()
 
         own_tile(u, go)
 
+    def ag_own(u, has_next, sems, dev):
+        @pl.when(has_next)
+        def _():
+            def go(src):
+                rcopy(src, W.at[u, me], sems.at[u, z], ag_recv.at[u, me], dev).start()
+
+            own_tile(u, go)
+
     def relay(u, j, has_next, sems, dev):
-        slot = u % NW
         sj = j * 2 + c
-        ag_tile(slot, sj, agS.at[slot, j], sib).wait_recv()
+        ag_tile(u, sj, agS.at[u, j], sib).wait_recv()
 
         @pl.when(has_next)
         def _():
-            ag_tile(slot, sj, sems.at[slot, j], dev).start()
-
-        ag_tile(slot, sj, agS.at[slot, j], sib).start()
-
-    def ag_line(u, has_next, credit_sem, sems, dev, sign):
-        slot = u % NW
-
-        @pl.when(has_next)
-        def _():
-            @pl.when(u >= NW)
-            def _():
-                pl.semaphore_wait(credit_sem, 1)
-
-            def go(src):
-                rcopy(src, W.at[slot, me], sems.at[slot, z], ag_recv.at[slot, me], dev).start()
-
-            own_tile(u, go)
-
+            ag_tile(u, sj, sems.at[u, j], dev).start()
+
+        ag_tile(u, sj, agS.at[u, j], sib).start()
+
+    def ag_line(u, has_next, sems, dev, sign):
         for k in range(1, n):
             j = z + sign * k
 
@@ -233,62 +245,77 @@
         def _():
             f(v)
 
+    def ahead(h):
+        return d.ahead[0] if h == 0 else d.ahead[1] + d.ahead[2] * (h - 1)
+
+    def ahead_of(h):
+        total = jnp.int32(0)
+        for k in range(n):
+            total = jnp.where(h == k, ahead(k), total)
+        return total
+
+    to_r, to_l = n - 1 - z, z
+
     def ag_step(s):
-        guarded(s + ES, ag_self)
-        guarded(
-            s + E + d.gap * (n - 1 - z),
-            lambda u: ag_line(u, has_r, credit.at[0], agR, right, -1),
-        )
-        guarded(s + E + d.gap * z, lambda u: ag_line(u, has_l, credit.at[1], agL, left, 1))
+        def late(v, f):
+            @pl.when((v >= d.burst) & (v < U))
+            def _():
+                f(v)
+
+        late(s + d.own, ag_self)
+
+        @pl.when(has_l)
+        def _():
+            late(s + ahead_of(to_r) + 1, lambda u: ag_own(u, has_r, agR, right))
+
+        @pl.when(has_r)
+        def _():
+            late(s + ahead_of(to_l) + 1, lambda u: ag_own(u, has_l, agL, left))
+
+        guarded(s + ahead_of(to_r), lambda u: ag_line(u, has_r, agR, right, -1))
+        guarded(s + ahead_of(to_l), lambda u: ag_line(u, has_l, agL, left, 1))
 
     def ag_wait(u):
-        slot = u % NW
-        pltpu.make_async_copy(OT.at[0], W.at[slot, me], own_sem.at[slot]).wait()
+        nothing = lambda: None
+        landed = lambda: own_load(wup.at[:, 0:UNIT], u).wait()
+        by_kind(u, landed, nothing, landed, nothing)
         for j in range(n):
-            ag_tile(slot, j * 2 + 1 - c, agS.at[slot, j], sib).wait_recv()
+            ag_tile(u, j * 2 + 1 - c, agS.at[u, j], sib).wait_recv()
 
     def ag_finish(u):
-        slot = u % NW
         for j in range(n):
 
             @pl.when(has_r & (j <= z))
             def _(j=j):
-                ag_tile(slot, j * 2 + c, agR.at[slot, j], right).wait_send()
+                ag_tile(u, j * 2 + c, agR.at[u, j], right).wait_send()
 
             @pl.when(has_l & (j >= z))
             def _(j=j):
-                ag_tile(slot, j * 2 + c, agL.at[slot, j], left).wait_send()
-
-            ag_tile(slot, j * 2 + c, agS.at[slot, j], sib).wait_send()
-
-        @pl.when(u + NW < U)
-        def _():
-            @pl.when(has_r)
-            def _():
-                signal(credit.at[1], right)
-
-            @pl.when(has_l)
-            def _():
-                signal(credit.at[0], left)
-
-            signal(credit.at[2], sib)
+                ag_tile(u, j * 2 + c, agL.at[u, j], left).wait_send()
+
+            ag_tile(u, j * 2 + c, agS.at[u, j], sib).wait_send()
+
+    def dead(v, j):
+        return W.at[v, j * 2 + 1 - c]
 
     def part_ref(v, zt):
-        if zt == 0:
-            return DL.at[v]
-        if zt == n - 1:
-            return DR.at[v]
+        if zt == 0 or zt == n - 1:
+            return dead(v, zt)
         return S.at[v % NS, zt - 1]
 
     def sb_copy(u):
         return rcopy(SB.at[u % 2], SR.at[u % NSR], sb_sem.at[u % 2], sr_sem.at[u % NSR], sib)
 
     def ls_copy(v, zt, to_right):
-        slot = zt if to_right else zt - 1
+        slot = zt if to_right else (zt - 1) % n
+        if isinstance(zt, int):
+            src = part_ref(v, zt)
+        else:
+            src = S.at[v % NS, zt - 1]
         return rcopy(
-            S.at[v % NS, zt - 1],
+            src,
             LR.at[v % NLR, slot],
-            ls_sem.at[v % NS, zt - 1],
+            ls_sem.at[v % NS, zt],
             lr_sem.at[v % NLR, slot],
             right if to_right else left,
         )
@@ -297,7 +324,7 @@
         a = aidx(u)
         g = G[u % 4]
         for j in range(n):
-            put(j, dot(At[a, core, j * Dsl : (j + 1) * Dsl, :], g).astype(BF16))
+            put(j, dot_tn(A[a, :, ds(j * 2 + core, Dsl)], g).astype(BF16))
 
     def dw_sib(u):
         @pl.when(u >= 2)
@@ -311,9 +338,14 @@
         sb_copy(u).start()
 
     def rs_finish(v):
-        for zt in range(1, n - 1):
-
-            @pl.when(zt != z)
+        for zt in range(n):
+            sent = zt != z
+            if zt == n - 1:
+                sent = sent & (z == 0)
+            if zt == 0:
+                sent = sent & (z == n - 1)
+
+            @pl.when(sent)
             def _(zt=zt):
                 ls_copy(v, zt, True).wait_send()
 
@@ -340,32 +372,52 @@
         def _():
             pl.semaphore_wait(lcredit.at[0], 1)
 
-        for zt in range(1, n - 1):
-
-            @pl.when(zt > z)
-            def _(zt=zt):
-                @pl.when(has_l)
-                def _():
-                    ls_copy(v, zt, True).wait_recv()
-                    add_into(S.at[v % NS, zt - 1], LR.at[v % NLR, zt])
-
+        for zt in range(1, n):
+            inner = zt < n - 1
+
+            def take(zt=zt):
+                ls_copy(v, zt, True).wait_recv()
+                add_into(part_ref(v, zt), LR.at[v % NLR, zt])
+
+            def go(zt=zt):
                 ls_copy(v, zt, True).start()
+
+            if inner:
+
+                @pl.when(zt > z)
+                def _(take=take, go=go):
+                    pl.when(has_l)(take)
+                    go()
+
+            else:
+                pl.when(z == 0)(go)
+                pl.when(z == 1)(take)
 
     def send_left(v):
         @pl.when((z - 1 >= 1) & (v >= NLR))
         def _():
             pl.semaphore_wait(lcredit.at[1], 1)
 
-        for zt in range(1, n - 1):
-
-            @pl.when(zt < z)
-            def _(zt=zt):
-                @pl.when(has_r)
-                def _():
-                    ls_copy(v, zt, False).wait_recv()
-                    add_into(S.at[v % NS, zt - 1], LR.at[v % NLR, zt - 1])
-
+        for zt in range(n - 2, -1, -1):
+            inner = zt > 0
+
+            def take(zt=zt):
+                ls_copy(v, zt, False).wait_recv()
+                add_into(part_ref(v, zt), LR.at[v % NLR, (zt - 1) % n])
+
+            def go(zt=zt):
                 ls_copy(v, zt, False).start()
+
+            if inner:
+
+                @pl.when(zt < z)
+                def _(take=take, go=go):
+                    pl.when(has_r)(take)
+                    go()
+
+            else:
+                pl.when(z == n - 1)(go)
+                pl.when(z == n - 2)(take)
 
     def out_wait(v):
         pltpu.make_async_copy(
@@ -374,35 +426,21 @@
 
     def out_start(v):
         slot = v % 2
-        sem = out_sem.at[slot]
-
-        @pl.when((v < A4) & (v % 4 != 3))
-        def _():
-            pltpu.make_async_copy(
-                stage.at[slot], dqkv_hbm.at[v % 4, :, ds(v // 4, UNIT)], sem
-            ).start()
-
-        @pl.when((v >= A4) & (v % 2 == 0))
-        def _():
-            pltpu.make_async_copy(
-                stage.at[slot], dup_hbm.at[:, ds((v - A4) // 2, UNIT)], sem
-            ).start()
-
-        @pl.when(((v < A4) & (v % 4 == 3)) | ((v >= A4) & (v % 2 == 1)))
+
+        def put(src, dst):
+            pltpu.make_async_copy(src.at[slot], dst, out_sem.at[slot]).start()
+
+        @pl.when(is_attn(v) & (v % 4 == 3) | jnp.logical_not(is_attn(v)) & (v % 2 == 1))
         def _():
             stage_t[slot] = jnp.transpose(stage[slot])
 
-            @pl.when(v < A4)
-            def _():
-                pltpu.make_async_copy(
-                    stage_t.at[slot], dout_hbm.at[ds(v // 4, UNIT), :], sem
-                ).start()
-
-            @pl.when(v >= A4)
-            def _():
-                pltpu.make_async_copy(
-                    stage_t.at[slot], ddown_hbm.at[ds((v - A4) // 2, UNIT), :], sem
-                ).start()
+        by_kind(
+            v,
+            lambda: put(stage, dqkv_hbm.at[v % 4, :, ds(head_of(v), UNIT)]),
+            lambda: put(stage_t, dout_hbm.at[ds(head_of(v), UNIT), :]),
+            lambda: put(stage, dup_hbm.at[:, ds(chunk_of(v), UNIT)]),
+            lambda: put(stage_t, ddown_hbm.at[ds(chunk_of(v), UNIT), :]),
+        )
 
     def final(v):
         @pl.when((z >= 1) & (z <= n - 2))
@@ -426,26 +464,28 @@
                 signal(lcredit.at[0], left)
                 signal(lcredit.at[1], right)
 
-    def rs_step(s):
-        base = s - LAG - 1
-        guarded(base, combine)
-        guarded(base - z, send_right)
-        guarded(base - (n - 1 - z), send_left)
-        guarded(base - jnp.maximum(z, n - 1 - z), final)
-
-    def p2_slot(i):
-        return W.at[i // n_dp, i % n_dp], ag_recv.at[i // n_dp, i % n_dp]
+    def behind(h):
+        return jnp.where(h == 0, 0, d.lag + (h - 1) * d.lag2)
+
+    def rs_step(q):
+        guarded(q - 1 - behind(z), send_right)
+        guarded(q - 1 - behind(n - 1 - z), send_left)
+        guarded(q - 1 - behind(jnp.maximum(z, n - 1 - z)), final)
 
     def p2_copy(u, to_right):
-        dst, rs = p2_slot(u if to_right else U + u)
-        src = DR.at[u] if to_right else DL.at[u]
-        sems = agR if to_right else agL
-        return rcopy(src, dst, sems.at[u // n, u % n], rs, right if to_right else left)
+        side = 0 if to_right else 1
+        return rcopy(
+            dead(u, n - 1 if to_right else 0),
+            dead(u, 1 if to_right else n - 2),
+            p2_s.at[side, u],
+            p2_r.at[side, u],
+            right if to_right else left,
+        )
 
     def p2_side(u, to_right):
-        has_prev, has_next = (has_l, has_r) if to_right else (has_r, has_l)
-        mine = DR.at[u] if to_right else DL.at[u]
-        got, _ = p2_slot(u if to_right else U + u)
+        has_prev, has_next = (z >= 2, has_r) if to_right else (z <= n - 3, has_l)
+        mine = dead(u, n - 1 if to_right else 0)
+        got = dead(u, 1 if to_right else n - 2)
         cp = p2_copy(u, to_right)
 
         @pl.when(has_prev)
@@ -469,9 +509,23 @@
             stage[u % 2] = mine[...].astype(F32) + got[...].astype(F32)
             out_start(u)
 
+    def p2_first(u):
+        @pl.when(z == 1)
+        def _():
+            p2_side(u, True)
+
+        @pl.when(z == n - 2)
+        def _():
+            p2_side(u, False)
+
     def p2_step(i):
-        guarded(i - z, lambda u: p2_side(u, True))
-        guarded(i - (n - 1 - z), lambda u: p2_side(u, False))
+        @pl.when(z >= 2)
+        def _():
+            guarded(i - d.hop * (z - 2), lambda u: p2_side(u, True))
+
+        @pl.when(z <= n - 3)
+        def _():
+            guarded(i - d.hop * (n - 3 - z), lambda u: p2_side(u, False))
 
     def layer_norm(x):
         mean = jnp.mean(x, axis=-1, keepdims=True)
@@ -479,25 +533,30 @@
         inv = lax.rsqrt(jnp.mean(cen * cen, axis=-1, keepdims=True) + norm_eps)
         return cen * inv, inv
 
+    def slabs(first, count, f):
+        def one(j, carry):
+            f(pl.ds(pl.multiple_of(first + j * SLAB, SLAB), SLAB), first + j * SLAB)
+            return carry
+
+        lax.fori_loop(0, count // SLAB, one, 0)
+
     def ln_block(i):
-        rows = ds(i, ROWS)
-        normed, _ = layer_norm(A[0, rows, :].astype(F32))
-        A[0, rows, :] = (normed * NB[0:1, :] + NB[1:2, :]).astype(BF16)
-        A[1, rows, :] = (normed * NB[2:3, :] + NB[3:4, :]).astype(BF16)
-        pos = lax.broadcasted_iota(jnp.int32, (ROWS, D), 0) + i * ROWS
-        grad = jnp.where(pos < seq_len, A[2, rows, :].astype(F32), 0.0)
-        A[2, rows, :] = grad.astype(BF16)
-        SM[4:5, :] += jnp.sum(grad, axis=0, keepdims=True)
+        def normalize(rows, at):
+            normed, _ = layer_norm(A[0, rows, :].astype(F32))
+            A[0, rows, :] = (normed * NB[0:1, :] + NB[1:2, :]).astype(BF16)
+            A[1, rows, :] = (normed * NB[2:3, :] + NB[3:4, :]).astype(BF16)
+            pos = lax.broadcasted_iota(jnp.int32, (SLAB, D), 0) + at
+            grad = jnp.where(pos < seq_len, A[2, rows, :].astype(F32), 0.0)
+            A[2, rows, :] = grad.astype(BF16)
+            SM[4:5, :] += jnp.sum(grad, axis=0, keepdims=True)
+
+        slabs(i * ROWS, ROWS, normalize)
         for a in range(3):
-            for j in range(2 * n):
-                At[a, j % 2, (j // 2) * Dsl : (j // 2 + 1) * Dsl, rows] = jnp.transpose(
-                    A[a, rows, j * Dsl : (j + 1) * Dsl]
-                )
-            Acc[a, rows, :] = jnp.zeros((ROWS, D), F32)
+            Acc[a, ds(i, ROWS), :] = jnp.zeros((ROWS, D), F32)
 
     def y_step(u):
         ag_wait(u)
-        w = W[u % NW].reshape(D, UNIT)
+        w = W[u].reshape(D, UNIT)
         Y[u % 4] = dot(A[aidx(u)], w)
 
     def acc_step(u):
@@ -505,7 +564,7 @@
         g = G[u % 4]
         for j in range(2 * n):
             cols = slice(j * Dsl, (j + 1) * Dsl)
-            Acc[a, :, cols] += dot_nt(g, W[u % NW, j])
+            Acc[a, :, cols] += dot_nt(g, W[u, j])
 
     lane = lax.broadcasted_iota(jnp.int32, (T, 128), 1)
 
@@ -597,6 +656,19 @@
     ]
     for cp in raws:
         cp.start()
+
+    def load_own(u, carry):
+        nothing = lambda: None
+        by_kind(
+            u,
+            lambda: own_load(wqkv.at[u % 4, :, ds(head_of(u), UNIT)], u).start(),
+            nothing,
+            lambda: own_load(wup.at[:, ds(chunk_of(u), UNIT)], u).start(),
+            nothing,
+        )
+        return carry
+
+    lax.fori_loop(0, U, load_own, 0)
     pl.semaphore_wait(barrier, n_dp - 1 + tn - 1)
 
     def sp_copy(p, where):
@@ -605,14 +677,30 @@
     each_dp(lambda p: sp_copy(p, me).start())
     RP[me] = sp_ref[...]
 
-    def early(s, carry):
-        ag_step(s)
+    def burst(u, carry):
+        ag_own(u, has_r, agR, right)
+        ag_own(u, has_l, agL, left)
+        ag_self(u)
         return carry
 
-    lax.fori_loop(-E0, 3 - E0, early, 0)
+    lax.fori_loop(0, d.burst, burst, 0)
     for i, cp in enumerate(raws):
         cp.wait()
-        OT[i] = jnp.transpose(spots[i][...])
+        u = 4 * i + 3 if i < heads else F1 + 2 * (i - heads) + 1
+        W[u, me] = jnp.transpose(spots[i][...])
+
+    def end_chip(u, carry):
+        @pl.when(z == 0)
+        def _():
+            ag_own(u, has_r, agR, right)
+
+        @pl.when(z == n - 1)
+        def _():
+            ag_own(u, has_l, agL, left)
+
+        return carry
+
+    lax.fori_loop(d.burst, U, end_chip, 0)
     SM[...] = jnp.zeros_like(SM)
     BG[...] = jnp.zeros_like(BG)
     BI[...] = jnp.zeros_like(BI)
@@ -623,55 +711,76 @@
         row = RP[0, 8 + i : 9 + i, :]
         for p in range(1, n_dp):
             row = row + RP[p, 8 + i : 9 + i, :]
-        u = 4 * (i // 3) + i % 3 if i < 3 * heads else A4 + 2 * (i - 3 * heads)
+        if i < 3 * heads:
+            u = F0 + 4 * (i // 3) + i % 3
+        else:
+            u = 2 * (i - 3 * heads)
+            u = u if u < F0 else u + 4 * heads
         BI[u] = jnp.broadcast_to(row, (8, UNIT))
     x_in.wait()
     c_in.wait()
     blocks = T // ROWS
 
+    fills = max(ahead(h) for h in range(n - 1))
+
     def fill(i, carry):
+        @pl.when(i < fills)
+        def _():
+            ag_step(i - fills)
+
         @pl.when(i < blocks)
         def _():
             ln_block(i)
 
-        @pl.when(i < E0 - 3)
-        def _():
-            ag_step(i + 3 - E0)
-
         return carry
 
-    lax.fori_loop(0, max(E0 - 3, blocks), fill, 0)
+    lax.fori_loop(0, max(fills, blocks), fill, 0)
+
+    def made(s):
+        return jnp.maximum(jnp.where(s < F1, s - 2, jnp.where(s == F1, s - 1, s)), 0)
+
+    sent_early = max(0, U - d.held - 1 - d.lag)
+
+    def early(q):
+        return jnp.clip(jnp.minimum(2 * (q - d.Q0 + 1), q - d.lag), 0, sent_early)
+
+    def first_one(u, carry):
+        p2_first(u)
+        return carry
+
+    def make(q, carry):
+        dw_sib(q)
+        guarded(q - 1, combine)
+
+        @pl.when(q < U - d.held)
+        def _():
+            rs_step(q)
+
+        acc_step(q)
+        dw_own(q)
+        lax.fori_loop(early(q - 1), early(q), first_one, 0)
+        return carry
 
     def body(s, carry):
         ag_step(s)
         guarded(s, y_step)
 
-        @pl.when(s == A4)
+        @pl.when(s == F1 + 2)
         def _():
             x_in.start()
 
-        @pl.when((s < A4) & (s % 4 == 3))
+        @pl.when(is_attn(s) & (s % 4 == 3))
         def _():
             attn_core(s)
 
-        @pl.when((s >= A4) & (s < U) & (s % 2 == 1))
+        @pl.when(jnp.logical_not(is_attn(s)) & (s < U) & (s % 2 == 1))
         def _():
             ffn_core(s)
 
-        u = s - LAG
-        guarded(u, dw_sib)
-        rs_step(s)
-
-        def rest(u):
-            dw_own(u)
-            acc_step(u)
-
-        guarded(u, rest)
-        guarded(u - 1, ag_finish)
+        lax.fori_loop(made(s - 1), made(s), make, 0)
         return carry
 
-    lax.fori_loop(0, U + LAG, body, 0)
-    ag_finish(U - 1)
+    lax.fori_loop(0, U + 1, body, 0)
     x_in.wait()
 
     @pl.when(has_r)
@@ -682,44 +791,104 @@
     def _():
         signal(ready.at[0], left)
 
-    def pr_copy(k, i, where):
+    lo = d.lo
+    hi = tn // lo
+    size = ((lo, hi), (hi, lo))
+    coord = ((mt % lo, mt // lo), (mt // lo, mt % lo))
+    acc_of = (2, 0)
+    own = ds(mt, Tr)
+
+    def block_of(k, a, b):
+        return b * lo + a if k == 0 else a * lo + b
+
+    def packed(mine, theirs):
+        return mine - jnp.where(mine > theirs, 1, 0)
+
+    def s1_copy(k, a, b, sender):
+        s2 = size[k][1]
         return rcopy_to(
-            A.at[k, ds(i, Tr), :],
-            pr_hbm.at[k, ds(where, Tr), :],
-            pr_s.at[k, i],
-            pr_r.at[k, where],
-            {"tensor": i},
-        )
-
-    def part_send(i):
-        @pl.when((i >= 0) & (i != mt))
-        def _():
-            pr_copy(0, i, mt).start()
-            pr_copy(1, i, mt).start()
+            A.at[k, ds(block_of(k, a, b), Tr), :],
+            pr_hbm.at[k, packed(sender, a) * s2 + b],
+            s1_s.at[k, a * s2 + b],
+            s1_r.at[k, sender * s2 + b],
+            {"tensor": block_of(k, a, coord[k][1])},
+        )
+
+    def s1_wait(k, q, b):
+        s2 = size[k][1]
+        c1 = coord[k][0]
+        return rcopy_to(
+            A.at[k, own, :],
+            pr_hbm.at[k, packed(q, c1) * s2 + b],
+            s1_s.at[k, q * s2 + b],
+            s1_r.at[k, q * s2 + b],
+            {"tensor": block_of(k, q, coord[k][1])},
+        )
+
+    def s2_copy(k, b, sender):
+        c1 = coord[k][0]
+        return rcopy_to(
+            A.at[k, ds(block_of(k, c1, b), Tr), :],
+            pr_hbm.at[k, d.P1 + packed(sender, b)],
+            s2_s.at[k, b],
+            s2_r.at[k, sender],
+            {"tensor": block_of(k, c1, b)},
+        )
+
+    def s2_wait(k, q):
+        c1, c2 = coord[k]
+        return rcopy_to(
+            A.at[k, own, :],
+            pr_hbm.at[k, d.P1 + packed(q, c2)],
+            s2_s.at[k, q],
+            s2_r.at[k, q],
+            {"tensor": block_of(k, c1, q)},
+        )
+
+    def others(k, which, f):
+        for q in range(size[k][which]):
+
+            @pl.when(q != coord[k][which])
+            def _(q=q):
+                f(q)
+
+    def s1_send(i):
+        @pl.when(i >= 0)
+        def _():
+            for k in range(2):
+                a = i % lo if k == 0 else i // lo
+                b = i // lo if k == 0 else i % lo
+
+                @pl.when(a != coord[k][0])
+                def _(k=k, a=a, b=b):
+                    s1_copy(k, a, b, coord[k][0]).start()
 
     def partial(i, carry):
-        rows = ds(i, Tr)
-        normed, _ = layer_norm(A[0, rows, :].astype(F32))
-        ab = Acc[0, rows, :]
-        fb = Acc[1, rows, :]
-        SM[0:1, :] += jnp.sum(ab * normed, axis=0, keepdims=True)
-        SM[1:2, :] += jnp.sum(ab, axis=0, keepdims=True)
-        SM[2:3, :] += jnp.sum(fb * normed, axis=0, keepdims=True)
-        SM[3:4, :] += jnp.sum(fb, axis=0, keepdims=True)
-        ng = ab * NB[0:1, :] + fb * NB[2:3, :]
-        Acc[0, rows, :] = ng
-        @pl.when(i != mt)
-        def _():
+        @pl.when(i == mt)
+        def _():
+            A[2, ds((mt + 1) % tn, Tr), :] = A[0, ds(i, Tr), :]
+
+        def rows_of(rows, at):
+            normed, _ = layer_norm(A[0, rows, :].astype(F32))
+            ab = Acc[0, rows, :]
+            fb = Acc[1, rows, :]
+            SM[0:1, :] += jnp.sum(ab * normed, axis=0, keepdims=True)
+            SM[1:2, :] += jnp.sum(ab, axis=0, keepdims=True)
+            SM[2:3, :] += jnp.sum(fb * normed, axis=0, keepdims=True)
+            SM[3:4, :] += jnp.sum(fb, axis=0, keepdims=True)
+            ng = ab * NB[0:1, :] + fb * NB[2:3, :]
+            Acc[0, rows, :] = ng
             A[1, rows, :] = ng.astype(BF16)
             A[0, rows, :] = Acc[2, rows, :].astype(BF16)
 
-        part_send(i - 1)
+        slabs(i * Tr, Tr, rows_of)
+        s1_send(i - 1)
         return carry
 
     lax.fori_loop(0, tn, partial, 0)
     for u in range(U):
         BGC[u : u + 1, :] = BG[u, 0:1, :]
-    part_send(tn - 1)
+    s1_send(tn - 1)
 
     def sm_copy(p, where):
         return rcopy(
@@ -745,17 +914,62 @@
     def _():
         pl.semaphore_wait(ready.at[1], 1)
 
-    def drain(i, carry):
-        @pl.when(i < n)
-        def _():
-            rs_step(i + U + LAG)
-
+    rest = d.held + d.lag + (n - 3) * d.lag2 + 1
+    steps = U + d.hop * (n - 3)
+
+    def p2_count(i):
+        fed = jnp.minimum(d.pace * (i + 1), sent_early + i)
+        return jnp.clip(jnp.where(i < rest, fed, steps), 0, steps)
+
+    def p2_one(i, carry):
         p2_step(i)
         return carry
 
-    steps = U + n - 1
-    middle = min(d.I1, steps)
-    lax.fori_loop(0, middle, drain, 0)
+    def drain(i, carry):
+        rs_step(i + U - d.held)
+        guarded(i + sent_early, p2_first)
+        lax.fori_loop(p2_count(i - 1), p2_count(i), p2_one, 0)
+        return carry
+
+    marks = [min(m, rest) for m in d.marks]
+    combine(U - 1)
+    lax.fori_loop(0, marks[0], drain, 0)
+
+    def load(k, slot, b):
+        return pltpu.make_async_copy(
+            pr_hbm.at[k, slot], A.at[k, ds(b, Tr), :], loc_sem.at[k, slot]
+        )
+
+    def gather_in(k, do):
+        s1, s2 = size[k]
+        for b in range(s2):
+            do(b, block_of(k, coord[k][0], b))
+
+    for k in range(2):
+        s1, s2 = size[k]
+
+        def take(q, k=k, s2=s2):
+            for b in range(s2):
+                s1_wait(k, q, b).wait_recv()
+
+        others(k, 0, take)
+        for q in range(s1 - 1):
+            for b in range(s2):
+                load(k, q * s2 + b, block_of(k, coord[k][0], b)).start()
+            for b in range(s2):
+                row_b = block_of(k, coord[k][0], b)
+                load(k, q * s2 + b, row_b).wait()
+                rows = ds(row_b, Tr)
+                Acc[acc_of[k], rows, :] += A[k, rows, :].astype(F32)
+
+        def pass_on(b, k=k):
+            rows = ds(block_of(k, coord[k][0], b), Tr)
+            A[k, rows, :] = Acc[acc_of[k], rows, :].astype(BF16)
+            s2_copy(k, b, coord[k][1]).start()
+
+        others(k, 1, pass_on)
+
+    lax.fori_loop(marks[0], marks[1], drain, 0)
 
     def small_wait(p):
         sm_copy(p, p).wait_recv()
@@ -770,62 +984,78 @@
     sb_ref[...] = bias_total
     ST[...] = total
 
-    def pr_load(k, p):
-        rows = ds(p, Tr)
-        return pltpu.make_async_copy(
-            pr_hbm.at[k, rows, :], A.at[k, rows, :], loc_sem.at[k, p]
-        )
-
-    def part_take(p):
-        for k in range(2):
-            pr_copy(k, p, mt).wait_send()
-            pr_copy(k, p, p).wait_recv()
-            pr_load(k, p).start()
-
-    each_tensor(part_take)
-    own = ds(mt, Tr)
-
-    def part_add(p):
-        for k in range(2):
-            pr_load(k, p).wait()
-            Acc[2 - 2 * k, own, :] += A[k, ds(p, Tr), :].astype(F32)
-
-    each_tensor(part_add)
+    for k in range(2):
+        others(k, 1, lambda q, k=k: s2_wait(k, q).wait_recv())
+        for q in range(size[k][1] - 1):
+            cp = load(k, d.P1 + q, mt)
+            cp.start()
+            cp.wait()
+            Acc[acc_of[k], own, :] += A[k, own, :].astype(F32)
 
     def st_copy(p, where):
         return rcopy_to(ST, RT.at[where], st_s.at[p], st_r.at[where], {"tensor": p})
 
     each_tensor(lambda p: st_copy(p, mt).start())
-    xr = A[0, own, :].astype(F32)
-    normed, inv = layer_norm(xr)
-    ng = Acc[0, own, :]
-    gm = jnp.mean(ng, axis=-1, keepdims=True)
-    gp = jnp.mean(ng * normed, axis=-1, keepdims=True)
-    A[0, own, :] = (xr + Acc[2, own, :] + NB[4:5, :]).astype(BF16)
-    A[1, own, :] = (A[2, own, :].astype(F32) + inv * (ng - gm - normed * gp)).astype(BF16)
+    def finish(rows, at):
+        off = pl.multiple_of((mt + 1) % tn * Tr + at - mt * Tr, SLAB)
+        xr = A[2, pl.ds(off, SLAB), :].astype(F32)
+        normed, inv = layer_norm(xr)
+        ng = Acc[0, rows, :]
+        gm = jnp.mean(ng, axis=-1, keepdims=True)
+        gp = jnp.mean(ng * normed, axis=-1, keepdims=True)
+        A[0, rows, :] = (xr + Acc[2, rows, :] + NB[4:5, :]).astype(BF16)
+        A[1, rows, :] = (A[2, rows, :].astype(F32) + inv * (ng - gm - normed * gp)).astype(BF16)
+
+    slabs(mt * Tr, Tr, finish)
     outs = (o_hbm, dx_hbm)
 
-    def fo_copy(k, p, where):
+    def f1_copy(k, b, sender):
+        c1 = coord[k][0]
         return rcopy_to(
             A.at[k, own, :],
-            outs[k].at[ds(where, Tr), :],
-            fo_s.at[k, p],
-            fo_r.at[k, where],
-            {"tensor": p},
-        )
-
-    def fo_send(p):
-        fo_copy(0, p, mt).start()
-        fo_copy(1, p, mt).start()
-
-    each_tensor(fo_send)
+            outs[k].at[ds(block_of(k, c1, sender), Tr), :],
+            f1_s.at[k, b],
+            f1_r.at[k, sender],
+            {"tensor": block_of(k, c1, b)},
+        )
+
+    def f2_copy(k, a, b, sender, src):
+        s2 = size[k][1]
+        return rcopy_to(
+            src,
+            outs[k].at[ds(block_of(k, sender, b), Tr), :],
+            f2_s.at[k, a * s2 + b],
+            f2_r.at[k, sender * s2 + b],
+            {"tensor": block_of(k, a, coord[k][1])},
+        )
+
     home = [
         pltpu.make_async_copy(A.at[k, own, :], outs[k].at[own, :], in_sem.at[k])
         for k in range(2)
     ]
-    for cp in home:
-        cp.start()
-    lax.fori_loop(middle, steps, drain, 0)
+    for k in range(2):
+        c1, c2 = coord[k]
+        others(k, 1, lambda b, k=k, c2=c2: f1_copy(k, b, c2).start())
+    for k in range(2):
+        c1, c2 = coord[k]
+
+        def mine_on(a, k=k, c1=c1, c2=c2):
+            f2_copy(k, a, c2, c1, A.at[k, own, :]).start()
+
+        others(k, 0, mine_on)
+        home[k].start()
+    lax.fori_loop(marks[1], marks[2], drain, 0)
+    for k in range(2):
+        c1, c2 = coord[k]
+
+        def forward(b, k=k, c1=c1):
+            f1_copy(k, b, b).wait_recv()
+            rows = ds(block_of(k, c1, b), Tr)
+            others(k, 0, lambda a: f2_copy(k, a, b, c1, outs[k].at[rows, :]).start())
+
+        others(k, 1, forward)
+    lax.fori_loop(marks[2], rest, drain, 0)
+    lax.fori_loop(p2_count(rest - 1), steps, p2_one, 0)
 
     each_tensor(lambda p: st_copy(p, p).wait_recv())
     RT[mt] = ST[...]
@@ -835,13 +1065,24 @@
     row = lax.broadcasted_iota(jnp.int32, (8, Dsl), 0)
     so_ref[...] = jnp.where(row < 4, whole, ST[...])
 
-    def ends(p):
-        for k in range(2):
-            fo_copy(k, p, mt).wait_send()
-            fo_copy(k, p, p).wait_recv()
-        st_copy(p, mt).wait_send()
-
-    each_tensor(ends)
+    for k in range(2):
+        c1, c2 = coord[k]
+        s1, s2 = size[k]
+
+        def end0(q, k=k, c1=c1, s2=s2):
+            for b in range(s2):
+                s1_copy(k, q, b, c1).wait_send()
+                f2_copy(k, q, b, c1, A.at[k, own, :]).wait_send()
+                f2_copy(k, q, b, q, A.at[k, own, :]).wait_recv()
+
+        def end1(b, k=k, c2=c2):
+            s2_copy(k, b, c2).wait_send()
+            f1_copy(k, b, c2).wait_send()
+
+        others(k, 0, end0)
+        others(k, 1, end1)
+
+    each_tensor(lambda p: st_copy(p, mt).wait_send())
 
     def dp_ends(p):
         sp_copy(p, me).wait_send()
@@ -852,18 +1093,17 @@
     for cp in home:
         cp.wait()
 
-    def p2_ends(u, carry):
-        @pl.when(has_r)
+    def line_ends(u, carry):
+        ag_finish(u)
+
+        @pl.when(has_r & has_l)
         def _():
             p2_copy(u, True).wait_send()
-
-        @pl.when(has_l)
-        def _():
             p2_copy(u, False).wait_send()
 
         return carry
 
-    lax.fori_loop(0, U, p2_ends, 0)
+    lax.fori_loop(0, U, line_ends, 0)
     for v in range(max(0, U - NS), U):
         rs_finish(v)
     for v in range(max(0, U - 2), U):
@@ -890,16 +1130,15 @@
             jax.ShapeDtypeStruct((width, Dsl), F32),
             jax.ShapeDtypeStruct((Dsl, hidden), F32),
             jax.ShapeDtypeStruct((hidden, Dsl), F32),
-            jax.ShapeDtypeStruct((2, T, D), BF16),
+            jax.ShapeDtypeStruct((2, d.P1 + d.P2, T // tn, D), BF16),
             jax.ShapeDtypeStruct((8, Dsl), F32),
             jax.ShapeDtypeStruct((up, UNIT), F32),
         ),
         in_specs=[pl.BlockSpec(memory_space=pltpu.SMEM), vm, vm] + [hbm] * 6,
         out_specs=(hbm,) * 7 + (vm, vm),
         scratch_shapes=[
-            pltpu.VMEM((d.NW, n_dp) + tile, BF16),
+            pltpu.VMEM((U, n_dp) + tile, BF16),
             pltpu.VMEM((3, T, D), BF16),
-            pltpu.VMEM((3, 2, n * Dsl, T), BF16),
             pltpu.VMEM((3, T, D), F32),
             pltpu.VMEM((4, T, UNIT), F32),
             pltpu.VMEM((4, T, UNIT), BF16),
@@ -907,14 +1146,11 @@
             pltpu.VMEM((T, T), BF16),
             pltpu.VMEM((T, T), BF16),
             pltpu.VMEM((d.NS, n - 2) + tile, BF16),
-            pltpu.VMEM((U,) + tile, BF16),
-            pltpu.VMEM((U,) + tile, BF16),
             pltpu.VMEM((2, n) + tile, BF16),
             pltpu.VMEM((d.NSR, n) + tile, BF16),
-            pltpu.VMEM((d.NLR, n - 1) + tile, BF16),
+            pltpu.VMEM((d.NLR, n) + tile, BF16),
             pltpu.VMEM((2,) + tile, F32),
             pltpu.VMEM((2, UNIT, Dsl), F32),
-            pltpu.VMEM((d.heads + d.chunks,) + tile, BF16),
             pltpu.VMEM((n_dp, rp, UNIT), F32),
             pltpu.VMEM((8, D), F32),
             pltpu.VMEM((U, 8, UNIT), F32),
@@ -926,18 +1162,17 @@
             pltpu.VMEM((8, Dsl), F32),
             pltpu.VMEM((tn, 8, Dsl), F32),
             dma((2,)),
-            dma((d.NW,)),
-            dma((d.NW, n_dp)),
-            dma((d.NW, n)),
-            dma((d.NW, n)),
-            dma((d.NW, n)),
-            reg((3,)),
+            dma((U,)),
+            dma((U, n_dp)),
+            dma((U, n)),
+            dma((U, n)),
+            dma((U, n)),
             reg((2,)),
             reg((2,)),
             dma((2,)),
             dma((d.NSR,)),
-            dma((d.NS, n - 2)),
-            dma((d.NLR, n - 1)),
+            dma((d.NS, n)),
+            dma((d.NLR, n)),
             dma((2,)),
             dma((n_dp,)),
             dma((n_dp,)),
@@ -950,7 +1185,13 @@
             dma((2, tn)),
             dma((2, tn)),
             dma((2, tn)),
+            dma((2, tn)),
+            dma((2, tn)),
+            dma((2, tn)),
+            dma((2, d.P1 + d.P2)),
             dma((d.heads + d.chunks,)),
+            dma((2, U)),
+            dma((2, U)),
         ],
         compiler_params=pltpu.CompilerParams(
             collective_id=0, has_side_effects=True, vmem_limit_bytes=67_000_000
@@ -1004,8 +1245,9 @@
     hidden = up_weight.shape[1]
     chunks = hidden // UNIT
     U = 4 * heads + 2 * chunks
-    gap = 2 if n <= 4 else 1
-    e0 = 1
+    F0, lag, lag2 = 0, 5, 2
+    hi = 2 if tn % 2 == 0 else 1
+    lo = tn // hi
     d = types.SimpleNamespace(
         n=n,
         tn=tn,
@@ -1015,16 +1257,23 @@
         U=U,
         heads=heads,
         chunks=chunks,
-        LAG=3,
-        E=e0,
-        gap=gap,
-        ES=e0 + gap * (n - 2),
-        E0=e0 + gap * (n - 1),
-        NW=min(U, e0 + gap * (n - 1) + 6),
-        NS=min(U, n + 3),
+        F0=F0,
+        held=3,
+        ahead=(1, 4, 2),
+        own=5,
+        burst=3,
+        hop=2,
+        lag=lag,
+        lag2=lag2,
+        pace=3,
+        Q0=U - 8,
+        NS=min(U, lag + (n - 3) * lag2 + 4),
         NSR=4,
-        NLR=n + 2,
-        I1=14,
+        NLR=min(U, lag + (n - 3) * lag2 + 2),
+        lo=lo,
+        P1=max((lo - 1) * hi, (hi - 1) * lo),
+        P2=max(lo, hi) - 1,
+        marks=(3, 4, 5),
     )
     me = lax.axis_index("dp")
 
@@ -1052,8 +1301,9 @@
         up_weight,
         down_weight,
     )
-    dqkv_b = sb[: 4 * heads].reshape(heads, 4, UNIT)[:, :3].transpose(1, 0, 2).reshape(3, width)
-    dup_b = sb[4 * heads : U].reshape(chunks, 2, UNIT)[:, 0].reshape(hidden)
+    F1 = F0 + 4 * heads
+    dqkv_b = sb[F0:F1].reshape(heads, 4, UNIT)[:, :3].transpose(1, 0, 2).reshape(3, width)
+    dup_b = jnp.concatenate([sb[:F0], sb[F1:U]]).reshape(chunks, 2, UNIT)[:, 0].reshape(hidden)
     return (
         out,
         dx,

time: 394 us -> 333 us (0.85)
  Pallas kernels: 373 us -> 312 us
    pallas_call x1, Pallas kernels: 373 us -> 312 us  [run_layer(): pl.pallas_call(functools.partial(layer_kernel, d), out_shape=(jax.ShapeDt...]
where the time goes in v4:
time: 333 us; the launch traced here: 332 us
  Pallas kernels  312 us (94%)
  local copies, waits for them, and re-layouts  16 us (5%)
    pallas_call x1, Pallas kernels, run_layer(): pl.pallas_call(functools.partial(layer_kernel, d), out_shape=(jax.ShapeDt...  312 us
    unnamed x30, local copies, waits for them, and re-layouts  11.5 us

profile of v4, /device:TPU:0, one launch (start us, length us, event | category | flops | bytes accessed | tf_op | source)
XLA Modules:
  0.0 332.5 jit_solution(12197759559987484159)
XLA Ops:
  0.6 0.0 copy-start.5
  0.7 0.0 copy-start.6
  0.7 0.0 copy-start.7
  0.7 0.0 copy-start.8
  0.7 0.0 copy-start.9
  0.7 0.0 copy-start.10
  0.7 0.0 copy-start.11
  0.7 1.0 fusion.1
  1.7 0.1 pad.18.clone
  1.8 0.1 pad.21.clone
  1.9 0.2 maximum_bitcast_fusion
  2.1 0.8 pad_maximum_fusion.rope_ref
  2.9 0.0 copy-done.5
  3.0 0.1 tile.7
  3.1 0.0 copy-done.7
  3.3 0.6 pad_maximum_fusion.1.sp_ref
  4.5 312.2 %shard_map.237 = (bf16[512,2048]{1,0:T(8,128)(2,1)}, bf16[512,2048]{1,0:T(8,128)(2,1)}, f32[3,256,512]{2,1,0:T(8,128)}, f32[512,256]{1,0:T(8,128)}, f32[256,2048...) custom-call(s32[1]{0:T(128)S(6)} %copy.36.len_ref, ...), custom_call_target="tpu_custom_call" | custom-call | flops 38654705664 | bytes 17825792 | tf_op jit(solution)/shard_map/pallas_call | solution.py:1124
  316.8 0.7 slice.34
  317.5 0.6 dynamic_slice.7
  318.2 0.7 slice.31
  318.9 0.6 constant_dynamic-slice_fusion
  319.5 1.5 fusion.9
  321.0 3.3 copy.37
  324.3 1.3 copy.38
  325.6 0.8 copy-done.3
  326.5 1.1 copy.39
  327.6 0.2 copy-done.4
  327.9 0.8 copy.40
  328.7 0.2 copy-done.1
  328.8 1.3 copy.41
  330.1 1.0 copy-done
  331.2 1.3 copy.42
  (32 shorter events, 0.2 us)
Async XLA Ops:
  0.6 2.3 copy-start.5
  0.7 2.4 copy-start.6
  0.7 2.5 copy-start.7
  0.7 2.5 copy-start.8
  0.7 2.5 copy-start.9
  0.7 2.5 copy-start.10
  0.7 2.5 copy-start.11
  321.0 3.3 copy-start.2
  324.3 2.2 copy-start.3
  326.5 1.4 copy-start.4
  326.5 2.3 copy-start.1
  328.8 2.3 copy-start

commit v5 on v4

--- a/solution.py
+++ b/solution.py
@@ -4,6 +4,7 @@
 
 import jax
 import jax.numpy as jnp
+import numpy as np
 from jax import lax
 from jax.experimental import pallas as pl
 from jax.experimental.pallas import tpu as pltpu
@@ -42,8 +43,14 @@
 def layer_kernel(
     d,
     len_ref,
-    sp_ref,
-    rope_ref,
+    ga_ref,
+    sa_ref,
+    gf_ref,
+    sf_ref,
+    ob_ref,
+    ub_ref,
+    qb_ref,
+    rope_hbm,
     x_hbm,
     cot_hbm,
     wqkv,
@@ -58,9 +65,9 @@
     ddown_hbm,
     pr_hbm,
     so_ref,
-    sb_ref,
     W,
     A,
+    rope_ref,
     Acc,
     Y,
     G,
@@ -83,9 +90,11 @@
     RB2,
     ST,
     RT,
+    SBT,
     in_sem,
     own_sem,
-    ag_recv,
+    line_r,
+    sib_r,
     agR,
     agL,
     agS,
@@ -114,6 +123,9 @@
     raw_sem,
     p2_s,
     p2_r,
+    rope_sem,
+    SP,
+    SW,
 ):
     n, tn, T, D, Dsl, U, heads = d.n, d.tn, d.T, d.D, d.Dsl, d.U, d.heads
     n_dp, NS, NSR, NLR = 2 * d.n, d.NS, d.NSR, d.NLR
@@ -202,15 +214,22 @@
             lambda: f(W.at[u, me]),
         )
 
-    def ag_tile(u, sj, sem, dev):
-        return rcopy(W.at[u, sj], W.at[u, sj], sem, ag_recv.at[u, sj], dev)
+    def to_line(u, j, src, sems, dev):
+        return rcopy(src, W.at[u, j * 2 + c], sems.at[j], line_r.at[u, j], dev)
+
+    def to_sib(u, j, src):
+        return rcopy(src, W.at[u, j * 2 + c], agS.at[j], sib_r.at[u], sib)
+
+    def own_all():
+        span = W.at[0 : 3 * heads + chunks, 0]
+        return pltpu.make_async_copy(span, span, own_sem.at[0])
 
     def own_load(src, u):
-        return pltpu.make_async_copy(src, W.at[u, me], own_sem.at[u])
+        return pltpu.make_async_copy(src, W.at[u, me], own_sem.at[0])
 
     def ag_self(u):
         def go(src):
-            rcopy(src, W.at[u, me], agS.at[u, z], ag_recv.at[u, me], sib).start()
+            to_sib(u, z, src).start()
 
         own_tile(u, go)
 
@@ -218,19 +237,19 @@
         @pl.when(has_next)
         def _():
             def go(src):
-                rcopy(src, W.at[u, me], sems.at[u, z], ag_recv.at[u, me], dev).start()
+                to_line(u, z, src, sems, dev).start()
 
             own_tile(u, go)
 
     def relay(u, j, has_next, sems, dev):
-        sj = j * 2 + c
-        ag_tile(u, sj, agS.at[u, j], sib).wait_recv()
+        tile = W.at[u, j * 2 + c]
+        to_line(u, j, tile, sems, dev).wait_recv()
 
         @pl.when(has_next)
         def _():
-            ag_tile(u, sj, sems.at[u, j], dev).start()
-
-        ag_tile(u, sj, agS.at[u, j], sib).start()
+            to_line(u, j, tile, sems, dev).start()
+
+        to_sib(u, j, tile).start()
 
     def ag_line(u, has_next, sems, dev, sign):
         for k in range(1, n):
@@ -276,24 +295,25 @@
         guarded(s + ahead_of(to_l), lambda u: ag_line(u, has_l, agL, left, 1))
 
     def ag_wait(u):
-        nothing = lambda: None
-        landed = lambda: own_load(wup.at[:, 0:UNIT], u).wait()
-        by_kind(u, landed, nothing, landed, nothing)
-        for j in range(n):
-            ag_tile(u, j * 2 + 1 - c, agS.at[u, j], sib).wait_recv()
-
-    def ag_finish(u):
+        span = W.at[u, 0:n]
+        rcopy(span, span, agS.at[0], sib_r.at[u], sib).wait_recv()
+
+    def units_sent(sem):
+        span = W.at[:, 0]
+        rcopy(span, span, sem, line_r.at[0, 0], sib).wait_send()
+
+    def ag_finish():
         for j in range(n):
 
             @pl.when(has_r & (j <= z))
             def _(j=j):
-                ag_tile(u, j * 2 + c, agR.at[u, j], right).wait_send()
+                units_sent(agR.at[j])
 
             @pl.when(has_l & (j >= z))
             def _(j=j):
-                ag_tile(u, j * 2 + c, agL.at[u, j], left).wait_send()
-
-            ag_tile(u, j * 2 + c, agS.at[u, j], sib).wait_send()
+                units_sent(agL.at[j])
+
+            units_sent(agS.at[j])
 
     def dead(v, j):
         return W.at[v, j * 2 + 1 - c]
@@ -315,7 +335,7 @@
         return rcopy(
             src,
             LR.at[v % NLR, slot],
-            ls_sem.at[v % NS, zt],
+            ls_sem.at[v % NS],
             lr_sem.at[v % NLR, slot],
             right if to_right else left,
         )
@@ -338,16 +358,13 @@
         sb_copy(u).start()
 
     def rs_finish(v):
-        for zt in range(n):
-            sent = zt != z
-            if zt == n - 1:
-                sent = sent & (z == 0)
-            if zt == 0:
-                sent = sent & (z == n - 1)
-
-            @pl.when(sent)
-            def _(zt=zt):
-                ls_copy(v, zt, True).wait_send()
+        def sent(count):
+            span = W.at[0, 0:count]
+            rcopy(span, span, ls_sem.at[v % NS], line_r.at[0, 0], sib).wait_send()
+
+        ends = (z == 0) | (z == n - 1)
+        pl.when(ends)(lambda: sent(n - 1))
+        pl.when(jnp.logical_not(ends))(lambda: sent(n - 3))
 
     def dw_own(u):
         @pl.when(u >= NS)
@@ -477,7 +494,7 @@
         return rcopy(
             dead(u, n - 1 if to_right else 0),
             dead(u, 1 if to_right else n - 2),
-            p2_s.at[side, u],
+            p2_s.at[side],
             p2_r.at[side, u],
             right if to_right else left,
         )
@@ -636,8 +653,10 @@
     each_tensor(lambda p: signal(barrier, p, "tensor"))
     x_in = pltpu.make_async_copy(x_hbm, A.at[0], in_sem.at[0])
     c_in = pltpu.make_async_copy(cot_hbm, A.at[2], in_sem.at[1])
+    rope_in = pltpu.make_async_copy(rope_hbm, rope_ref, rope_sem.at[0])
     x_in.start()
     c_in.start()
+    rope_in.start()
     spots = [
         buf.at[i, r * UNIT : (r + 1) * UNIT, 0:Dsl]
         for buf in (QK, G)
@@ -669,13 +688,32 @@
         return carry
 
     lax.fori_loop(0, U, load_own, 0)
+    def lanes_of(ref):
+        rows = ref[...].astype(F32)
+        return jnp.concatenate([rows[i : i + 1] for i in range(rows.shape[0])], axis=1)
+
+    SP[...] = jnp.zeros_like(SP)
+    SW[...] = jnp.zeros_like(SW)
+    for i, ref in enumerate((ga_ref, sa_ref, gf_ref, sf_ref, ob_ref)):
+        SP[i : i + 1, 0:Dsl] = lanes_of(ref)
+    SW[0, 0:3, 0 : d.nb] = qb_ref[...].astype(F32)
+    SW[1, 0:1, 0 : d.ub] = lanes_of(ub_ref)[:, 0 : d.ub]
+    at_q, at_u = me * d.nb, me * d.ub
+    qb = pltpu.roll(SW[0], at_q % UNIT, 1)
+    ub = pltpu.roll(SW[1], at_u % UNIT, 1)
+    for h in range(heads):
+        mine = jnp.where(at_q // UNIT == h, 1.0, 0.0)
+        SP[8 + 3 * h : 11 + 3 * h, :] = qb[0:3, :] * mine
+    for i in range(chunks):
+        mine = jnp.where(at_u // UNIT == i, 1.0, 0.0)
+        SP[8 + 3 * heads + i : 9 + 3 * heads + i, :] = ub[0:1, :] * mine
     pl.semaphore_wait(barrier, n_dp - 1 + tn - 1)
 
     def sp_copy(p, where):
-        return rcopy(sp_ref, RP.at[where], sp_s.at[p], sp_r.at[where], p)
+        return rcopy(SP, RP.at[where], sp_s.at[0], sp_r.at[where], p)
 
     each_dp(lambda p: sp_copy(p, me).start())
-    RP[me] = sp_ref[...]
+    RP[me] = SP[...]
 
     def burst(u, carry):
         ag_own(u, has_r, agR, right)
@@ -719,6 +757,8 @@
         BI[u] = jnp.broadcast_to(row, (8, UNIT))
     x_in.wait()
     c_in.wait()
+    rope_in.wait()
+    own_all().wait()
     blocks = T // ROWS
 
     fills = max(ahead(h) for h in range(n - 1))
@@ -892,11 +932,11 @@
 
     def sm_copy(p, where):
         return rcopy(
-            SM.at[:, ds(p, Dsl)], RS1.at[where], sm_s.at[0, p], sm_r.at[0, where], p
+            SM.at[:, ds(p, Dsl)], RS1.at[where], sm_s.at[0], sm_r.at[0, where], p
         )
 
     def bg_copy(p, where):
-        return rcopy(BGC, RB2.at[where], sm_s.at[1, p], sm_r.at[1, where], p)
+        return rcopy(BGC, RB2.at[where], sm_s.at[1], sm_r.at[1, where], p)
 
     def small_send(p):
         sm_copy(p, me).start()
@@ -981,7 +1021,7 @@
     for p in range(1, n_dp):
         total = total + RS1[p]
         bias_total = bias_total + RB2[p]
-    sb_ref[...] = bias_total
+    SBT[...] = bias_total
     ST[...] = total
 
     for k in range(2):
@@ -993,7 +1033,7 @@
             Acc[acc_of[k], own, :] += A[k, own, :].astype(F32)
 
     def st_copy(p, where):
-        return rcopy_to(ST, RT.at[where], st_s.at[p], st_r.at[where], {"tensor": p})
+        return rcopy_to(ST, RT.at[where], st_s.at[0], st_r.at[where], {"tensor": p})
 
     each_tensor(lambda p: st_copy(p, mt).start())
     def finish(rows, at):
@@ -1063,7 +1103,17 @@
     for p in range(1, tn):
         whole = whole + RT[p]
     row = lax.broadcasted_iota(jnp.int32, (8, Dsl), 0)
-    so_ref[...] = jnp.where(row < 4, whole, ST[...])
+    so_ref[0:8, 0:Dsl] = jnp.where(row < 4, whole, ST[...])
+
+    def share(first, stride, size):
+        at = me * size
+        one = SBT[pl.ds(first + stride * (at // UNIT), 1), :]
+        wide = jnp.broadcast_to(one, (8, UNIT))
+        return pltpu.roll(wide, (UNIT - at % UNIT) % UNIT, 1)[0:1, :]
+
+    so_ref[8:9, :] = share(F1, 2, d.ub)
+    for r in range(3):
+        so_ref[9 + r : 10 + r, :] = share(r, 4, d.nb)
 
     for k in range(2):
         c1, c2 = coord[k]
@@ -1082,28 +1132,25 @@
         others(k, 0, end0)
         others(k, 1, end1)
 
-    each_tensor(lambda p: st_copy(p, mt).wait_send())
-
-    def dp_ends(p):
-        sp_copy(p, me).wait_send()
-        sm_copy(p, me).wait_send()
-        bg_copy(p, me).wait_send()
-
-    each_dp(dp_ends)
+    for buf, sem, count in (
+        (RP, sp_s.at[0], n_dp - 1),
+        (RS1, sm_s.at[0], n_dp - 1),
+        (RB2, sm_s.at[1], n_dp - 1),
+        (RT, st_s.at[0], tn - 1),
+    ):
+        if count:
+            span = buf.at[0:count]
+            rcopy(span, span, sem, sp_r.at[0], sib).wait_send()
     for cp in home:
         cp.wait()
 
-    def line_ends(u, carry):
-        ag_finish(u)
-
-        @pl.when(has_r & has_l)
-        def _():
-            p2_copy(u, True).wait_send()
-            p2_copy(u, False).wait_send()
-
-        return carry
-
-    lax.fori_loop(0, U, line_ends, 0)
+    ag_finish()
+
+    @pl.when(has_r & has_l)
+    def _():
+        units_sent(p2_s.at[0])
+        units_sent(p2_s.at[1])
+
     for v in range(max(0, U - NS), U):
         rs_finish(v)
     for v in range(max(0, U - 2), U):
@@ -1111,11 +1158,11 @@
         out_wait(v)
 
 
-def run_layer(d, seq_len, sp, rope, x, cot, wqkv, wout, wup, wdown):
+def run_layer(d, seq_len, small, rope, x, cot, wqkv, wout, wup, wdown):
     n, tn, T, D, Dsl, U = d.n, d.tn, d.T, d.D, d.Dsl, d.U
     n_dp = 2 * n
     width, hidden = d.heads * UNIT, d.chunks * UNIT
-    rp, up = sp.shape[0], (U + 7) // 8 * 8
+    rp, up = (8 + 3 * d.heads + d.chunks + 7) // 8 * 8, (U + 7) // 8 * 8
     dma = pltpu.SemaphoreType.DMA
     reg = pltpu.SemaphoreType.REGULAR
     vm = pl.BlockSpec(memory_space=pltpu.VMEM)
@@ -1124,21 +1171,21 @@
     return pl.pallas_call(
         functools.partial(layer_kernel, d),
         out_shape=(
-            jax.ShapeDtypeStruct((T, D), BF16),
+            pltpu.VMEM((T, D), BF16),
             jax.ShapeDtypeStruct((T, D), BF16),
             jax.ShapeDtypeStruct((3, Dsl, width), F32),
             jax.ShapeDtypeStruct((width, Dsl), F32),
             jax.ShapeDtypeStruct((Dsl, hidden), F32),
             jax.ShapeDtypeStruct((hidden, Dsl), F32),
             jax.ShapeDtypeStruct((2, d.P1 + d.P2, T // tn, D), BF16),
-            jax.ShapeDtypeStruct((8, Dsl), F32),
-            jax.ShapeDtypeStruct((up, UNIT), F32),
+            jax.ShapeDtypeStruct((16, UNIT), F32),
         ),
-        in_specs=[pl.BlockSpec(memory_space=pltpu.SMEM), vm, vm] + [hbm] * 6,
-        out_specs=(hbm,) * 7 + (vm, vm),
+        in_specs=[pl.BlockSpec(memory_space=pltpu.SMEM)] + [vm] * 7 + [hbm] * 7,
+        out_specs=(hbm,) * 7 + (vm,),
         scratch_shapes=[
             pltpu.VMEM((U, n_dp) + tile, BF16),
             pltpu.VMEM((3, T, D), BF16),
+            pltpu.VMEM((2, T, 128), F32),
             pltpu.VMEM((3, T, D), F32),
             pltpu.VMEM((4, T, UNIT), F32),
             pltpu.VMEM((4, T, UNIT), BF16),
@@ -1161,24 +1208,26 @@
             pltpu.VMEM((n_dp, up, UNIT), F32),
             pltpu.VMEM((8, Dsl), F32),
             pltpu.VMEM((tn, 8, Dsl), F32),
+            pltpu.VMEM((up, UNIT), F32),
             dma((2,)),
+            dma((1,)),
+            dma((U, n)),
             dma((U,)),
-            dma((U, n_dp)),
-            dma((U, n)),
-            dma((U, n)),
-            dma((U, n)),
+            dma((n,)),
+            dma((n,)),
+            dma((n,)),
             reg((2,)),
             reg((2,)),
             dma((2,)),
             dma((d.NSR,)),
-            dma((d.NS, n)),
+            dma((d.NS,)),
             dma((d.NLR, n)),
             dma((2,)),
+            dma((1,)),
             dma((n_dp,)),
-            dma((n_dp,)),
+            dma((2,)),
             dma((2, n_dp)),
-            dma((2, n_dp)),
-            dma((tn,)),
+            dma((1,)),
             dma((tn,)),
             dma((2, tn)),
             dma((2, tn)),
@@ -1190,33 +1239,33 @@
             dma((2, tn)),
             dma((2, d.P1 + d.P2)),
             dma((d.heads + d.chunks,)),
+            dma((2,)),
             dma((2, U)),
-            dma((2, U)),
+            dma((1,)),
+            pltpu.VMEM((rp, UNIT), F32),
+            pltpu.VMEM((2, 8, UNIT), F32),
         ],
         compiler_params=pltpu.CompilerParams(
-            collective_id=0, has_side_effects=True, vmem_limit_bytes=67_000_000
+            collective_id=0, has_side_effects=True, vmem_limit_bytes=64_850_000
         ),
         cost_estimate=pl.CostEstimate(
             flops=6 * U * T * D * UNIT,
             bytes_accessed=6 * U * Dsl * UNIT + 8 * T * D,
             transcendentals=T * UNIT * U,
         ),
-    )(seq_len, sp, rope, x, cot, wqkv, wout, wup, wdown)
+    )(seq_len, *small, rope, x, cot, wqkv, wout, wup, wdown)
 
 
 def rope_pair(rows):
     half = ROT // 2
-    freq_idx = jnp.arange(half, dtype=F32)
-    inv_freq = jnp.exp(-(2.0 * freq_idx / ROT) * math.log(rope_base))
-    angles = jnp.arange(rows, dtype=F32)[:, None] * inv_freq[None, :]
-    cosine, sine = jnp.cos(angles), jnp.sin(angles)
-    rest = 128 - ROT
-    return jnp.stack(
-        [
-            jnp.concatenate([cosine, cosine, jnp.ones((rows, rest), F32)], axis=1),
-            jnp.concatenate([-sine, sine, jnp.zeros((rows, rest), F32)], axis=1),
-        ]
-    )
+    inv_freq = np.exp(-(2.0 * np.arange(half) / ROT) * math.log(rope_base))
+    angles = np.arange(rows)[:, None] * inv_freq[None, :]
+    table = np.zeros((2, rows, 128), np.float32)
+    table[0] = 1.0
+    table[0, :, :half] = table[0, :, half:ROT] = np.cos(angles)
+    table[1, :, :half] = -np.sin(angles)
+    table[1, :, half:ROT] = np.sin(angles)
+    return jnp.asarray(table)
 
 
 def per_device(
@@ -1246,6 +1295,7 @@
     chunks = hidden // UNIT
     U = 4 * heads + 2 * chunks
     F0, lag, lag2 = 0, 5, 2
+    nb, ub = qkv_bias.shape[1], up_bias.shape[0]
     hi = 2 if tn % 2 == 0 else 1
     lo = tn // hi
     d = types.SimpleNamespace(
@@ -1265,34 +1315,24 @@
         hop=2,
         lag=lag,
         lag2=lag2,
+        nb=nb,
+        ub=ub,
         pace=3,
         Q0=U - 8,
         NS=min(U, lag + (n - 3) * lag2 + 4),
         NSR=4,
-        NLR=min(U, lag + (n - 3) * lag2 + 2),
+        NLR=min(U, lag + (n - 3) * lag2 + 1),
         lo=lo,
         P1=max((lo - 1) * hi, (hi - 1) * lo),
         P2=max(lo, hi) - 1,
         marks=(3, 4, 5),
     )
-    me = lax.axis_index("dp")
-
-    nb, ub = qkv_bias.shape[1], up_bias.shape[0]
-    norm_rows = jnp.stack([attn_gain, attn_shift, ffn_gain, ffn_shift, out_bias])
-    norm_rows = jnp.pad(norm_rows.astype(F32), ((0, 3), (0, UNIT - Dsl)))
-    qkv_rows = jnp.where(
-        jnp.arange(width) // nb == me, jnp.tile(qkv_bias.astype(F32), (1, n_dp)), 0.0
-    )
-    qkv_rows = qkv_rows.reshape(3, heads, UNIT).transpose(1, 0, 2).reshape(3 * heads, UNIT)
-    up_rows = jnp.where(jnp.arange(hidden) // ub == me, jnp.tile(up_bias.astype(F32), n_dp), 0.0)
-    bias_rows = jnp.concatenate([qkv_rows, up_rows.reshape(chunks, UNIT)])
-    spare = -bias_rows.shape[0] % 8
-    sp = jnp.concatenate([norm_rows, jnp.pad(bias_rows, ((0, spare), (0, 0)))])
-
-    out, dx, dqkv, dout, dup, ddown, _, so, sb = run_layer(
+    flat = (attn_gain, attn_shift, ffn_gain, ffn_shift, out_bias, jnp.pad(up_bias, (0, -ub % 128)))
+    small = [v.reshape(-1, 128) for v in flat] + [qkv_bias]
+    out, dx, dqkv, dout, dup, ddown, _, so = run_layer(
         d,
         lengths,
-        sp,
+        small,
         rope_pair(T),
         block_input,
         cotangent,
@@ -1301,22 +1341,19 @@
         up_weight,
         down_weight,
     )
-    F1 = F0 + 4 * heads
-    dqkv_b = sb[F0:F1].reshape(heads, 4, UNIT)[:, :3].transpose(1, 0, 2).reshape(3, width)
-    dup_b = jnp.concatenate([sb[:F0], sb[F1:U]]).reshape(chunks, 2, UNIT)[:, 0].reshape(hidden)
     return (
         out,
         dx,
-        so[0],
-        so[1],
-        so[2],
-        so[3],
+        so[0, :Dsl],
+        so[1, :Dsl],
+        so[2, :Dsl],
+        so[3, :Dsl],
         dqkv,
-        lax.dynamic_slice_in_dim(dqkv_b, me * nb, nb, axis=1),
+        so[9:12, :nb],
         dout,
-        so[4],
+        so[4, :Dsl],
         dup,
-        lax.dynamic_slice_in_dim(dup_b, me * ub, ub, axis=0),
+        so[8, :ub],
         ddown,
     )
 

time: 333 us -> 319 us (0.958)
  local copies, waits for them, and re-layouts: 16 us -> 10.7 us
  Pallas kernels: 312 us -> 307 us
    pallas_call x1, Pallas kernels: 312 us -> 307 us  [run_layer(): pl.pallas_call(functools.partial(layer_kernel, d), out_shape=(pltpu.VMEM(...]
    unnamed x30 -> x18, local copies, waits for them, and re-layouts: 11.5 us -> 9.49 us
where the time goes in v5:
time: 319 us
  Pallas kernels  307 us (96%)
  local copies, waits for them, and re-layouts  10.7 us (3%)
    pallas_call x1, Pallas kernels, run_layer(): pl.pallas_call(functools.partial(layer_kernel, d), out_shape=(pltpu.VMEM(...  307 us
    unnamed x18, local copies, waits for them, and re-layouts  9.49 us

profile of v5, /device:TPU:0, one launch (start us, length us, event | category | flops | bytes accessed | tf_op | source)
XLA Modules:
  0.0 318.9 jit_solution(1798205592482215545)
XLA Ops:
  1.3 306.9 %shard_map.246 = (bf16[512,2048]{1,0:T(8,128)(2,1)S(1)}, bf16[512,2048]{1,0:T(8,128)(2,1)}, f32[3,256,512]{2,1,0:T(8,128)}, f32[512,256]{1,0:T(8,128)}, f32[256,...) custom-call(s32[1]{0:T(128)S(6)} %copy.35.len_ref, ...), custom_call_target="tpu_custom_call" | custom-call | flops 38654705664 | bytes 17825792 | tf_op jit(solution)/shard_map/pallas_call | solution.py:1171
  308.2 0.0 copy-start.5
  308.2 0.0 copy-start.2
  308.2 1.3 copy.34
  309.5 0.0 copy-done.5
  309.5 0.6 slice.25
  310.1 0.6 fusion
  310.7 0.0 copy-done.2
  310.7 0.0 copy-start.3
  310.7 1.3 copy.36
  312.0 0.8 copy-done.3
  312.9 0.0 copy-start.4
  312.9 0.0 copy-start.1
  312.9 1.1 copy.37
  314.0 0.2 copy-done.4
  314.2 0.8 copy.38
  315.0 0.2 copy-done.1
  315.2 0.0 copy-start
  315.2 1.3 copy.39
  316.5 1.0 copy-done
  317.6 1.3 copy.40
Async XLA Ops:
  308.2 1.3 copy-start.5
  308.2 2.5 copy-start.2
  310.7 2.2 copy-start.3
  312.9 1.4 copy-start.4
  312.9 2.3 copy-start.1
  315.2 2.3 copy-start

commit v6 on v5

--- a/solution.py
+++ b/solution.py
@@ -588,7 +588,10 @@
     def rotate(y, sign):
         lo = y[:, :128]
         swapped = jnp.where(lane < 32, pltpu.roll(lo, 96, 1), pltpu.roll(lo, 32, 1))
-        lo = lo * rope_ref[0] + swapped * (rope_ref[1] * sign)
+        table = rope_ref[...]
+        cosine = jnp.where(lane < ROT, table, 1.0)
+        sine = jnp.where(lane < ROT, pltpu.roll(table, 128 - ROT, 1), 0.0)
+        lo = lo * cosine + swapped * (sine * sign)
         return jnp.concatenate([lo, y[:, 128:]], axis=1)
 
     def attn_core(s):
@@ -779,7 +782,8 @@
     def made(s):
         return jnp.maximum(jnp.where(s < F1, s - 2, jnp.where(s == F1, s - 1, s)), 0)
 
-    sent_early = max(0, U - d.held - 1 - d.lag)
+    whole_by = U - d.held - 1 - d.lag
+    sent_early = max(0, whole_by)
 
     def early(q):
         return jnp.clip(jnp.minimum(2 * (q - d.Q0 + 1), q - d.lag), 0, sent_early)
@@ -892,8 +896,10 @@
             def _(q=q):
                 f(q)
 
-    def s1_send(i):
-        @pl.when(i >= 0)
+    def s1_send(j):
+        i = block_at(j)
+
+        @pl.when(j >= 0)
         def _():
             for k in range(2):
                 a = i % lo if k == 0 else i // lo
@@ -903,7 +909,13 @@
                 def _(k=k, a=a, b=b):
                     s1_copy(k, a, b, coord[k][0]).start()
 
-    def partial(i, carry):
+    def block_at(j):
+        o = tn - 1 - j
+        return (mt // lo + o // lo) % hi * lo + (mt % lo + o % lo) % lo
+
+    def partial(j, carry):
+        i = block_at(j)
+
         @pl.when(i == mt)
         def _():
             A[2, ds((mt + 1) % tn, Tr), :] = A[0, ds(i, Tr), :]
@@ -922,7 +934,7 @@
             A[0, rows, :] = Acc[2, rows, :].astype(BF16)
 
         slabs(i * Tr, Tr, rows_of)
-        s1_send(i - 1)
+        s1_send(j - 1)
         return carry
 
     lax.fori_loop(0, tn, partial, 0)
@@ -958,7 +970,7 @@
     steps = U + d.hop * (n - 3)
 
     def p2_count(i):
-        fed = jnp.minimum(d.pace * (i + 1), sent_early + i)
+        fed = jnp.minimum(d.pace * (i + 1), whole_by + i)
         return jnp.clip(jnp.where(i < rest, fed, steps), 0, steps)
 
     def p2_one(i, carry):
@@ -967,7 +979,7 @@
 
     def drain(i, carry):
         rs_step(i + U - d.held)
-        guarded(i + sent_early, p2_first)
+        guarded(i + whole_by, p2_first)
         lax.fori_loop(p2_count(i - 1), p2_count(i), p2_one, 0)
         return carry
 
@@ -980,29 +992,21 @@
             pr_hbm.at[k, slot], A.at[k, ds(b, Tr), :], loc_sem.at[k, slot]
         )
 
-    def gather_in(k, do):
+    def s1_take(k, b):
         s1, s2 = size[k]
-        for b in range(s2):
-            do(b, block_of(k, coord[k][0], b))
+        row_b = block_of(k, coord[k][0], b)
+        rows = ds(row_b, Tr)
+        others(k, 0, lambda q: s1_wait(k, q, b).wait_recv())
+        for q in range(s1 - 1):
+            cp = load(k, q * s2 + b, row_b)
+            cp.start()
+            cp.wait()
+            Acc[acc_of[k], rows, :] += A[k, rows, :].astype(F32)
 
     for k in range(2):
-        s1, s2 = size[k]
-
-        def take(q, k=k, s2=s2):
-            for b in range(s2):
-                s1_wait(k, q, b).wait_recv()
-
-        others(k, 0, take)
-        for q in range(s1 - 1):
-            for b in range(s2):
-                load(k, q * s2 + b, block_of(k, coord[k][0], b)).start()
-            for b in range(s2):
-                row_b = block_of(k, coord[k][0], b)
-                load(k, q * s2 + b, row_b).wait()
-                rows = ds(row_b, Tr)
-                Acc[acc_of[k], rows, :] += A[k, rows, :].astype(F32)
 
         def pass_on(b, k=k):
+            s1_take(k, b)
             rows = ds(block_of(k, coord[k][0], b), Tr)
             A[k, rows, :] = Acc[acc_of[k], rows, :].astype(BF16)
             s2_copy(k, b, coord[k][1]).start()
@@ -1025,6 +1029,7 @@
     ST[...] = total
 
     for k in range(2):
+        s1_take(k, coord[k][1])
         others(k, 1, lambda q, k=k: s2_wait(k, q).wait_recv())
         for q in range(size[k][1] - 1):
             cp = load(k, d.P1 + q, mt)
@@ -1185,7 +1190,7 @@
         scratch_shapes=[
             pltpu.VMEM((U, n_dp) + tile, BF16),
             pltpu.VMEM((3, T, D), BF16),
-            pltpu.VMEM((2, T, 128), F32),
+            pltpu.VMEM((T, 128), F32),
             pltpu.VMEM((3, T, D), F32),
             pltpu.VMEM((4, T, UNIT), F32),
             pltpu.VMEM((4, T, UNIT), BF16),
@@ -1260,11 +1265,8 @@
     half = ROT // 2
     inv_freq = np.exp(-(2.0 * np.arange(half) / ROT) * math.log(rope_base))
     angles = np.arange(rows)[:, None] * inv_freq[None, :]
-    table = np.zeros((2, rows, 128), np.float32)
-    table[0] = 1.0
-    table[0, :, :half] = table[0, :, half:ROT] = np.cos(angles)
-    table[1, :, :half] = -np.sin(angles)
-    table[1, :, half:ROT] = np.sin(angles)
+    cosine, sine = np.cos(angles), np.sin(angles)
+    table = np.concatenate([cosine, cosine, -sine, sine], axis=1).astype(np.float32)
     return jnp.asarray(table)
 
 

time: 319 us -> 316 us (level)
    pallas_call x1, Pallas kernels: 307 us -> 304 us  [run_layer(): pl.pallas_call(functools.partial(layer_kernel, d), out_shape=(pltpu.VMEM(...]
where the time goes in v6:
time: 316 us
  Pallas kernels  304 us (96%)
  local copies, waits for them, and re-layouts  10.7 us (3%)
    pallas_call x1, Pallas kernels, run_layer(): pl.pallas_call(functools.partial(layer_kernel, d), out_shape=(pltpu.VMEM(...  304 us
    unnamed x18, local copies, waits for them, and re-layouts  9.49 us

profile of v6, /device:TPU:0, one launch (start us, length us, event | category | flops | bytes accessed | tf_op | source)
XLA Modules:
  0.0 315.5 jit_solution(4823189763532129893)
XLA Ops:
  1.3 303.5 %shard_map.246 = (bf16[512,2048]{1,0:T(8,128)(2,1)S(1)}, bf16[512,2048]{1,0:T(8,128)(2,1)}, f32[3,256,512]{2,1,0:T(8,128)}, f32[512,256]{1,0:T(8,128)}, f32[256,...) custom-call(s32[1]{0:T(128)S(6)} %copy.35.len_ref, ...), custom_call_target="tpu_custom_call" | custom-call | flops 38654705664 | bytes 17825792 | tf_op jit(solution)/shard_map/pallas_call | solution.py:1176
  304.9 0.0 copy-start.5
  304.9 0.0 copy-start.2
  304.9 1.3 copy.34
  306.2 0.0 copy-done.5
  306.2 0.6 slice.25
  306.8 0.6 fusion
  307.4 0.0 copy-done.2
  307.4 0.0 copy-start.3
  307.4 1.3 copy.36
  308.7 0.8 copy-done.3
  309.5 0.0 copy-start.4
  309.5 0.0 copy-start.1
  309.5 1.1 copy.37
  310.7 0.2 copy-done.4
  310.9 0.8 copy.38
  311.7 0.2 copy-done.1
  311.9 0.0 copy-start
  311.9 1.3 copy.39
  313.2 1.0 copy-done
  314.2 1.3 copy.40
Async XLA Ops:
  304.9 1.3 copy-start.5
  304.9 2.5 copy-start.2
  307.4 2.2 copy-start.3
  309.5 1.4 copy-start.4
  309.5 2.3 copy-start.1
  311.9 2.3 copy-start

commit v7 on v6

--- a/solution.py
+++ b/solution.py
@@ -1296,7 +1296,7 @@
     hidden = up_weight.shape[1]
     chunks = hidden // UNIT
     U = 4 * heads + 2 * chunks
-    F0, lag, lag2 = 0, 5, 2
+    F0, lag, lag2 = 0, 5, 1
     nb, ub = qkv_bias.shape[1], up_bias.shape[0]
     hi = 2 if tn % 2 == 0 else 1
     lo = tn // hi
@@ -1327,7 +1327,7 @@
         lo=lo,
         P1=max((lo - 1) * hi, (hi - 1) * lo),
         P2=max(lo, hi) - 1,
-        marks=(3, 4, 5),
+        marks=(3, 4, 6),
     )
     flat = (attn_gain, attn_shift, ffn_gain, ffn_shift, out_bias, jnp.pad(up_bias, (0, -ub % 128)))
     small = [v.reshape(-1, 128) for v in flat] + [qkv_bias]

time: 316 us -> 315 us (level)
  no operation moved by 1% of the time
where the time goes in v7:
time: 315 us; the launch traced here: 314 us
  Pallas kernels  302 us (96%)
  local copies, waits for them, and re-layouts  10.7 us (3%)
    pallas_call x1, Pallas kernels, run_layer(): pl.pallas_call(functools.partial(layer_kernel, d), out_shape=(pltpu.VMEM(...  302 us
    unnamed x18, local copies, waits for them, and re-layouts  9.49 us

profile of v7, /device:TPU:0, one launch (start us, length us, event | category | flops | bytes accessed | tf_op | source)
XLA Modules:
  0.0 314.1 jit_solution(3870222532741772045)
XLA Ops:
  1.3 302.1 %shard_map.246 = (bf16[512,2048]{1,0:T(8,128)(2,1)S(1)}, bf16[512,2048]{1,0:T(8,128)(2,1)}, f32[3,256,512]{2,1,0:T(8,128)}, f32[512,256]{1,0:T(8,128)}, f32[256,...) custom-call(s32[1]{0:T(128)S(6)} %copy.35.len_ref, ...), custom_call_target="tpu_custom_call" | custom-call | flops 38654705664 | bytes 17825792 | tf_op jit(solution)/shard_map/pallas_call | solution.py:1176
  303.4 0.0 copy-start.5
  303.4 0.0 copy-start.2
  303.4 1.3 copy.34
  304.7 0.0 copy-done.5
  304.8 0.6 slice.25
  305.3 0.6 fusion
  305.9 0.0 copy-done.2
  305.9 0.0 copy-start.3
  305.9 1.3 copy.36
  307.2 0.8 copy-done.3
  308.1 0.0 copy-start.4
  308.1 0.0 copy-start.1
  308.1 1.1 copy.37
  309.2 0.2 copy-done.4
  309.5 0.8 copy.38
  310.3 0.2 copy-done.1
  310.4 0.0 copy-start
  310.4 1.3 copy.39
  311.7 1.0 copy-done
  312.8 1.3 copy.40
Async XLA Ops:
  303.4 1.3 copy-start.5
  303.4 2.5 copy-start.2
  305.9 2.2 copy-start.3
  308.1 1.4 copy-start.4
  308.1 2.3 copy-start.1
  310.4 2.3 copy-start

commit v8 on v7

--- a/solution.py
+++ b/solution.py
@@ -1311,7 +1311,7 @@
         chunks=chunks,
         F0=F0,
         held=3,
-        ahead=(1, 4, 2),
+        ahead=(1, 3, 2),
         own=5,
         burst=3,
         hop=2,

time: 315 us -> 315 us (level)
  no operation moved by 1% of the time
where the time goes in v8:
time: 315 us
  Pallas kernels  303 us (96%)
  local copies, waits for them, and re-layouts  10.7 us (3%)
    pallas_call x1, Pallas kernels, run_layer(): pl.pallas_call(functools.partial(layer_kernel, d), out_shape=(pltpu.VMEM(...  303 us
    unnamed x18, local copies, waits for them, and re-layouts  9.49 us

profile of v8, /device:TPU:0, one launch (start us, length us, event | category | flops | bytes accessed | tf_op | source)
XLA Modules:
  0.0 314.5 jit_solution(1257053731464668487)
XLA Ops:
  1.3 302.6 %shard_map.246 = (bf16[512,2048]{1,0:T(8,128)(2,1)S(1)}, bf16[512,2048]{1,0:T(8,128)(2,1)}, f32[3,256,512]{2,1,0:T(8,128)}, f32[512,256]{1,0:T(8,128)}, f32[256,...) custom-call(s32[1]{0:T(128)S(6)} %copy.35.len_ref, ...), custom_call_target="tpu_custom_call" | custom-call | flops 38654705664 | bytes 17825792 | tf_op jit(solution)/shard_map/pallas_call | solution.py:1176
  303.9 0.0 copy-start.5
  303.9 0.0 copy-start.2
  303.9 1.3 copy.34
  305.2 0.0 copy-done.5
  305.2 0.6 slice.25
  305.8 0.6 fusion
  306.4 0.0 copy-done.2
  306.4 0.0 copy-start.3
  306.4 1.3 copy.36
  307.7 0.8 copy-done.3
  308.5 0.0 copy-start.4
  308.5 0.0 copy-start.1
  308.5 1.1 copy.37
  309.7 0.2 copy-done.4
  309.9 0.8 copy.38
  310.7 0.2 copy-done.1
  310.9 0.0 copy-start
  310.9 1.3 copy.39
  312.2 1.0 copy-done
  313.2 1.3 copy.40
Async XLA Ops:
  303.9 1.3 copy-start.5
  303.9 2.5 copy-start.2
  306.4 2.2 copy-start.3
  308.5 1.4 copy-start.4
  308.5 2.3 copy-start.1
  310.9 2.3 copy-start
